TPU v7x, 32 devices: a whole 2x2x4 slice. The times are simulated.
32 devices in a mesh: ex: 32 (over z, y, x, core), cls: 1.
Axes of the slice: x: 2, y: 2, z: 4, core: 2. Of those that a mesh axis runs over, the one named last changes fastest.
Arguments:
- features: bfloat16 [32768, 1664], P('ex'), may hold values from -16 to 16
- labels: int32 [32768], P('ex'), may hold values from 0 to 1407
- weight: bfloat16 [1664, 1408], P(None, 'cls'), may hold values from -1 to 1
- noise: bfloat16 [1664, 1408], P('ex', 'cls'), may hold values from -5 to 5
Outputs:
- new_weight: bfloat16 [1664, 1408], P(None, 'cls')
All inputs are finite; a program needn't handle non-finite values.
Results may differ from a plain program's by a relative error of at most 0.0013.
Values may be sent and summed in bfloat16 or wider, within the bound.
No kernel may reach another device: no remote copies, remote signals or barrier semaphores. Data moves between devices by JAX's collectives and lax.ppermute only.
A program may use at most 128 MiB of HBM per device.

v0:
```python
import jax
import jax.numpy as jnp
from jax import lax
from jax.sharding import PartitionSpec as P


def local(features, labels, weight, noise):
    clip_norm = 48.0
    cls_width = weight.shape[1]
    logits = jnp.dot(features, weight, preferred_element_type=jnp.float32)
    offset = lax.axis_index("cls") * cls_width
    local_lab = labels - offset
    columns = lax.broadcasted_iota(jnp.int32, (1, cls_width), 1)
    onehot = columns == local_lab[:, None]
    label_part = jnp.sum(jnp.where(onehot, logits, 0.0), axis=1)
    top = lax.pmax(jnp.max(logits, axis=1), "cls")
    expo = jnp.exp(logits - top[:, None])
    total, squares, label_logit = lax.psum(
        (jnp.sum(expo, axis=1), jnp.sum(expo * expo, axis=1), label_part), "cls"
    )
    probs = expo / total[:, None]
    label_prob = jnp.exp(label_logit - top) / total
    resid_sq = squares / (total * total) - 2.0 * label_prob + 1.0
    resid_norm = jnp.sqrt(jnp.maximum(resid_sq, 0.0))
    feat = features.astype(jnp.float32)
    feat_norm = jnp.sqrt(jnp.sum(feat * feat, axis=1))
    factor = clip_norm / jnp.maximum(feat_norm * resid_norm, clip_norm)
    resid = probs - onehot.astype(jnp.float32)
    coef = (factor[:, None] * resid).astype(jnp.bfloat16)
    partial_grad = lax.dot_general(
        features, coef, (((0,), (0,)), ((), ())), preferred_element_type=jnp.float32
    )
    classes = cls_width * lax.axis_size("cls")
    batch = features.shape[0] * lax.axis_size("ex")
    scale = 0.1 * classes / batch
    grad_part = lax.psum_scatter(partial_grad, "ex", scatter_dimension=1, tiled=True)
    noise_part = lax.all_to_all(noise, "ex", split_axis=1, concat_axis=0, tiled=True)
    span = grad_part.shape[1]
    own_weight = lax.dynamic_slice_in_dim(weight, lax.axis_index("ex") * span, span, 1)
    updated = own_weight.astype(jnp.float32) - scale * (
        grad_part + 0.96 * clip_norm * noise_part.astype(jnp.float32)
    )
    return lax.all_gather(updated.astype(jnp.bfloat16), "ex", axis=1, tiled=True)


def solution(mesh):
    in_specs = (P("ex", None), P("ex"), P(None, "cls"), P("ex", "cls"))
    out_specs = P(None, "cls")
    return jax.shard_map(local, mesh=mesh, in_specs=in_specs, out_specs=out_specs, check_vma=False)
```

profile of v0, /device:TPU:0, one launch (start us, length us, event | category | flops | bytes accessed | tf_op | source)
XLA Modules:
  0.0 267.7 jit_solution(13339853644834071383)
XLA Ops:
  6.5 2.1 all_to_all.10
  8.7 0.6 copy.12
  9.3 1.2 reshape.35
  10.5 7.3 %all-to-all-start = ((bf16[32,2,1144]{2,1,0:T(2,128)(2,1)}), bf16[32,2,1144]{2,1,0:T(2,128)(2,1)S(1)}, u32[]{:S(2)}, u32[]{:S(2)}) async-start(bf16[32,2,1144]{2,1,0:T(2,128)(2,1)} %reshape.35), calls=%async_computation | async-start | bytes 294912 | tf_op jit(solution)/shard_map/all_to_all | solution.py:37
  17.8 0.0 all-gather.3.cloned.1.call-start
  17.9 2.7 %multiply_reduce_fusion = f32[1024]{0:T(1024)S(1)} fusion(bf16[1024,1664]{1,0:T(8,128)(2,1)} %param.4), kind=kLoop, calls=%fused_computation.1 | loop fusion | flops 5110784 | bytes 3411968 | tf_op jit(solution)/shard_map/reduce_sum | solution.py:26
  20.6 0.0 copy-start.1
  20.6 9.3 %fusion.10 = (f32[1024]{0:T(1024)S(1)}, f32[1024,1408]{1,0:T(8,128)S(1)}) fusion(bf16[1024,1664]{1,0:T(8,128)(2,1)} %param.4, bf16[1664,1408]{1,0:T(8,128)(2,1)} %param.6), kind=kOutput, calls=%fused_computation.20 | convolution fusion | flops 4799724544 | bytes 13864960 | tf_op jit(solution)/shard_map/dot_general | solution.py:10
  29.9 0.0 copy-start
  29.9 0.0 copy-done.1
  29.9 2.4 multiply_reduce_fusion.1
  32.4 0.0 copy-done
  32.4 10.2 %convolution_bitcast_fusion = f32[1664,1408]{0,1:T(8,128)} fusion(bf16[1024,1664]{1,0:T(8,128)(2,1)S(1)} %copy-done, f32[1024,1408]{1,0:T(8,128)S(1)} %get-tuple-element.9, f32[1024]{0:T(1024)S(1)} %get-tuple-element.6, f32[1024]{0:T(1024)S(1)} %maximum_divide_fusion, s32[1024]{0:T(1024)S(1)} %copy-done.1, f32[1024]{0:T(1024)S(1)} %get-tuple-element.8), kind=kOutput, calls=%fused_computation | convolution fusion | flops 4808376320 | bytes 18563072 | tf_op jit(solution)/shard_map/dot_general | solution.py:30
  42.6 114.2 %fusion = f32[1664,48]{0,1:T(8,128)S(1)} fusion(f32[1664,1408]{0,1:T(8,128)} %convolution_bitcast_fusion), kind=kCustom, calls=%all-reduce-scatter | all-reduce-scatter fusion | flops 2555905 | bytes 9691136
  156.7 2.3 collective-permute-start
  159.1 4.3 %collective-permute-start.1 = (f32[1664,48]{0,1:T(8,128)S(1)}, f32[1664,48]{0,1:T(8,128)S(1)}, u32[]{:S(2)}, u32[]{:S(2)}) collective-permute-start(f32[1664,48]{0,1:T(8,128)S(1)} %fusion), channel_id=1, source_target_pairs={{0,2},{1,3},{2,4},{3,5},{4,6},{5,7},{6,8},{7,9},{8,10},{9,11},{10,... | collective-permute-start | bytes 958472
  163.4 4.7 %collective-permute-start.2 = (f32[1664,28]{0,1:T(8,128)S(1)}, f32[1664,28]{0,1:T(8,128)S(1)}, u32[]{:S(2)}, u32[]{:S(2)}) collective-permute-start(f32[1664,28]{0,1:T(8,128)S(1)} %slice), channel_id=1, source_target_pairs={{0,3},{1,4},{2,5},{3,6},{4,7},{5,8},{6,9},{7,10},{8,11},{9,12},{10... | collective-permute-start | bytes 559112
  168.1 1.4 constant_dynamic-slice_fusion
  169.5 0.2 copy.15
  169.7 0.0 all-to-all-done
  169.7 0.6 reshape.36
  170.3 0.1 multiply_bitcast_fusion
  170.4 0.2 copy.13
  170.6 0.4 mul.72
  171.1 3.4 %collective-permute-done.2 = f32[1664,28]{0,1:T(8,128)S(1)} collective-permute-done((f32[1664,28]{0,1:T(8,128)S(1)}, f32[1664,28]{0,1:T(8,128)S(1)}, u32[]{:S(2)}, u32[]{:S(2)}) %collective-permute-start.2) | collective-permute-done | bytes 186400
  174.5 0.0 collective-permute-done
  174.5 0.0 collective-permute-done.1
  174.5 0.8 concatenate
  175.3 0.8 fusion.9
  176.1 0.0 all-gather.3.cloned.1.call-update
  176.1 70.1 %all-gather.3.cloned.1.call-done = bf16[32,44,1664]{2,1,0:T(8,128)(2,1)} async-done(((bf16[1,44,1664]{2,1,0:T(8,128)(2,1)}), bf16[32,44,1664]{2,1,0:T(8,128)(2,1)}) %all-gather.3.cloned.1.call-update) | async-done | bytes 4685840 | tf_op jit(solution)/shard_map/all_gather | solution.py:43
  246.1 7.2 %reshape.34 = bf16[1408,1664]{1,0:T(8,128)(2,1)} reshape(bf16[32,44,1664]{2,1,0:T(8,128)(2,1)} %all-gather.3.cloned.1.call-done) | data formatting | bytes 9371648
  253.3 7.6 %copy.14 = bf16[1664,1408]{1,0:T(8,128)(2,1)} copy(bf16[1664,1408]{0,1:T(8,128)(2,1)} %bitcast.17) | data formatting | bytes 9371648
  (2 shorter events, 0.0 us)
Async XLA Ops:
  10.5 159.3 %all-to-all-start = ((bf16[32,2,1144]{2,1,0:T(2,128)(2,1)}), bf16[32,2,1144]{2,1,0:T(2,128)(2,1)S(1)}, u32[]{:S(2)}, u32[]{:S(2)}) async-start(bf16[32,2,1144]{2,1,0:T(2,128)(2,1)} %reshape.35), calls=%async_computation | async-start | bytes 294912 | tf_op jit(solution)/shard_map/all_to_all | solution.py:37
  17.8 228.3 %all-gather.3.cloned.1.call-start = ((), (), s32[]{:S(2)}) async-start(), calls=%async_computation.1 | async-start | bytes 5271552 | tf_op jit(solution)/shard_map/all_gather | solution.py:43
  20.6 9.3 %copy-start.1 = (s32[1024]{0:T(1024)S(1)}, s32[1024]{0:T(1024)}, u32[]{:S(2)}) copy-start(s32[1024]{0:T(1024)} %param.5) | copy-start | bytes 12292
  29.9 2.5 copy-start
  156.7 17.7 %collective-permute-start = (f32[1664,48]{0,1:T(8,128)S(1)}, f32[1664,48]{0,1:T(8,128)S(1)}, u32[]{:S(2)}, u32[]{:S(2)}) collective-permute-start(f32[1664,48]{0,1:T(8,128)S(1)} %fusion), channel_id=1, source_target_pairs={{0,1},{1,2},{2,3},{3,4},{4,5},{5,6},{6,7},{7,8},{8,9},{9,10},{10,1... | collective-permute-start | bytes 958472
  159.1 15.4 %collective-permute-start.1 = (f32[1664,48]{0,1:T(8,128)S(1)}, f32[1664,48]{0,1:T(8,128)S(1)}, u32[]{:S(2)}, u32[]{:S(2)}) collective-permute-start(f32[1664,48]{0,1:T(8,128)S(1)} %fusion), channel_id=1, source_target_pairs={{0,2},{1,3},{2,4},{3,5},{4,6},{5,7},{6,8},{7,9},{8,10},{9,11},{10,... | collective-permute-start | bytes 958472
  163.4 11.1 %collective-permute-start.2 = (f32[1664,28]{0,1:T(8,128)S(1)}, f32[1664,28]{0,1:T(8,128)S(1)}, u32[]{:S(2)}, u32[]{:S(2)}) collective-permute-start(f32[1664,28]{0,1:T(8,128)S(1)} %slice), channel_id=1, source_target_pairs={{0,3},{1,4},{2,5},{3,6},{4,7},{5,8},{6,9},{7,10},{8,11},{9,12},{10... | collective-permute-start | bytes 559112
Sparse Core Ops, SparseCore 0:
  176.2 69.8 all-gather.2
where the time goes:
time: 268 us
  blocking collectives  114 us (43%)
  waiting for transfers between devices  73.4 us (27%)
  local copies, waits for them, and re-layouts  22.4 us (8%)
  matrix products  19.5 us (7%)
  starting transfers between devices  18.7 us (7%)
  between operations  13.6 us (5%)
  other arithmetic  5.96 us (2%)
    unnamed x1, blocking collectives  114 us
    all_gather x1, waiting for transfers between devices, local(): lax.all_gather(updated.astype(jnp.bfloat16), 'ex', axis=1, tiled=True)  70.1 us
    unnamed x11, local copies, waits for them, and re-layouts  17.6 us
    unnamed x3, starting transfers between devices  11.3 us
    dot_general x1, matrix products, local(): lax.dot_general(features, coef, (((0,), (0,)), ((), ())), preferred_eleme...  10.2 us
    dot_general x1, matrix products, local(): logits = jnp.dot(features, weight, preferred_element_type=jnp.float32)  9.31 us
    all_to_all x1, starting transfers between devices, local(): lax.all_to_all(noise, 'ex', split_axis=1, concat_axis=0, tiled=True)  7.33 us
  transfers between devices with their start and end apart: 5, of which 2 were waited for; matrix products, arithmetic and copies ran while one was open for 53% of the time, Pallas kernels for 0%

commit v1 on v0

v1 whole, which is shorter than its diff:
```python
import functools

import jax
import jax.numpy as jnp
from jax import lax
from jax.experimental import pallas as pl
from jax.experimental.pallas import tpu as pltpu
from jax.sharding import PartitionSpec as P

CLIP = 48.0
SIDES = 4
ROW = 8


def coefficients(features, labels, weight):
    cls_width = weight.shape[1]
    logits = jnp.dot(features, weight, preferred_element_type=jnp.float32)
    offset = lax.axis_index("cls") * cls_width
    local_lab = labels - offset
    columns = lax.broadcasted_iota(jnp.int32, (1, cls_width), 1)
    onehot = columns == local_lab[:, None]
    label_part = jnp.sum(jnp.where(onehot, logits, 0.0), axis=1)
    top = lax.pmax(jnp.max(logits, axis=1), "cls")
    expo = jnp.exp(logits - top[:, None])
    total, squares, label_logit = lax.psum(
        (jnp.sum(expo, axis=1), jnp.sum(expo * expo, axis=1), label_part), "cls"
    )
    probs = expo / total[:, None]
    label_prob = jnp.exp(label_logit - top) / total
    resid_sq = squares / (total * total) - 2.0 * label_prob + 1.0
    resid_norm = jnp.sqrt(jnp.maximum(resid_sq, 0.0))
    feat = features.astype(jnp.float32)
    feat_norm = jnp.sqrt(jnp.sum(feat * feat, axis=1))
    factor = CLIP / jnp.maximum(feat_norm * resid_norm, CLIP)
    resid = probs - onehot.astype(jnp.float32)
    return (factor[:, None] * resid).astype(jnp.bfloat16)


def place_kernel(rows, offsets_ref, *refs):
    blocks, out_ref, sems = refs[:-2], refs[-2], refs[-1]
    copies = []
    for i, block in enumerate(blocks):
        start = pl.multiple_of(offsets_ref[i] * rows, ROW)
        copies.append(
            pltpu.make_async_copy(block, out_ref.at[pl.ds(start, rows), :], sems.at[i])
        )
    for copy in copies:
        copy.start()
    for copy in copies:
        copy.wait()


def place(blocks, offsets, total):
    rows, width = blocks[0].shape
    grid_spec = pltpu.PrefetchScalarGridSpec(
        num_scalar_prefetch=1,
        grid=(1,),
        in_specs=[
            pl.BlockSpec((rows, width), lambda i, off: (0, 0)) for _ in blocks
        ],
        out_specs=pl.BlockSpec(memory_space=pl.ANY),
        scratch_shapes=[pltpu.SemaphoreType.DMA((len(blocks),))],
    )
    return pl.pallas_call(
        functools.partial(place_kernel, rows),
        grid_spec=grid_spec,
        out_shape=jax.ShapeDtypeStruct((total, width), blocks[0].dtype),
    )(offsets, *blocks)


def by_rows(features, labels, weight, noise):
    bf16, f32 = jnp.bfloat16, jnp.float32
    n = lax.axis_size("ex")
    depth, width = weight.shape
    coef = coefficients(features, labels, weight)
    partial_grad = lax.dot_general(
        features, coef, (((0,), (0,)), ((), ())), preferred_element_type=f32
    )
    me = lax.axis_index("ex")
    layers = n // (2 * SIDES)
    half, side, own = depth // 2, depth // (2 * SIDES), depth // n
    core, pos_a, pos_b, layer = me % 2, me // 2 % 2, me // 4 % 2, me // 8

    def swap(x, pairs):
        return lax.ppermute(x, "ex", pairs)

    cores = [(i, i ^ 1) for i in range(n)]
    first = [(i, i ^ (4 if i % 2 else 2)) for i in range(n)]
    second = [(i, i ^ (2 if i % 2 else 4)) for i in range(n)]
    layer_swaps = [[(i, i ^ (8 * d)) for i in range(n)] for d in range(1, layers)]

    target = []
    for d in range(n):
        c, q, k = d // (SIDES * layers), d // layers % SIDES, d % layers
        target.append((d, k * 2 * SIDES + q * 2 + c))
    noise_own = swap(noise, target)

    def block_index(far_first, far_second):
        flip_a = jnp.where(core == 0, far_first, far_second)
        flip_b = jnp.where(core == 0, far_second, far_first)
        return (pos_a ^ flip_a) + 2 * (pos_b ^ flip_b)

    def rows_of(x, start, count):
        return lax.dynamic_slice_in_dim(x, start, count, 0)

    sent = rows_of(partial_grad, half * (1 - core), half).astype(bf16)
    got = swap(sent, cores)
    kept = rows_of(partial_grad, half * core, half) + got.astype(f32)

    def side_of(far_first, far_second):
        return rows_of(kept, side * block_index(far_first, far_second), side)

    got_far = swap(side_of(1, 1).astype(bf16), first)
    got_near = swap(side_of(1, 0).astype(bf16), first)
    got_second = swap((side_of(0, 1) + got_far.astype(f32)).astype(bf16), second)
    summed = side_of(0, 0) + got_near.astype(f32) + got_second.astype(f32)

    starts = [own * k // ROW * ROW for k in range(layers)]
    window = max(
        -(-own * (k + 1) // ROW) * ROW - starts[k] for k in range(layers)
    )
    starts = [min(s, side - window) for s in starts]
    table = jnp.asarray(starts, jnp.int32)

    def window_of(k):
        return rows_of(summed, table[k], window)

    grad = window_of(layer)
    for d in range(1, layers):
        grad = grad + swap(window_of(layer ^ d).astype(bf16), layer_swaps[d - 1]).astype(f32)

    inner = own * layer - table[layer]
    noise_rows = lax.dynamic_update_slice_in_dim(
        jnp.zeros((window, width), noise.dtype), noise_own, inner, 0
    )
    begin = half * core + side * block_index(0, 0) + table[layer]
    own_weight = rows_of(weight, begin, window)
    classes = width * lax.axis_size("cls")
    batch = features.shape[0] * n
    scale = 0.1 * classes / batch
    updated = own_weight.astype(f32) - scale * (
        grad + 0.96 * CLIP * noise_rows.astype(f32)
    )
    updated = updated.astype(bf16)

    parts = [updated] + [swap(updated, layer_swaps[d - 1]) for d in range(1, layers)]
    ordered = []
    for k in range(layers):
        piece = lax.select_n(jnp.broadcast_to(layer ^ k, parts[0].shape), *parts)
        skip = own * k - starts[k]
        ordered.append(piece[skip : skip + own])
    mine = jnp.concatenate(ordered, axis=0)
    from_second = swap(mine, second)
    from_first = swap(mine, first)
    from_both = swap(from_second, first)
    here = [mine, from_second, from_first, from_both]
    there = [swap(block, cores) for block in here]
    flips = [(0, 0), (0, 1), (1, 0), (1, 1)]
    offsets = [SIDES * core + block_index(*f) for f in flips]
    offsets += [SIDES * (1 - core) + block_index(f[1], f[0]) for f in flips]
    return place(here + there, jnp.stack(offsets).astype(jnp.int32), depth)


def by_columns(features, labels, weight, noise):
    coef = coefficients(features, labels, weight)
    partial_grad = lax.dot_general(
        features, coef, (((0,), (0,)), ((), ())), preferred_element_type=jnp.float32
    )
    classes = weight.shape[1] * lax.axis_size("cls")
    batch = features.shape[0] * lax.axis_size("ex")
    scale = 0.1 * classes / batch
    grad_part = lax.psum_scatter(partial_grad, "ex", scatter_dimension=0, tiled=True)
    span = grad_part.shape[0]
    own_weight = lax.dynamic_slice_in_dim(weight, lax.axis_index("ex") * span, span, 0)
    updated = own_weight.astype(jnp.float32) - scale * (
        grad_part + 0.96 * CLIP * noise.astype(jnp.float32)
    )
    return lax.all_gather(updated.astype(jnp.bfloat16), "ex", axis=0, tiled=True)


def local(features, labels, weight, noise):
    n = lax.axis_size("ex")
    layers = n // (2 * SIDES)
    fits = n % (2 * SIDES) == 0 and layers & (layers - 1) == 0 and layers > 1
    fits = fits and weight.shape[0] % (2 * SIDES * ROW) == 0 and weight.shape[0] % n == 0
    step = by_rows if fits else by_columns
    return step(features, labels, weight, noise)


def solution(mesh):
    in_specs = (P("ex", None), P("ex"), P(None, "cls"), P("ex", "cls"))
    out_specs = P(None, "cls")
    return jax.shard_map(local, mesh=mesh, in_specs=in_specs, out_specs=out_specs, check_vma=False)
```

time: 268 us -> 138 us (0.51)
  blocking collectives: 114 us -> 0 us
  waiting for transfers between devices: 73.4 us -> 54.8 us
  local copies, waits for them, and re-layouts: 22.4 us -> 7.31 us
  starting transfers between devices: 18.7 us -> 29 us
  other arithmetic: 5.96 us -> 12.8 us
  Pallas kernels: 0 us -> 5.2 us
  between operations: 13.6 us -> 8.78 us
    unnamed x1 -> x0, blocking collectives: 114 us -> none
    all_gather x1 -> x0, waiting for transfers between devices: 70.1 us -> none  [local(): lax.all_gather(updated.astype(jnp.bfloat16), 'ex', axis=1, tiled=True)]
    ppermute x0 -> x18, waiting for transfers between devices: none -> 54.8 us  [swap(): return lax.ppermute(x, 'ex', pairs)]
    ppermute x0 -> x18, starting transfers between devices: none -> 29 us  [swap(): return lax.ppermute(x, 'ex', pairs)]
    unnamed x11 -> x20, local copies, waits for them, and re-layouts: 17.6 us -> 2.21 us
    unnamed x3 -> x0, starting transfers between devices: 11.3 us -> none
    all_to_all x1 -> x0, starting transfers between devices: 7.33 us -> none  [local(): lax.all_to_all(noise, 'ex', split_axis=1, concat_axis=0, tiled=True)]
    pallas_call x0 -> x1, Pallas kernels: none -> 5.2 us  [place(): pl.pallas_call(functools.partial(place_kernel, rows), grid_spec=grid_spec...]
  transfers between devices with their start and end apart: 5 -> 18, of which waited for: 2 -> 9; matrix products, arithmetic and copies ran while one was open for 53% -> 3% of each run, Pallas kernels for 0% -> 0%
where the time goes in v1:
time: 138 us; the launch traced here: 137 us
  waiting for transfers between devices  54.8 us (40%)
  starting transfers between devices  29 us (21%)
  matrix products  19.2 us (14%)
  other arithmetic  12.8 us (9%)
  between operations  8.78 us (6%)
  local copies, waits for them, and re-layouts  7.31 us (5%)
  Pallas kernels  5.2 us (4%)
    ppermute x18, waiting for transfers between devices, swap(): return lax.ppermute(x, 'ex', pairs)  54.8 us
    ppermute x18, starting transfers between devices, swap(): return lax.ppermute(x, 'ex', pairs)  29 us
    dot_general x1, matrix products, by_rows(): lax.dot_general(features, coef, (((0,), (0,)), ((), ())), preferred_eleme...  9.94 us
    dot_general x1, matrix products, coefficients(): logits = jnp.dot(features, weight, preferred_element_type=jnp.float32)  9.27 us
    pallas_call x1, Pallas kernels, place(): pl.pallas_call(functools.partial(place_kernel, rows), grid_spec=grid_spec...  5.2 us
    add x1, other arithmetic, by_rows(): kept = rows_of(partial_grad, half * core, half) + got.astype(f32)  3.43 us
  transfers between devices with their start and end apart: 18, of which 9 were waited for; matrix products, arithmetic and copies ran while one was open for 3% of the time, Pallas kernels for 0%

profile of v1, /device:TPU:0, one launch (start us, length us, event | category | flops | bytes accessed | tf_op | source)
XLA Modules:
  0.0 137.2 jit_solution(9505417798411494661)
XLA Ops:
  0.0 2.7 %multiply_reduce_fusion = f32[1024]{0:T(1024)S(1)} fusion(bf16[1024,1664]{1,0:T(8,128)(2,1)} %param.5), kind=kLoop, calls=%fused_computation | loop fusion | flops 5110784 | bytes 3411968 | tf_op jit(solution)/shard_map/reduce_sum | solution.py:33
  2.7 0.0 copy-start.9
  2.7 9.3 %fusion.8 = (f32[1024]{0:T(1024)S(1)}, f32[1024,1408]{1,0:T(8,128)S(1)}) fusion(bf16[1024,1664]{1,0:T(8,128)(2,1)} %param.5, bf16[1664,1408]{1,0:T(8,128)(2,1)} %param.7), kind=kOutput, calls=%fused_computation.30 | convolution fusion | flops 4799724544 | bytes 13864960 | tf_op jit(solution)/shard_map/dot_general | solution.py:17
  12.0 0.0 copy-start.1
  12.0 0.0 copy-done.9
  12.0 2.4 %multiply_reduce_fusion.1 = (f32[1024]{0:T(1024)S(1)}, f32[1024]{0:T(1024)S(1)}, f32[1024]{0:T(1024)S(1)}) fusion(f32[1024,1408]{1,0:T(8,128)S(1)} %get-tuple-element.22, f32[1024]{0:T(1024)S(1)} %get-tuple-element.21, s32[1024]{0:T(1024)S(1)} %copy-done.9), kind=kLoop, calls=%fused_computation.4 | loop fusion | flops 10089472 | bytes 5787648 | tf_op jit(solution)/shard_map/reduce_sum | solution.py:26
  14.4 0.0 copy-done.1
  14.4 9.9 %fusion.1 = f32[1408,1664]{0,1:T(8,128)} fusion(bf16[1024,1664]{1,0:T(8,128)(2,1)S(1)} %copy-done.1, f32[1024,1408]{1,0:T(8,128)S(1)} %get-tuple-element.22, f32[1024]{0:T(1024)S(1)} %get-tuple-element.6, f32[1024]{0:T(1024)S(1)} %maximum_divide_fusion, s32[1024]{0:T(1024)S(1)} %copy-done.9, f32[1024]{0:T(1024)S(1)} %get-tuple-element.21), kind=kOutput, calls=%fused_computation.9 | convolution fusion | flops 4808376320 | bytes 18563072 | tf_op jit(solution)/shard_map/dot_general | solution.py:76
  24.4 2.6 %fusion.6 = bf16[832,1408]{1,0:T(8,128)(2,1)S(1)} fusion(f32[1408,1664]{0,1:T(8,128)} %fusion.1, s32[]{:T(128)S(6)} %select_n.208), kind=kLoop, calls=%fused_computation.14 | loop fusion | bytes 4685828 | tf_op jit(solution)/shard_map/convert_element_type | solution.py:106
  27.0 0.6 collective-permute-start
  27.5 4.3 %collective-permute-done = bf16[832,1408]{1,0:T(8,128)(2,1)} collective-permute-done((bf16[832,1408]{1,0:T(8,128)(2,1)S(1)}, bf16[832,1408]{1,0:T(8,128)(2,1)}, u32[]{:S(2)}, u32[]{:S(2)}) %collective-permute-start) | collective-permute-done | bytes 2342944 | tf_op jit(solution)/shard_map/ppermute | solution.py:85
  31.8 3.4 %bitcast_add_fusion = f32[832,1408]{1,0:T(8,128)S(1)} fusion(bf16[832,1408]{1,0:T(8,128)(2,1)} %collective-permute-done, f32[1408,1664]{0,1:T(8,128)} %fusion.1, s32[]{:T(128)S(6)} %select_n.207), kind=kLoop, calls=%fused_computation.6 | loop fusion | flops 2342912 | bytes 11714564 | tf_op jit(solution)/shard_map/add | solution.py:108
  35.2 0.0 copy-start
  35.3 2.2 %copy-done = f32[832,1408]{1,0:T(8,128)} copy-done((f32[832,1408]{1,0:T(8,128)}, f32[832,1408]{1,0:T(8,128)S(1)}, u32[]{:S(2)}) %copy-start) | copy-done | bytes 4685848
  37.4 0.1 dynamic-slice_convert_fusion.2
  37.6 2.9 %collective-permute-start.2 = (bf16[208,1408]{1,0:T(8,128)(2,1)S(1)}, bf16[208,1408]{1,0:T(8,128)(2,1)S(1)}, u32[]{:S(2)}, u32[]{:S(2)}) collective-permute-start(bf16[208,1408]{1,0:T(8,128)(2,1)S(1)} %get-tuple-element.9), channel_id=1, source_target_pairs={{0,2},{1,5},{2,0},{3,7},{4,6},{5,1},{6,4},{7,3},{8,10},{9,13},{10,... | collective-permute-start | bytes 1757192 | tf_op jit(solution)/shard_map/ppermute | solution.py:85
  40.5 0.1 collective-permute-start.1
  40.6 7.7 %collective-permute-done.2 = bf16[208,1408]{1,0:T(8,128)(2,1)S(1)} collective-permute-done((bf16[208,1408]{1,0:T(8,128)(2,1)S(1)}, bf16[208,1408]{1,0:T(8,128)(2,1)S(1)}, u32[]{:S(2)}, u32[]{:S(2)}) %collective-permute-start.2) | collective-permute-done | bytes 585760 | tf_op jit(solution)/shard_map/ppermute | solution.py:85
  48.3 1.4 %add_convert_fusion = bf16[208,1408]{1,0:T(8,128)(2,1)S(1)} fusion(bf16[208,1408]{1,0:T(8,128)(2,1)S(1)} %collective-permute-done.2, f32[832,1408]{1,0:T(8,128)} %copy-done, s32[]{:T(128)S(6)} %select_n.211), kind=kLoop, calls=%fused_computation.16 | loop fusion | flops 878592 | bytes 2342916 | tf_op jit(solution)/shard_map/convert_element_type | solution.py:115
  49.7 2.1 %collective-permute-start.3 = (bf16[208,1408]{1,0:T(8,128)(2,1)S(1)}, bf16[208,1408]{1,0:T(8,128)(2,1)S(1)}, u32[]{:S(2)}, u32[]{:S(2)}) collective-permute-start(bf16[208,1408]{1,0:T(8,128)(2,1)S(1)} %add_convert_fusion), channel_id=1, source_target_pairs={{0,4},{1,3},{2,6},{3,1},{4,0},{5,7},{6,2},{7,5},{8,12},{9,11},{10,... | collective-permute-start | bytes 1757192 | tf_op jit(solution)/shard_map/ppermute | solution.py:85
  51.8 0.0 copy-done.8
  51.8 0.7 fusion.7
  57.9 0.0 collective-permute-done.1
  57.9 2.5 %collective-permute-done.3 = bf16[208,1408]{1,0:T(8,128)(2,1)S(1)} collective-permute-done((bf16[208,1408]{1,0:T(8,128)(2,1)S(1)}, bf16[208,1408]{1,0:T(8,128)(2,1)S(1)}, u32[]{:S(2)}, u32[]{:S(2)}) %collective-permute-start.3) | collective-permute-done | bytes 585760 | tf_op jit(solution)/shard_map/ppermute | solution.py:85
  60.4 1.5 %convert_add_fusion = f32[208,1408]{1,0:T(8,128)S(1)} fusion(bf16[208,1408]{1,0:T(8,128)(2,1)S(1)} %collective-permute-done.3, bf16[208,1408]{1,0:T(8,128)(2,1)S(1)} %collective-permute-done.1, f32[832,1408]{1,0:T(8,128)} %copy-done, s32[]{:T(128)S(6)} %select_n.209), kind=kLoop, calls=%fused_computation.15 | loop fusion | flops 1171456 | bytes 3514372 | tf_op jit(solution)/shard_map/add | solution.py:116
  61.8 0.1 dynamic-slice_convert_fusion.5
  61.9 1.8 %collective-permute-start.4 = (bf16[56,1408]{1,0:T(8,128)(2,1)S(1)}, bf16[56,1408]{1,0:T(8,128)(2,1)S(1)}, u32[]{:S(2)}, u32[]{:S(2)}) collective-permute-start(bf16[56,1408]{1,0:T(8,128)(2,1)S(1)} %get-tuple-element.10), channel_id=1, source_target_pairs={{0,8},{1,9},{2,10},{3,11},{4,12},{5,13},{6,14},{7,15},{8,0},{9,1},... | collective-permute-start | bytes 473096 | tf_op jit(solution)/shard_map/ppermute | solution.py:85
  63.8 2.6 %collective-permute-start.5 = (bf16[56,1408]{1,0:T(8,128)(2,1)S(1)}, bf16[56,1408]{1,0:T(8,128)(2,1)S(1)}, u32[]{:S(2)}, u32[]{:S(2)}) collective-permute-start(bf16[56,1408]{1,0:T(8,128)(2,1)S(1)} %get-tuple-element.12), channel_id=1, source_target_pairs={{0,16},{1,17},{2,18},{3,19},{4,20},{5,21},{6,22},{7,23},{8,24},{9,... | collective-permute-start | bytes 473096 | tf_op jit(solution)/shard_map/ppermute | solution.py:85
  66.3 0.0 collective-permute-start.6
  66.4 1.6 %collective-permute-start.7 = (bf16[52,1408]{1,0:T(8,128)(2,1)}, bf16[52,1408]{1,0:T(8,128)(2,1)S(1)}, u32[]{:S(2)}, u32[]{:S(2)}) collective-permute-start(bf16[52,1408]{1,0:T(8,128)(2,1)} %param.8), channel_id=1, source_target_pairs={{0,0},{1,8},{2,16},{3,24},{4,2},{5,10},{6,18},{7,26},{8,4},{9,12},... | collective-permute-start | bytes 439304 | tf_op jit(solution)/shard_map/ppermute | solution.py:85
  71.1 0.0 collective-permute-done.7
  71.1 1.0 dynamic_update_slice.3
  72.1 0.0 collective-permute-done.4
  72.1 9.7 %collective-permute-done.5 = bf16[56,1408]{1,0:T(8,128)(2,1)S(1)} collective-permute-done((bf16[56,1408]{1,0:T(8,128)(2,1)S(1)}, bf16[56,1408]{1,0:T(8,128)(2,1)S(1)}, u32[]{:S(2)}, u32[]{:S(2)}) %collective-permute-start.5) | collective-permute-done | bytes 157728 | tf_op jit(solution)/shard_map/ppermute | solution.py:85
  81.8 0.0 collective-permute-done.6
  81.8 1.1 subtract_convert_fusion
  82.9 2.3 %collective-permute-start.10 = (bf16[56,1408]{1,0:T(8,128)(2,1)S(1)}, bf16[56,1408]{1,0:T(8,128)(2,1)S(1)}, u32[]{:S(2)}, u32[]{:S(2)}) collective-permute-start(bf16[56,1408]{1,0:T(8,128)(2,1)S(1)} %subtract_convert_fusion), channel_id=1, source_target_pairs={{0,24},{1,25},{2,26},{3,27},{4,28},{5,29},{6,30},{7,31},{8,16},{9,... | collective-permute-start | bytes 473096 | tf_op jit(solution)/shard_map/ppermute | solution.py:85
  85.2 5.1 %collective-permute-start.8 = (bf16[56,1408]{1,0:T(8,128)(2,1)S(1)}, bf16[56,1408]{1,0:T(8,128)(2,1)S(1)}, u32[]{:S(2)}, u32[]{:S(2)}) collective-permute-start(bf16[56,1408]{1,0:T(8,128)(2,1)S(1)} %subtract_convert_fusion), channel_id=1, source_target_pairs={{0,8},{1,9},{2,10},{3,11},{4,12},{5,13},{6,14},{7,15},{8,0},{9,1},... | collective-permute-start | bytes 473096 | tf_op jit(solution)/shard_map/ppermute | solution.py:85
  90.4 0.0 collective-permute-start.9
  90.4 0.0 collective-permute-done.10
  90.4 4.5 %collective-permute-done.8 = bf16[56,1408]{1,0:T(8,128)(2,1)S(1)} collective-permute-done((bf16[56,1408]{1,0:T(8,128)(2,1)S(1)}, bf16[56,1408]{1,0:T(8,128)(2,1)S(1)}, u32[]{:S(2)}, u32[]{:S(2)}) %collective-permute-start.8) | collective-permute-done | bytes 157728 | tf_op jit(solution)/shard_map/ppermute | solution.py:85
  94.8 8.2 %collective-permute-done.9 = bf16[56,1408]{1,0:T(8,128)(2,1)S(1)} collective-permute-done((bf16[56,1408]{1,0:T(8,128)(2,1)S(1)}, bf16[56,1408]{1,0:T(8,128)(2,1)S(1)}, u32[]{:S(2)}, u32[]{:S(2)}) %collective-permute-start.9) | collective-permute-done | bytes 157728 | tf_op jit(solution)/shard_map/ppermute | solution.py:85
  103.1 0.1 select_select_fusion.3
  103.1 0.2 select_select_fusion.2
  103.3 0.1 pad_maximum_fusion.refs_0_
  103.5 0.0 copy-start.2
  103.5 1.5 %collective-permute-start.11 = (bf16[208,1408]{1,0:T(8,128)(2,1)S(1)}, bf16[208,1408]{1,0:T(8,128)(2,1)S(1)}, u32[]{:S(2)}, u32[]{:S(2)}) collective-permute-start(bf16[208,1408]{1,0:T(8,128)(2,1)S(1)} %pad_maximum_fusion.refs_0_), channel_id=1, source_target_pairs={{0,4},{1,3},{2,6},{3,1},{4,0},{5,7},{6,2},{7,5},{8,12},{9,11},{10,... | collective-permute-start | bytes 1757192 | tf_op jit(solution)/shard_map/ppermute | solution.py:85
  104.9 3.5 %collective-permute-start.12 = (bf16[208,1408]{1,0:T(8,128)(2,1)S(1)}, bf16[208,1408]{1,0:T(8,128)(2,1)S(1)}, u32[]{:S(2)}, u32[]{:S(2)}) collective-permute-start(bf16[208,1408]{1,0:T(8,128)(2,1)S(1)} %pad_maximum_fusion.refs_0_), channel_id=1, source_target_pairs={{0,2},{1,5},{2,0},{3,7},{4,6},{5,1},{6,4},{7,3},{8,10},{9,13},{10,... | collective-permute-start | bytes 1757192 | tf_op jit(solution)/shard_map/ppermute | solution.py:85
  108.4 9.3 %collective-permute-done.11.refs_1_ = bf16[208,1408]{1,0:T(8,128)(2,1)S(1)} collective-permute-done((bf16[208,1408]{1,0:T(8,128)(2,1)S(1)}, bf16[208,1408]{1,0:T(8,128)(2,1)S(1)}, u32[]{:S(2)}, u32[]{:S(2)}) %collective-permute-start.11) | collective-permute-done | bytes 585760 | tf_op jit(solution)/shard_map/ppermute | solution.py:85
  117.7 4.3 %collective-permute-start.13 = (bf16[208,1408]{1,0:T(8,128)(2,1)S(1)}, bf16[208,1408]{1,0:T(8,128)(2,1)S(1)}, u32[]{:S(2)}, u32[]{:S(2)}) collective-permute-start(bf16[208,1408]{1,0:T(8,128)(2,1)S(1)} %collective-permute-done.11.refs_1_), channel_id=1, source_target_pairs={{0,2},{1,5},{2,0},{3,7},{4,6},{5,1},{6,4},{7,3},{8,10},{9,13},{10,... | collective-permute-start | bytes 1757192 | tf_op jit(solution)/shard_map/ppermute | solution.py:85
  122.0 0.0 collective-permute-start.14
  122.0 0.5 collective-permute-start.15
  122.5 0.0 collective-permute-done.12.refs_2_
  122.5 0.1 collective-permute-start.16
  122.6 7.2 %collective-permute-done.13.refs_3_ = bf16[208,1408]{1,0:T(8,128)(2,1)S(1)} collective-permute-done((bf16[208,1408]{1,0:T(8,128)(2,1)S(1)}, bf16[208,1408]{1,0:T(8,128)(2,1)S(1)}, u32[]{:S(2)}, u32[]{:S(2)}) %collective-permute-start.13) | collective-permute-done | bytes 585760 | tf_op jit(solution)/shard_map/ppermute | solution.py:85
  129.8 0.0 collective-permute-start.17
  129.8 0.7 stack.35.offsets_ref
  130.5 0.0 collective-permute-done.14.refs_4_
  130.5 0.0 collective-permute-done.15.refs_5_
  130.5 0.0 copy-start.7
  130.5 0.0 collective-permute-done.16.refs_6_
  130.5 1.4 %collective-permute-done.17.refs_7_ = bf16[208,1408]{1,0:T(8,128)(2,1)} collective-permute-done((bf16[208,1408]{1,0:T(8,128)(2,1)S(1)}, bf16[208,1408]{1,0:T(8,128)(2,1)}, u32[]{:S(2)}, u32[]{:S(2)}) %collective-permute-start.17) | collective-permute-done | bytes 585760 | tf_op jit(solution)/shard_map/ppermute | solution.py:85
  132.0 0.0 copy-done.2
  132.0 5.2 %shard_map.55 = bf16[1664,1408]{1,0:T(8,128)(2,1)} custom-call(s32[8]{0:T(128)} %stack.35.offsets_ref, bf16[208,1408]{1,0:T(8,128)(2,1)} %copy-done.2, bf16[208,1408]{1,0:T(8,128)(2,1)} %copy-done.3, bf16[208,1408]{1,0:T(8,128)(2,1)} %copy-done.4, bf16[208,1408]{1,0:T(8,128)(2,1)} %copy-done.5, bf16[208,1408]{1,0:T(8,128)(2,1)} %copy-done.6, ...), custom_call_target="tpu_custom_call" | custom-call | tf_op jit(solution)/shard_map/pallas_call | solution.py:64
  (12 shorter events, 0.1 us)
Async XLA Ops:
  2.7 9.3 %copy-start.9 = (s32[1024]{0:T(1024)S(1)}, s32[1024]{0:T(1024)}, u32[]{:S(2)}) copy-start(s32[1024]{0:T(1024)} %param.6) | copy-start | bytes 12292
  12.0 2.4 %copy-start.1 = (bf16[1024,1664]{1,0:T(8,128)(2,1)S(1)}, bf16[1024,1664]{1,0:T(8,128)(2,1)}, u32[]{:S(2)}) copy-start(bf16[1024,1664]{1,0:T(8,128)(2,1)} %param.5) | copy-start | bytes 10223620
  27.0 4.8 %collective-permute-start = (bf16[832,1408]{1,0:T(8,128)(2,1)S(1)}, bf16[832,1408]{1,0:T(8,128)(2,1)}, u32[]{:S(2)}, u32[]{:S(2)}) collective-permute-start(bf16[832,1408]{1,0:T(8,128)(2,1)S(1)} %fusion.6), channel_id=1, source_target_pairs={{0,1},{1,0},{2,3},{3,2},{4,5},{5,4},{6,7},{7,6},{8,9},{9,8},{10,11... | collective-permute-start | bytes 7028744 | tf_op jit(solution)/shard_map/ppermute | solution.py:85
  35.2 2.2 %copy-start = (f32[832,1408]{1,0:T(8,128)}, f32[832,1408]{1,0:T(8,128)S(1)}, u32[]{:S(2)}) copy-start(f32[832,1408]{1,0:T(8,128)S(1)} %bitcast_add_fusion) | copy-start | bytes 14057476
  37.4 14.4 %copy-start.8 = (s32[4]{0:T(128)S(1)}, s32[4]{0:T(128)}, u32[]{:S(2)}) copy-start(s32[4]{0:T(128)} %constant.96.clone) | copy-start | bytes 52
  37.6 10.7 %collective-permute-start.2 = (bf16[208,1408]{1,0:T(8,128)(2,1)S(1)}, bf16[208,1408]{1,0:T(8,128)(2,1)S(1)}, u32[]{:S(2)}, u32[]{:S(2)}) collective-permute-start(bf16[208,1408]{1,0:T(8,128)(2,1)S(1)} %get-tuple-element.9), channel_id=1, source_target_pairs={{0,2},{1,5},{2,0},{3,7},{4,6},{5,1},{6,4},{7,3},{8,10},{9,13},{10,... | collective-permute-start | bytes 1757192 | tf_op jit(solution)/shard_map/ppermute | solution.py:85
  40.5 17.4 %collective-permute-start.1 = (bf16[208,1408]{1,0:T(8,128)(2,1)S(1)}, bf16[208,1408]{1,0:T(8,128)(2,1)S(1)}, u32[]{:S(2)}, u32[]{:S(2)}) collective-permute-start(bf16[208,1408]{1,0:T(8,128)(2,1)S(1)} %get-tuple-element.8), channel_id=1, source_target_pairs={{0,2},{1,5},{2,0},{3,7},{4,6},{5,1},{6,4},{7,3},{8,10},{9,13},{10,... | collective-permute-start | bytes 1757192 | tf_op jit(solution)/shard_map/ppermute | solution.py:85
  49.7 10.7 %collective-permute-start.3 = (bf16[208,1408]{1,0:T(8,128)(2,1)S(1)}, bf16[208,1408]{1,0:T(8,128)(2,1)S(1)}, u32[]{:S(2)}, u32[]{:S(2)}) collective-permute-start(bf16[208,1408]{1,0:T(8,128)(2,1)S(1)} %add_convert_fusion), channel_id=1, source_target_pairs={{0,4},{1,3},{2,6},{3,1},{4,0},{5,7},{6,2},{7,5},{8,12},{9,11},{10,... | collective-permute-start | bytes 1757192 | tf_op jit(solution)/shard_map/ppermute | solution.py:85
  61.9 10.2 %collective-permute-start.4 = (bf16[56,1408]{1,0:T(8,128)(2,1)S(1)}, bf16[56,1408]{1,0:T(8,128)(2,1)S(1)}, u32[]{:S(2)}, u32[]{:S(2)}) collective-permute-start(bf16[56,1408]{1,0:T(8,128)(2,1)S(1)} %get-tuple-element.10), channel_id=1, source_target_pairs={{0,8},{1,9},{2,10},{3,11},{4,12},{5,13},{6,14},{7,15},{8,0},{9,1},... | collective-permute-start | bytes 473096 | tf_op jit(solution)/shard_map/ppermute | solution.py:85
  63.8 18.1 %collective-permute-start.5 = (bf16[56,1408]{1,0:T(8,128)(2,1)S(1)}, bf16[56,1408]{1,0:T(8,128)(2,1)S(1)}, u32[]{:S(2)}, u32[]{:S(2)}) collective-permute-start(bf16[56,1408]{1,0:T(8,128)(2,1)S(1)} %get-tuple-element.12), channel_id=1, source_target_pairs={{0,16},{1,17},{2,18},{3,19},{4,20},{5,21},{6,22},{7,23},{8,24},{9,... | collective-permute-start | bytes 473096 | tf_op jit(solution)/shard_map/ppermute | solution.py:85
  66.3 15.5 %collective-permute-start.6 = (bf16[56,1408]{1,0:T(8,128)(2,1)S(1)}, bf16[56,1408]{1,0:T(8,128)(2,1)S(1)}, u32[]{:S(2)}, u32[]{:S(2)}) collective-permute-start(bf16[56,1408]{1,0:T(8,128)(2,1)S(1)} %get-tuple-element.11), channel_id=1, source_target_pairs={{0,24},{1,25},{2,26},{3,27},{4,28},{5,29},{6,30},{7,31},{8,16},{9,... | collective-permute-start | bytes 473096 | tf_op jit(solution)/shard_map/ppermute | solution.py:85
  66.4 4.7 %collective-permute-start.7 = (bf16[52,1408]{1,0:T(8,128)(2,1)}, bf16[52,1408]{1,0:T(8,128)(2,1)S(1)}, u32[]{:S(2)}, u32[]{:S(2)}) collective-permute-start(bf16[52,1408]{1,0:T(8,128)(2,1)} %param.8), channel_id=1, source_target_pairs={{0,0},{1,8},{2,16},{3,24},{4,2},{5,10},{6,18},{7,26},{8,4},{9,12},... | collective-permute-start | bytes 439304 | tf_op jit(solution)/shard_map/ppermute | solution.py:85
  82.9 7.5 %collective-permute-start.10 = (bf16[56,1408]{1,0:T(8,128)(2,1)S(1)}, bf16[56,1408]{1,0:T(8,128)(2,1)S(1)}, u32[]{:S(2)}, u32[]{:S(2)}) collective-permute-start(bf16[56,1408]{1,0:T(8,128)(2,1)S(1)} %subtract_convert_fusion), channel_id=1, source_target_pairs={{0,24},{1,25},{2,26},{3,27},{4,28},{5,29},{6,30},{7,31},{8,16},{9,... | collective-permute-start | bytes 473096 | tf_op jit(solution)/shard_map/ppermute | solution.py:85
  85.2 9.6 %collective-permute-start.8 = (bf16[56,1408]{1,0:T(8,128)(2,1)S(1)}, bf16[56,1408]{1,0:T(8,128)(2,1)S(1)}, u32[]{:S(2)}, u32[]{:S(2)}) collective-permute-start(bf16[56,1408]{1,0:T(8,128)(2,1)S(1)} %subtract_convert_fusion), channel_id=1, source_target_pairs={{0,8},{1,9},{2,10},{3,11},{4,12},{5,13},{6,14},{7,15},{8,0},{9,1},... | collective-permute-start | bytes 473096 | tf_op jit(solution)/shard_map/ppermute | solution.py:85
  90.4 12.7 %collective-permute-start.9 = (bf16[56,1408]{1,0:T(8,128)(2,1)S(1)}, bf16[56,1408]{1,0:T(8,128)(2,1)S(1)}, u32[]{:S(2)}, u32[]{:S(2)}) collective-permute-start(bf16[56,1408]{1,0:T(8,128)(2,1)S(1)} %subtract_convert_fusion), channel_id=1, source_target_pairs={{0,16},{1,17},{2,18},{3,19},{4,20},{5,21},{6,22},{7,23},{8,24},{9,... | collective-permute-start | bytes 473096 | tf_op jit(solution)/shard_map/ppermute | solution.py:85
  103.5 28.5 %copy-start.2 = (bf16[208,1408]{1,0:T(8,128)(2,1)}, bf16[208,1408]{1,0:T(8,128)(2,1)S(1)}, u32[]{:S(2)}) copy-start(bf16[208,1408]{1,0:T(8,128)(2,1)S(1)} %pad_maximum_fusion.refs_0_) | copy-start | bytes 1757188
  103.5 14.3 %collective-permute-start.11 = (bf16[208,1408]{1,0:T(8,128)(2,1)S(1)}, bf16[208,1408]{1,0:T(8,128)(2,1)S(1)}, u32[]{:S(2)}, u32[]{:S(2)}) collective-permute-start(bf16[208,1408]{1,0:T(8,128)(2,1)S(1)} %pad_maximum_fusion.refs_0_), channel_id=1, source_target_pairs={{0,4},{1,3},{2,6},{3,1},{4,0},{5,7},{6,2},{7,5},{8,12},{9,11},{10,... | collective-permute-start | bytes 1757192 | tf_op jit(solution)/shard_map/ppermute | solution.py:85
  104.9 17.6 %collective-permute-start.12 = (bf16[208,1408]{1,0:T(8,128)(2,1)S(1)}, bf16[208,1408]{1,0:T(8,128)(2,1)S(1)}, u32[]{:S(2)}, u32[]{:S(2)}) collective-permute-start(bf16[208,1408]{1,0:T(8,128)(2,1)S(1)} %pad_maximum_fusion.refs_0_), channel_id=1, source_target_pairs={{0,2},{1,5},{2,0},{3,7},{4,6},{5,1},{6,4},{7,3},{8,10},{9,13},{10,... | collective-permute-start | bytes 1757192 | tf_op jit(solution)/shard_map/ppermute | solution.py:85
  117.7 14.2 %copy-start.3 = (bf16[208,1408]{1,0:T(8,128)(2,1)}, bf16[208,1408]{1,0:T(8,128)(2,1)S(1)}, u32[]{:S(2)}) copy-start(bf16[208,1408]{1,0:T(8,128)(2,1)S(1)} %collective-permute-done.11.refs_1_) | copy-start | bytes 1757188
  117.7 12.1 %collective-permute-start.13 = (bf16[208,1408]{1,0:T(8,128)(2,1)S(1)}, bf16[208,1408]{1,0:T(8,128)(2,1)S(1)}, u32[]{:S(2)}, u32[]{:S(2)}) collective-permute-start(bf16[208,1408]{1,0:T(8,128)(2,1)S(1)} %collective-permute-done.11.refs_1_), channel_id=1, source_target_pairs={{0,2},{1,5},{2,0},{3,7},{4,6},{5,1},{6,4},{7,3},{8,10},{9,13},{10,... | collective-permute-start | bytes 1757192 | tf_op jit(solution)/shard_map/ppermute | solution.py:85
  122.0 8.5 %collective-permute-start.14 = (bf16[208,1408]{1,0:T(8,128)(2,1)S(1)}, bf16[208,1408]{1,0:T(8,128)(2,1)S(1)}, u32[]{:S(2)}, u32[]{:S(2)}) collective-permute-start(bf16[208,1408]{1,0:T(8,128)(2,1)S(1)} %pad_maximum_fusion.refs_0_), channel_id=1, source_target_pairs={{0,1},{1,0},{2,3},{3,2},{4,5},{5,4},{6,7},{7,6},{8,9},{9,8},{10,11... | collective-permute-start | bytes 1757192 | tf_op jit(solution)/shard_map/ppermute | solution.py:85
  122.0 8.5 %collective-permute-start.15 = (bf16[208,1408]{1,0:T(8,128)(2,1)S(1)}, bf16[208,1408]{1,0:T(8,128)(2,1)S(1)}, u32[]{:S(2)}, u32[]{:S(2)}) collective-permute-start(bf16[208,1408]{1,0:T(8,128)(2,1)S(1)} %collective-permute-done.11.refs_1_), channel_id=1, source_target_pairs={{0,1},{1,0},{2,3},{3,2},{4,5},{5,4},{6,7},{7,6},{8,9},{9,8},{10,11... | collective-permute-start | bytes 1757192 | tf_op jit(solution)/shard_map/ppermute | solution.py:85
  122.5 9.4 %copy-start.4 = (bf16[208,1408]{1,0:T(8,128)(2,1)}, bf16[208,1408]{1,0:T(8,128)(2,1)S(1)}, u32[]{:S(2)}) copy-start(bf16[208,1408]{1,0:T(8,128)(2,1)S(1)} %collective-permute-done.12.refs_2_) | copy-start | bytes 1757188
  122.5 8.0 %collective-permute-start.16 = (bf16[208,1408]{1,0:T(8,128)(2,1)S(1)}, bf16[208,1408]{1,0:T(8,128)(2,1)}, u32[]{:S(2)}, u32[]{:S(2)}) collective-permute-start(bf16[208,1408]{1,0:T(8,128)(2,1)S(1)} %collective-permute-done.12.refs_2_), channel_id=1, source_target_pairs={{0,1},{1,0},{2,3},{3,2},{4,5},{5,4},{6,7},{7,6},{8,9},{9,8},{10,11... | collective-permute-start | bytes 1757192 | tf_op jit(solution)/shard_map/ppermute | solution.py:85
  129.8 2.1 %copy-start.5 = (bf16[208,1408]{1,0:T(8,128)(2,1)}, bf16[208,1408]{1,0:T(8,128)(2,1)S(1)}, u32[]{:S(2)}) copy-start(bf16[208,1408]{1,0:T(8,128)(2,1)S(1)} %collective-permute-done.13.refs_3_) | copy-start | bytes 1757188
  129.8 2.1 %collective-permute-start.17 = (bf16[208,1408]{1,0:T(8,128)(2,1)S(1)}, bf16[208,1408]{1,0:T(8,128)(2,1)}, u32[]{:S(2)}, u32[]{:S(2)}) collective-permute-start(bf16[208,1408]{1,0:T(8,128)(2,1)S(1)} %collective-permute-done.13.refs_3_), channel_id=1, source_target_pairs={{0,1},{1,0},{2,3},{3,2},{4,5},{5,4},{6,7},{7,6},{8,9},{9,8},{10,11... | collective-permute-start | bytes 1757192 | tf_op jit(solution)/shard_map/ppermute | solution.py:85
  130.5 1.5 %copy-start.6 = (bf16[208,1408]{1,0:T(8,128)(2,1)}, bf16[208,1408]{1,0:T(8,128)(2,1)S(1)}, u32[]{:S(2)}) copy-start(bf16[208,1408]{1,0:T(8,128)(2,1)S(1)} %collective-permute-done.14.refs_4_) | copy-start | bytes 1757188
  130.5 1.5 %copy-start.7 = (bf16[208,1408]{1,0:T(8,128)(2,1)}, bf16[208,1408]{1,0:T(8,128)(2,1)S(1)}, u32[]{:S(2)}) copy-start(bf16[208,1408]{1,0:T(8,128)(2,1)S(1)} %collective-permute-done.15.refs_5_) | copy-start | bytes 1757188

commit v2 on v0

v2 whole, which is shorter than its diff:
```python
import jax
import jax.numpy as jnp
from jax import lax
from jax.experimental import pallas as pl
from jax.experimental.pallas import tpu as pltpu
from jax.sharding import PartitionSpec as P

CLIP = 48.0
SIDES = 4
ROW, LANE = 8, 128


def coefficients(features, labels, weight):
    cls_width = weight.shape[1]
    logits = jnp.dot(features, weight, preferred_element_type=jnp.float32)
    offset = lax.axis_index("cls") * cls_width
    local_lab = labels - offset
    columns = lax.broadcasted_iota(jnp.int32, (1, cls_width), 1)
    onehot = columns == local_lab[:, None]
    label_part = jnp.sum(jnp.where(onehot, logits, 0.0), axis=1)
    top = lax.pmax(jnp.max(logits, axis=1), "cls")
    expo = jnp.exp(logits - top[:, None])
    total, squares, label_logit = lax.psum(
        (jnp.sum(expo, axis=1), jnp.sum(expo * expo, axis=1), label_part), "cls"
    )
    probs = expo / total[:, None]
    label_prob = jnp.exp(label_logit - top) / total
    resid_sq = squares / (total * total) - 2.0 * label_prob + 1.0
    resid_norm = jnp.sqrt(jnp.maximum(resid_sq, 0.0))
    feat = features.astype(jnp.float32)
    feat_norm = jnp.sqrt(jnp.sum(feat * feat, axis=1))
    factor = CLIP / jnp.maximum(feat_norm * resid_norm, CLIP)
    resid = probs - onehot.astype(jnp.float32)
    return (factor[:, None] * resid).astype(jnp.bfloat16)


def copy_out(rows_ref, blocks, columns, out_ref, sems):
    copies = []
    for i, (block, first) in enumerate(zip(blocks, columns)):
        count, width = block.shape
        start = pl.multiple_of(rows_ref[i], ROW)
        place_at = out_ref.at[pl.ds(start, count), pl.ds(first, width)]
        copies.append(pltpu.make_async_copy(block, place_at, sems.at[i]))
    for copy in copies:
        copy.start()
    for copy in copies:
        copy.wait()


def place(blocks, rows, columns, shape, into=None):
    def kernel(rows_ref, *refs):
        out_ref, sems = refs[-2:]
        copy_out(rows_ref, refs[: len(blocks)], columns, out_ref, sems)

    where = pl.BlockSpec(memory_space=pl.ANY)
    extra = () if into is None else (into,)
    return pl.pallas_call(
        kernel,
        in_specs=[pl.BlockSpec(memory_space=pltpu.SMEM)]
        + [where] * (len(blocks) + len(extra)),
        out_specs=where,
        out_shape=jax.ShapeDtypeStruct(shape, blocks[0].dtype),
        scratch_shapes=[pltpu.SemaphoreType.DMA((len(blocks),))],
        input_output_aliases={len(blocks) + 1: 0} if extra else {},
        compiler_params=pltpu.CompilerParams(vmem_limit_bytes=1 << 20),
    )(jnp.stack(rows).astype(jnp.int32), *blocks, *extra)


def cut(total, pieces):
    own = total // pieces
    starts = [own * k // ROW * ROW for k in range(pieces)]
    window = max(-(-own * (k + 1) // ROW) * ROW - starts[k] for k in range(pieces))
    return [min(s, total - window) for s in starts], window


def rows_of(x, start, count):
    return lax.dynamic_slice_in_dim(x, start, count, 0)


def narrow_share(width):
    tiles = width // LANE
    return max(1, round(tiles * 4 / 11)) * LANE


class Ring:
    def __init__(self):
        n = self.n = lax.axis_size("ex")
        me = lax.axis_index("ex")
        self.layers = n // (2 * SIDES)
        self.core, self.layer = me % 2, me // (2 * SIDES)
        self.side = me // 2 % SIDES
        self.cores = [(i, i ^ 1) for i in range(n)]
        self.first = [(i, i ^ (4 if i % 2 else 2)) for i in range(n)]
        self.second = [(i, i ^ (2 if i % 2 else 4)) for i in range(n)]

    def swap(self, x, pairs):
        return lax.ppermute(x, "ex", pairs)

    def up(self, x, d):
        return self.swap(x, [(i, i ^ (2 * SIDES * d)) for i in range(self.n)])

    def side_at(self, far_first, far_second):
        flip_a = jnp.where(self.core == 0, far_first, far_second)
        flip_b = jnp.where(self.core == 0, far_second, far_first)
        return self.side ^ (flip_a + 2 * flip_b)

    def order_of_side(self, q):
        flip = self.side ^ q
        return jnp.where(self.core == 0, flip % 2 * 2 + flip // 2, flip)


def sum_sides(ring, x, starts, count):
    bf16, f32 = jnp.bfloat16, jnp.float32

    def at(a, b):
        return rows_of(x, starts[ring.side_at(a, b)], count)

    sent = jnp.concatenate([at(1, 1), at(1, 0)], axis=0).astype(bf16)
    got = ring.swap(sent, ring.first).astype(f32)
    passed = (at(0, 1) + got[:count]).astype(bf16)
    return at(0, 0) + got[count:] + ring.swap(passed, ring.second).astype(f32)


def sum_layers(ring, x, starts, count):
    bf16, f32 = jnp.bfloat16, jnp.float32
    total = rows_of(x, starts[ring.layer], count)
    for d in range(1, ring.layers):
        sent = rows_of(x, starts[ring.layer ^ d], count).astype(bf16)
        total = total + ring.up(sent, d).astype(f32)
    return total


def spread_sides(ring, x):
    second = ring.swap(x, ring.second)
    first = ring.swap(x, ring.first)
    return [x, second, first, ring.swap(second, ring.first)]


def spread_layers(ring, x):
    return [x] + [ring.up(x, d) for d in range(1, ring.layers)]


def join(parts, index_of, own, starts):
    ordered = []
    for k, start in enumerate(starts):
        which = jnp.broadcast_to(index_of(k), parts[0].shape)
        piece = lax.select_n(which.astype(jnp.int32), *parts)
        skip = own * k - start
        ordered.append(piece[skip : skip + own])
    return jnp.concatenate(ordered, axis=0)


def by_rows(features, labels, weight, noise):
    bf16, f32 = jnp.bfloat16, jnp.float32
    ring = Ring()
    n, layers = ring.n, ring.layers
    depth, width = weight.shape
    half, own = depth // 2, depth // n
    by_side, by_layer = half // SIDES, half // layers
    narrow = narrow_share(width)
    wide = width - narrow
    classes = width * lax.axis_size("cls")
    batch = features.shape[0] * n
    scale = 0.1 * classes / batch

    to_wide, to_narrow = [], []
    for d in range(n):
        c, rest = d // (SIDES * layers), d % (SIDES * layers)
        q, k = rest // layers, rest % layers
        to_wide.append((d, (k * SIDES + q) * 2 + c))
        k, q = rest // SIDES, rest % SIDES
        to_narrow.append((d, (k * SIDES + q) * 2 + c))
    noise_narrow = ring.swap(noise[:, wide:], to_narrow)
    noise_wide = ring.swap(noise[:, :wide], to_wide)

    def updated(grad, noise_own, base, start, inner, columns):
        count = grad.shape[0]
        noise_rows = lax.dynamic_update_slice_in_dim(
            jnp.zeros((count, grad.shape[1]), noise.dtype), noise_own, inner, 0
        )
        rows = lax.dynamic_slice(
            weight, (base + start, jnp.int32(columns)), (count, grad.shape[1])
        )
        return (
            rows.astype(f32) - scale * (grad + 0.96 * CLIP * noise_rows.astype(f32))
        ).astype(bf16)

    def core_sum(part):
        sent = rows_of(part, half * (1 - ring.core), half).astype(bf16)
        got = ring.swap(sent, ring.cores)
        return rows_of(part, half * ring.core, half) + got.astype(f32)

    coef = lax.optimization_barrier(coefficients(features, labels, weight))

    def gradient(columns):
        return lax.dot_general(
            features, columns, (((0,), (0,)), ((), ())), preferred_element_type=f32
        )

    side_rows = jnp.arange(SIDES, dtype=jnp.int32) * by_side
    layer_rows = jnp.arange(layers, dtype=jnp.int32) * by_layer
    wide_starts, wide_count = cut(by_side, layers)
    narrow_starts, narrow_count = cut(by_layer, SIDES)
    wide_table = jnp.asarray(wide_starts, jnp.int32)
    narrow_table = jnp.asarray(narrow_starts, jnp.int32)

    half_narrow = core_sum(gradient(coef[:, wide:]))
    half_wide = core_sum(gradient(coef[:, :wide]))
    layer_sum = sum_layers(ring, half_narrow, layer_rows, by_layer)
    side_sum = sum_sides(ring, half_wide, side_rows, by_side)
    grad_narrow = sum_sides(ring, layer_sum, narrow_table, narrow_count)
    grad_wide = sum_layers(ring, side_sum, wide_table, wide_count)

    start = narrow_table[ring.side]
    new_narrow = updated(
        grad_narrow,
        noise_narrow,
        half * ring.core + by_layer * ring.layer,
        start,
        own * ring.side - start,
        wide,
    )
    start = wide_table[ring.layer]
    new_wide = updated(
        grad_wide,
        noise_wide,
        half * ring.core + by_side * ring.side,
        start,
        own * ring.layer - start,
        0,
    )

    parts = spread_sides(ring, new_narrow)
    layer_block = join(parts, ring.order_of_side, own, narrow_starts)
    parts = spread_layers(ring, new_wide)
    side_block = join(parts, lambda k: ring.layer ^ k, own, wide_starts)
    narrow_blocks = spread_layers(ring, layer_block)
    wide_blocks = spread_sides(ring, side_block)

    narrow_rows = [by_layer * (ring.layer ^ d) for d in range(layers)]
    flips = [(0, 0), (0, 1), (1, 0), (1, 1)]
    wide_rows = [by_side * ring.side_at(a, b) for a, b in flips]
    other_rows = [by_side * ring.side_at(b, a) for a, b in flips]
    mine, theirs = half * ring.core, half * (1 - ring.core)
    blocks = narrow_blocks + wide_blocks
    far = [ring.swap(b, ring.cores) for b in blocks]
    columns = [wide] * layers + [0] * SIDES
    rows = [mine + r for r in narrow_rows + wide_rows]
    rows += [theirs + r for r in narrow_rows + other_rows]
    return place(blocks + far, rows, columns * 2, weight.shape)


def by_columns(features, labels, weight, noise):
    coef = coefficients(features, labels, weight)
    partial_grad = lax.dot_general(
        features, coef, (((0,), (0,)), ((), ())), preferred_element_type=jnp.float32
    )
    classes = weight.shape[1] * lax.axis_size("cls")
    batch = features.shape[0] * lax.axis_size("ex")
    scale = 0.1 * classes / batch
    grad_part = lax.psum_scatter(partial_grad, "ex", scatter_dimension=0, tiled=True)
    span = grad_part.shape[0]
    own_weight = lax.dynamic_slice_in_dim(weight, lax.axis_index("ex") * span, span, 0)
    updated = own_weight.astype(jnp.float32) - scale * (
        grad_part + 0.96 * CLIP * noise.astype(jnp.float32)
    )
    return lax.all_gather(updated.astype(jnp.bfloat16), "ex", axis=0, tiled=True)


def local(features, labels, weight, noise):
    n = lax.axis_size("ex")
    depth, width = weight.shape
    layers = n // (2 * SIDES)
    fits = n % (2 * SIDES) == 0 and layers > 1 and layers & (layers - 1) == 0
    fits = fits and depth % n == 0 and width % LANE == 0 and width > LANE
    fits = fits and depth % (2 * ROW * SIDES) == 0 and depth % (2 * ROW * layers) == 0
    step = by_rows if fits else by_columns
    return step(features, labels, weight, noise)


def solution(mesh):
    in_specs = (P("ex", None), P("ex"), P(None, "cls"), P("ex", "cls"))
    out_specs = P(None, "cls")
    return jax.shard_map(local, mesh=mesh, in_specs=in_specs, out_specs=out_specs, check_vma=False)
```

time: 268 us -> 167 us (0.62)
  blocking collectives: 114 us -> 0 us
  waiting for transfers between devices: 73.4 us -> 33.3 us
  starting transfers between devices: 18.7 us -> 38.1 us
  other arithmetic: 5.96 us -> 22.4 us
  Pallas kernels: 0 us -> 14.7 us
  between operations: 13.6 us -> 17.7 us
    unnamed x1 -> x0, blocking collectives: 114 us -> none
    all_gather x1 -> x0, waiting for transfers between devices: 70.1 us -> none  [local(): lax.all_gather(updated.astype(jnp.bfloat16), 'ex', axis=1, tiled=True)]
    ppermute x0 -> x34, starting transfers between devices: none -> 38.1 us  [swap(): return lax.ppermute(x, 'ex', pairs)]
    ppermute x0 -> x34, waiting for transfers between devices: none -> 33.3 us  [swap(): return lax.ppermute(x, 'ex', pairs)]
    pallas_call x0 -> x1, Pallas kernels: none -> 14.7 us  [place(): pl.pallas_call(kernel, in_specs=[pl.BlockSpec(memory_space=pltpu.SMEM)] +...]
    unnamed x3 -> x0, starting transfers between devices: 11.3 us -> none
    convert_element_type x0 -> x7, other arithmetic: none -> 8.28 us  [the longest x1 3.35 us: coefficients(): return (factor[:, None] * resid).astype(jnp.bfloat16)]
    all_to_all x1 -> x0, starting transfers between devices: 7.33 us -> none  [local(): lax.all_to_all(noise, 'ex', split_axis=1, concat_axis=0, tiled=True)]
  transfers between devices with their start and end apart: 5 -> 34, of which waited for: 2 -> 7; matrix products, arithmetic and copies ran while one was open for 53% -> 12% of each run, Pallas kernels for 0% -> 0%
where the time goes in v2:
time: 167 us; the launch traced here: 166 us
  starting transfers between devices  38.1 us (23%)
  waiting for transfers between devices  33.3 us (20%)
  other arithmetic  22.4 us (13%)
  local copies, waits for them, and re-layouts  20.1 us (12%)
  matrix products  19.3 us (12%)
  between operations  17.7 us (11%)
  Pallas kernels  14.7 us (9%)
    ppermute x34, starting transfers between devices, swap(): return lax.ppermute(x, 'ex', pairs)  38.1 us
    ppermute x34, waiting for transfers between devices, swap(): return lax.ppermute(x, 'ex', pairs)  33.3 us
    pallas_call x1, Pallas kernels, place(): pl.pallas_call(kernel, in_specs=[pl.BlockSpec(memory_space=pltpu.SMEM)] +...  14.7 us
    unnamed x36, local copies, waits for them, and re-layouts  11.5 us
    dot_general x2, matrix products, gradient(): lax.dot_general(features, columns, (((0,), (0,)), ((), ())), preferred_el...  11 us
    dot_general x1, matrix products, coefficients(): logits = jnp.dot(features, weight, preferred_element_type=jnp.float32)  8.31 us
    convert_element_type x2, local copies, waits for them, and re-layouts, core_sum(): sent = rows_of(part, half * (1 - ring.core), half).astype(bf16)  4.22 us
    add x2, other arithmetic, core_sum(): return rows_of(part, half * ring.core, half) + got.astype(f32)  4.14 us
  transfers between devices with their start and end apart: 34, of which 7 were waited for; matrix products, arithmetic and copies ran while one was open for 12% of the time, Pallas kernels for 0%

profile of v2, /device:TPU:0, one launch (start us, length us, event | category | flops | bytes accessed | tf_op | source)
XLA Modules:
  0.0 165.7 jit_solution(5655760703440663722)
XLA Ops:
  0.0 2.8 %multiply_reduce_fusion = f32[1024]{0:T(1024)S(1)} fusion(bf16[1024,1664]{1,0:T(8,128)(2,1)} %param.6), kind=kLoop, calls=%fused_computation | loop fusion | flops 5110784 | bytes 3411968 | tf_op jit(solution)/shard_map/reduce_sum | solution.py:31
  3.0 8.3 %fusion.16 = (f32[1024]{0:T(1024)S(1)}, f32[1024,1408]{1,0:T(8,128)S(1)}) fusion(bf16[1024,1664]{1,0:T(8,128)(2,1)S(1)} %copy-done.10, bf16[1664,1408]{1,0:T(8,128)(2,1)} %param.8), kind=kOutput, calls=%fused_computation.55 | convolution fusion | flops 4799724544 | bytes 13864960 | tf_op jit(solution)/shard_map/dot_general | solution.py:15
  11.3 2.4 %multiply_reduce_fusion.1 = (f32[1024]{0:T(1024)S(1)}, f32[1024]{0:T(1024)S(1)}, f32[1024]{0:T(1024)S(1)}) fusion(f32[1024,1408]{1,0:T(8,128)S(1)} %get-tuple-element.35, f32[1024]{0:T(1024)S(1)} %get-tuple-element.34, s32[1024]{0:T(1024)S(1)} %copy-done.17), kind=kLoop, calls=%fused_computation.4 | loop fusion | flops 10089472 | bytes 5787648 | tf_op jit(solution)/shard_map/reduce_sum | solution.py:24
  13.8 3.3 %multiply_convert_fusion = bf16[1024,1408]{1,0:T(8,128)(2,1)} fusion(f32[1024,1408]{1,0:T(8,128)S(1)} %get-tuple-element.35, f32[1024]{0:T(1024)S(1)} %get-tuple-element.6, f32[1024]{0:T(1024)S(1)} %maximum_divide_fusion, s32[1024]{0:T(1024)S(1)} %copy-done.17, f32[1024]{0:T(1024)S(1)} %get-tuple-element.34), kind=kLoop, calls=%fused_computation.1 | loop fusion | flops 10092544 | bytes 8667136 | tf_op jit(solution)/shard_map/convert_element_type | solution.py:34
  17.1 7.8 %fusion.1 = f32[896,1664]{0,1:T(8,128)} fusion(bf16[1024,1664]{1,0:T(8,128)(2,1)S(1)} %copy-done.10, bf16[1024,1408]{1,0:T(8,128)(2,1)} %multiply_convert_fusion), kind=kOutput, calls=%fused_computation.9 | convolution fusion | flops 3053453312 | bytes 11206656 | tf_op jit(solution)/shard_map/dot_general | solution.py:196
  24.9 3.2 %fusion.3 = bf16[832,896]{1,0:T(8,128)(2,1)} fusion(f32[896,1664]{0,1:T(8,128)} %fusion.1, s32[]{:T(128)S(6)} %select_n.384), kind=kLoop, calls=%fused_computation.13 | loop fusion | bytes 2981892 | tf_op jit(solution)/shard_map/convert_element_type | solution.py:189
  28.6 3.2 %fusion.4 = f32[512,1664]{0,1:T(8,128)S(1)} fusion(bf16[1024,1664]{1,0:T(8,128)(2,1)S(1)} %copy-done.10, bf16[1024,1408]{1,0:T(8,128)(2,1)} %multiply_convert_fusion), kind=kOutput, calls=%fused_computation.14 | convolution fusion | flops 1744830464 | bytes 7864320 | tf_op jit(solution)/shard_map/dot_general | solution.py:196
  31.9 1.7 %copy-done.12 = f32[512,1664]{0,1:T(8,128)} copy-done((f32[512,1664]{0,1:T(8,128)}, f32[512,1664]{0,1:T(8,128)S(1)}, u32[]{:S(2)}) %copy-start.12) | copy-done | bytes 3407896
  33.6 1.0 fusion.6
  34.6 2.7 %bitcast_add_fusion = f32[832,896]{1,0:T(8,128)S(1)} fusion(bf16[832,896]{1,0:T(8,128)(2,1)} %collective-permute-done.13, f32[896,1664]{0,1:T(8,128)} %fusion.1, s32[]{:T(128)S(6)} %select_n.383), kind=kLoop, calls=%fused_computation.7 | loop fusion | flops 1490944 | bytes 7454724 | tf_op jit(solution)/shard_map/add | solution.py:191
  37.4 0.9 pad_maximum_fusion
  38.4 3.0 %collective-permute-start.14 = (bf16[416,896]{1,0:T(8,128)(2,1)}, bf16[416,896]{1,0:T(8,128)(2,1)}, u32[]{:S(2)}, u32[]{:S(2)}) collective-permute-start(bf16[416,896]{1,0:T(8,128)(2,1)} %pad_maximum_fusion), channel_id=1, source_target_pairs={{0,2},{1,5},{2,0},{3,7},{4,6},{5,1},{6,4},{7,3},{8,10},{9,13},{10,... | collective-permute-start | bytes 2236424 | tf_op jit(solution)/shard_map/ppermute | solution.py:97
  41.3 1.5 bitcast_add_fusion.1
  42.8 1.2 copy-done.9
  44.0 0.9 dynamic-slice_convert_fusion.6
  44.9 3.6 %collective-permute-start.3 = (bf16[208,512]{1,0:T(8,128)(2,1)}, bf16[208,512]{1,0:T(8,128)(2,1)S(1)}, u32[]{:S(2)}, u32[]{:S(2)}) collective-permute-start(bf16[208,512]{1,0:T(8,128)(2,1)} %get-tuple-element.11), channel_id=1, source_target_pairs={{0,24},{1,25},{2,26},{3,27},{4,28},{5,29},{6,30},{7,31},{8,16},{9,... | collective-permute-start | bytes 638984 | tf_op jit(solution)/shard_map/ppermute | solution.py:97
  48.5 0.8 collective-permute-start.1
  49.3 0.7 fusion.15
  53.3 1.8 %collective-permute-done.3 = bf16[208,512]{1,0:T(8,128)(2,1)S(1)} collective-permute-done((bf16[208,512]{1,0:T(8,128)(2,1)}, bf16[208,512]{1,0:T(8,128)(2,1)S(1)}, u32[]{:S(2)}, u32[]{:S(2)}) %collective-permute-start.3) | collective-permute-done | bytes 213024 | tf_op jit(solution)/shard_map/ppermute | solution.py:97
  55.1 11.7 %collective-permute-done.2 = bf16[208,512]{1,0:T(8,128)(2,1)} collective-permute-done((bf16[208,512]{1,0:T(8,128)(2,1)}, bf16[208,512]{1,0:T(8,128)(2,1)}, u32[]{:S(2)}, u32[]{:S(2)}) %collective-permute-start.2) | collective-permute-done | bytes 213024 | tf_op jit(solution)/shard_map/ppermute | solution.py:97
  66.8 1.4 convert_add_fusion
  68.3 1.2 convert_element_type.123
  69.6 1.1 copy-done.8
  70.7 0.8 fusion.7
  71.5 0.5 collective-permute-start.15
  72.0 0.6 pad_maximum_fusion.3
  72.6 1.5 collective-permute-start.4
  74.2 0.7 collective-permute-start.6
  74.8 0.6 slice.59
  75.5 2.1 %collective-permute-start.19 = (bf16[52,896]{1,0:T(8,128)(2,1)}, bf16[52,896]{1,0:T(8,128)(2,1)}, u32[]{:S(2)}, u32[]{:S(2)}) collective-permute-start(bf16[52,896]{1,0:T(8,128)(2,1)} %slice.59), channel_id=1, source_target_pairs={{0,0},{1,8},{2,16},{3,24},{4,2},{5,10},{6,18},{7,26},{8,4},{9,12},... | collective-permute-start | bytes 279560 | tf_op jit(solution)/shard_map/ppermute | solution.py:97
  88.7 0.9 convert_element_type.114
  89.6 5.5 %collective-permute-start.5 = (bf16[56,512]{1,0:T(8,128)(2,1)S(1)}, bf16[56,512]{1,0:T(8,128)(2,1)S(1)}, u32[]{:S(2)}, u32[]{:S(2)}) collective-permute-start(bf16[56,512]{1,0:T(8,128)(2,1)S(1)} %fusion.9), channel_id=1, source_target_pairs={{0,4},{1,3},{2,6},{3,1},{4,0},{5,7},{6,2},{7,5},{8,12},{9,11},{10,... | collective-permute-start | bytes 172040 | tf_op jit(solution)/shard_map/ppermute | solution.py:97
  95.1 1.3 fusion.8
  96.5 0.9 copy-done.11
  97.6 1.3 collective-permute-start.17
  99.0 2.9 %collective-permute-start.16 = (bf16[56,896]{1,0:T(8,128)(2,1)S(1)}, bf16[56,896]{1,0:T(8,128)(2,1)S(1)}, u32[]{:S(2)}, u32[]{:S(2)}) collective-permute-start(bf16[56,896]{1,0:T(8,128)(2,1)S(1)} %get-tuple-element.13), channel_id=1, source_target_pairs={{0,8},{1,9},{2,10},{3,11},{4,12},{5,13},{6,14},{7,15},{8,0},{9,1},... | collective-permute-start | bytes 301064 | tf_op jit(solution)/shard_map/ppermute | solution.py:97
  101.8 0.9 fusion.14
  106.1 1.5 dynamic_update_slice.7
  107.6 1.3 collective-permute-start.8
  108.9 0.7 collective-permute-start.9
  109.7 1.1 subtract_convert_fusion
  110.8 1.5 collective-permute-start.22
  112.3 2.9 %collective-permute-start.20 = (bf16[56,896]{1,0:T(8,128)(2,1)S(1)}, bf16[56,896]{1,0:T(8,128)(2,1)S(1)}, u32[]{:S(2)}, u32[]{:S(2)}) collective-permute-start(bf16[56,896]{1,0:T(8,128)(2,1)S(1)} %subtract_convert_fusion), channel_id=1, source_target_pairs={{0,8},{1,9},{2,10},{3,11},{4,12},{5,13},{6,14},{7,15},{8,0},{9,1},... | collective-permute-start | bytes 301064 | tf_op jit(solution)/shard_map/ppermute | solution.py:97
  115.3 3.0 %collective-permute-done.22 = bf16[56,896]{1,0:T(8,128)(2,1)S(1)} collective-permute-done((bf16[56,896]{1,0:T(8,128)(2,1)S(1)}, bf16[56,896]{1,0:T(8,128)(2,1)S(1)}, u32[]{:S(2)}, u32[]{:S(2)}) %collective-permute-start.22) | collective-permute-done | bytes 100384 | tf_op jit(solution)/shard_map/ppermute | solution.py:97
  118.4 3.0 %collective-permute-done.21 = bf16[56,896]{1,0:T(8,128)(2,1)S(1)} collective-permute-done((bf16[56,896]{1,0:T(8,128)(2,1)S(1)}, bf16[56,896]{1,0:T(8,128)(2,1)S(1)}, u32[]{:S(2)}, u32[]{:S(2)}) %collective-permute-start.21) | collective-permute-done | bytes 100384 | tf_op jit(solution)/shard_map/ppermute | solution.py:97
  121.6 1.3 collective-permute-start.23
  123.1 2.8 %collective-permute-start.11 = (bf16[208,512]{1,0:T(8,128)(2,1)S(1)}, bf16[208,512]{1,0:T(8,128)(2,1)S(1)}, u32[]{:S(2)}, u32[]{:S(2)}) collective-permute-start(bf16[208,512]{1,0:T(8,128)(2,1)S(1)} %pad_maximum_fusion.2.refs_0_), channel_id=1, source_target_pairs={{0,16},{1,17},{2,18},{3,19},{4,20},{5,21},{6,22},{7,23},{8,24},{9,... | collective-permute-start | bytes 638984 | tf_op jit(solution)/shard_map/ppermute | solution.py:97
  126.4 5.4 %collective-permute-done.23.refs_5_ = bf16[208,896]{1,0:T(8,128)(2,1)S(1)} collective-permute-done((bf16[208,896]{1,0:T(8,128)(2,1)S(1)}, bf16[208,896]{1,0:T(8,128)(2,1)S(1)}, u32[]{:S(2)}, u32[]{:S(2)}) %collective-permute-start.23) | collective-permute-done | bytes 372768 | tf_op jit(solution)/shard_map/ppermute | solution.py:97
  131.8 1.1 collective-permute-start.25
  132.9 1.4 collective-permute-start.12
  134.3 6.6 %collective-permute-done.11.refs_2_ = bf16[208,512]{1,0:T(8,128)(2,1)S(1)} collective-permute-done((bf16[208,512]{1,0:T(8,128)(2,1)S(1)}, bf16[208,512]{1,0:T(8,128)(2,1)S(1)}, u32[]{:S(2)}, u32[]{:S(2)}) %collective-permute-start.11) | collective-permute-done | bytes 213024 | tf_op jit(solution)/shard_map/ppermute | solution.py:97
  140.9 0.5 collective-permute-start.28
  141.5 0.7 copy-done
  142.1 0.7 copy-done.2
  142.8 0.7 copy-done.4
  143.5 0.5 collective-permute-start.31
  144.0 0.5 collective-permute-start.33
  144.6 0.7 copy-done.6
  145.4 1.6 collective-permute-done.29.refs_11_
  147.1 0.9 copy-done.1
  148.0 0.9 copy-done.3
  148.9 0.9 copy-done.5
  149.9 0.9 copy-done.7
  150.8 14.7 %shard_map.64 = bf16[1664,1408]{1,0:T(8,128)(2,1)} custom-call(s32[16]{0:T(128)S(1)} %stack.67.rows_ref, bf16[208,512]{1,0:T(8,128)(2,1)S(1)} %pad_maximum_fusion.2.refs_0_, bf16[208,512]{1,0:T(8,128)(2,1)S(1)} %collective-permute-done.10.refs_1_, bf16[208,512]{1,0:T(8,128)(2,1)S(1)} %copy-done.1, bf16[208,512]{1,0:T(8,128)(2,1)} %collective-permute-done.12.refs_3_, ...), custom_call_target="tpu_custom_call" | custom-call | tf_op jit(solution)/shard_map/pallas_call | solution.py:57
  (80 shorter events, 2.9 us)
Async XLA Ops:
  0.0 3.0 %copy-start.10 = (bf16[1024,1664]{1,0:T(8,128)(2,1)S(1)}, bf16[1024,1664]{1,0:T(8,128)(2,1)}, u32[]{:S(2)}) copy-start(bf16[1024,1664]{1,0:T(8,128)(2,1)} %param.6) | copy-start | bytes 10223620
  3.0 8.3 %copy-start.17 = (s32[1024]{0:T(1024)S(1)}, s32[1024]{0:T(1024)}, u32[]{:S(2)}) copy-start(s32[1024]{0:T(1024)} %param.7) | copy-start | bytes 12292
  28.1 6.5 %collective-permute-start.13 = (bf16[832,896]{1,0:T(8,128)(2,1)}, bf16[832,896]{1,0:T(8,128)(2,1)}, u32[]{:S(2)}, u32[]{:S(2)}) collective-permute-start(bf16[832,896]{1,0:T(8,128)(2,1)} %fusion.3), channel_id=1, source_target_pairs={{0,1},{1,0},{2,3},{3,2},{4,5},{5,4},{6,7},{7,6},{8,9},{9,8},{10,11... | collective-permute-start | bytes 4472840 | tf_op jit(solution)/shard_map/ppermute | solution.py:97
  31.8 1.8 %copy-start.12 = (f32[512,1664]{0,1:T(8,128)}, f32[512,1664]{0,1:T(8,128)S(1)}, u32[]{:S(2)}) copy-start(f32[512,1664]{0,1:T(8,128)S(1)} %fusion.4) | copy-start | bytes 10223620
  34.6 6.7 %collective-permute-start = (bf16[832,512]{1,0:T(8,128)(2,1)}, bf16[832,512]{1,0:T(8,128)(2,1)}, u32[]{:S(2)}, u32[]{:S(2)}) collective-permute-start(bf16[832,512]{1,0:T(8,128)(2,1)} %fusion.6), channel_id=1, source_target_pairs={{0,1},{1,0},{2,3},{3,2},{4,5},{5,4},{6,7},{7,6},{8,9},{9,8},{10,11... | collective-permute-start | bytes 2555912 | tf_op jit(solution)/shard_map/ppermute | solution.py:97
  34.6 6.7 %copy-start.13 = (f32[512,1664]{0,1:T(8,128)S(1)}, f32[512,1664]{0,1:T(8,128)}, u32[]{:S(2)}) copy-start(f32[512,1664]{0,1:T(8,128)} %copy-done.12) | copy-start | bytes 10223620
  37.4 11.8 %copy-start.16 = (s32[4]{0:T(128)S(1)}, s32[4]{0:T(128)}, u32[]{:S(2)}) copy-start(s32[4]{0:T(128)} %constant.157.clone) | copy-start | bytes 52
  38.4 29.9 %collective-permute-start.14 = (bf16[416,896]{1,0:T(8,128)(2,1)}, bf16[416,896]{1,0:T(8,128)(2,1)}, u32[]{:S(2)}, u32[]{:S(2)}) collective-permute-start(bf16[416,896]{1,0:T(8,128)(2,1)} %pad_maximum_fusion), channel_id=1, source_target_pairs={{0,2},{1,5},{2,0},{3,7},{4,6},{5,1},{6,4},{7,3},{8,10},{9,13},{10,... | collective-permute-start | bytes 2236424 | tf_op jit(solution)/shard_map/ppermute | solution.py:97
  42.8 1.2 copy-start.9
  44.9 10.2 %collective-permute-start.3 = (bf16[208,512]{1,0:T(8,128)(2,1)}, bf16[208,512]{1,0:T(8,128)(2,1)S(1)}, u32[]{:S(2)}, u32[]{:S(2)}) collective-permute-start(bf16[208,512]{1,0:T(8,128)(2,1)} %get-tuple-element.11), channel_id=1, source_target_pairs={{0,24},{1,25},{2,26},{3,27},{4,28},{5,29},{6,30},{7,31},{8,16},{9,... | collective-permute-start | bytes 638984 | tf_op jit(solution)/shard_map/ppermute | solution.py:97
  48.5 18.4 %collective-permute-start.2 = (bf16[208,512]{1,0:T(8,128)(2,1)}, bf16[208,512]{1,0:T(8,128)(2,1)}, u32[]{:S(2)}, u32[]{:S(2)}) collective-permute-start(bf16[208,512]{1,0:T(8,128)(2,1)} %get-tuple-element.12), channel_id=1, source_target_pairs={{0,16},{1,17},{2,18},{3,19},{4,20},{5,21},{6,22},{7,23},{8,24},{9,... | collective-permute-start | bytes 638984 | tf_op jit(solution)/shard_map/ppermute | solution.py:97
  48.5 18.4 %collective-permute-start.1 = (bf16[208,512]{1,0:T(8,128)(2,1)S(1)}, bf16[208,512]{1,0:T(8,128)(2,1)}, u32[]{:S(2)}, u32[]{:S(2)}) collective-permute-start(bf16[208,512]{1,0:T(8,128)(2,1)S(1)} %get-tuple-element.10), channel_id=1, source_target_pairs={{0,8},{1,9},{2,10},{3,11},{4,12},{5,13},{6,14},{7,15},{8,0},{9,1},... | collective-permute-start | bytes 638984 | tf_op jit(solution)/shard_map/ppermute | solution.py:97
  53.3 20.8 %copy-start.15 = (bf16[52,1408]{1,0:T(8,128)(2,1)S(1)}, bf16[52,1408]{1,0:T(8,128)(2,1)}, u32[]{:S(2)}) copy-start(bf16[52,1408]{1,0:T(8,128)(2,1)} %param.9) | copy-start | bytes 439300
  55.1 11.7 %copy-start.14 = (bf16[208,512]{1,0:T(8,128)(2,1)}, bf16[208,512]{1,0:T(8,128)(2,1)S(1)}, u32[]{:S(2)}) copy-start(bf16[208,512]{1,0:T(8,128)(2,1)S(1)} %collective-permute-done.3) | copy-start | bytes 638980
  69.5 1.1 copy-start.8
  71.5 23.7 %collective-permute-start.15 = (bf16[208,896]{1,0:T(8,128)(2,1)}, bf16[208,896]{1,0:T(8,128)(2,1)}, u32[]{:S(2)}, u32[]{:S(2)}) collective-permute-start(bf16[208,896]{1,0:T(8,128)(2,1)} %fusion.7), channel_id=1, source_target_pairs={{0,4},{1,3},{2,6},{3,1},{4,0},{5,7},{6,2},{7,5},{8,12},{9,11},{10,... | collective-permute-start | bytes 1118216 | tf_op jit(solution)/shard_map/ppermute | solution.py:97
  72.6 16.0 %collective-permute-start.4 = (bf16[112,512]{1,0:T(8,128)(2,1)}, bf16[112,512]{1,0:T(8,128)(2,1)}, u32[]{:S(2)}, u32[]{:S(2)}) collective-permute-start(bf16[112,512]{1,0:T(8,128)(2,1)} %pad_maximum_fusion.3), channel_id=1, source_target_pairs={{0,2},{1,5},{2,0},{3,7},{4,6},{5,1},{6,4},{7,3},{8,10},{9,13},{10,... | collective-permute-start | bytes 344072 | tf_op jit(solution)/shard_map/ppermute | solution.py:97
  74.2 14.0 %collective-permute-start.6 = (bf16[52,512]{1,0:T(8,128)(2,1)S(1)}, bf16[52,512]{1,0:T(8,128)(2,1)S(1)}, u32[]{:S(2)}, u32[]{:S(2)}) collective-permute-start(bf16[52,512]{1,0:T(8,128)(2,1)S(1)} %slice.51), channel_id=1, source_target_pairs={{0,0},{1,2},{2,4},{3,6},{4,8},{5,10},{6,12},{7,14},{8,16},{9,18},{... | collective-permute-start | bytes 159752 | tf_op jit(solution)/shard_map/ppermute | solution.py:97
  75.5 30.6 %collective-permute-start.19 = (bf16[52,896]{1,0:T(8,128)(2,1)}, bf16[52,896]{1,0:T(8,128)(2,1)}, u32[]{:S(2)}, u32[]{:S(2)}) collective-permute-start(bf16[52,896]{1,0:T(8,128)(2,1)} %slice.59), channel_id=1, source_target_pairs={{0,0},{1,8},{2,16},{3,24},{4,2},{5,10},{6,18},{7,26},{8,4},{9,12},... | collective-permute-start | bytes 279560 | tf_op jit(solution)/shard_map/ppermute | solution.py:97
  89.6 12.2 %collective-permute-start.5 = (bf16[56,512]{1,0:T(8,128)(2,1)S(1)}, bf16[56,512]{1,0:T(8,128)(2,1)S(1)}, u32[]{:S(2)}, u32[]{:S(2)}) collective-permute-start(bf16[56,512]{1,0:T(8,128)(2,1)S(1)} %fusion.9), channel_id=1, source_target_pairs={{0,4},{1,3},{2,6},{3,1},{4,0},{5,7},{6,2},{7,5},{8,12},{9,11},{10,... | collective-permute-start | bytes 172040 | tf_op jit(solution)/shard_map/ppermute | solution.py:97
  96.4 0.9 copy-start.11
  97.4 12.3 %collective-permute-start.18 = (bf16[56,896]{1,0:T(8,128)(2,1)S(1)}, bf16[56,896]{1,0:T(8,128)(2,1)S(1)}, u32[]{:S(2)}, u32[]{:S(2)}) collective-permute-start(bf16[56,896]{1,0:T(8,128)(2,1)S(1)} %get-tuple-element.14), channel_id=1, source_target_pairs={{0,24},{1,25},{2,26},{3,27},{4,28},{5,29},{6,30},{7,31},{8,16},{9,... | collective-permute-start | bytes 301064 | tf_op jit(solution)/shard_map/ppermute | solution.py:97
  97.6 12.1 %collective-permute-start.17 = (bf16[56,896]{1,0:T(8,128)(2,1)S(1)}, bf16[56,896]{1,0:T(8,128)(2,1)S(1)}, u32[]{:S(2)}, u32[]{:S(2)}) collective-permute-start(bf16[56,896]{1,0:T(8,128)(2,1)S(1)} %get-tuple-element.15), channel_id=1, source_target_pairs={{0,16},{1,17},{2,18},{3,19},{4,20},{5,21},{6,22},{7,23},{8,24},{9,... | collective-permute-start | bytes 301064 | tf_op jit(solution)/shard_map/ppermute | solution.py:97
  99.0 10.7 %collective-permute-start.16 = (bf16[56,896]{1,0:T(8,128)(2,1)S(1)}, bf16[56,896]{1,0:T(8,128)(2,1)S(1)}, u32[]{:S(2)}, u32[]{:S(2)}) collective-permute-start(bf16[56,896]{1,0:T(8,128)(2,1)S(1)} %get-tuple-element.13), channel_id=1, source_target_pairs={{0,8},{1,9},{2,10},{3,11},{4,12},{5,13},{6,14},{7,15},{8,0},{9,1},... | collective-permute-start | bytes 301064 | tf_op jit(solution)/shard_map/ppermute | solution.py:97
  102.7 6.3 %collective-permute-start.7 = (bf16[56,512]{1,0:T(8,128)(2,1)S(1)}, bf16[56,512]{1,0:T(8,128)(2,1)S(1)}, u32[]{:S(2)}, u32[]{:S(2)}) collective-permute-start(bf16[56,512]{1,0:T(8,128)(2,1)S(1)} %fusion.14), channel_id=1, source_target_pairs={{0,4},{1,3},{2,6},{3,1},{4,0},{5,7},{6,2},{7,5},{8,12},{9,11},{10,... | collective-permute-start | bytes 172040 | tf_op jit(solution)/shard_map/ppermute | solution.py:97
  107.6 7.7 %collective-permute-start.8 = (bf16[56,512]{1,0:T(8,128)(2,1)S(1)}, bf16[56,512]{1,0:T(8,128)(2,1)S(1)}, u32[]{:S(2)}, u32[]{:S(2)}) collective-permute-start(bf16[56,512]{1,0:T(8,128)(2,1)S(1)} %fusion.14), channel_id=1, source_target_pairs={{0,2},{1,5},{2,0},{3,7},{4,6},{5,1},{6,4},{7,3},{8,10},{9,13},{10,... | collective-permute-start | bytes 172040 | tf_op jit(solution)/shard_map/ppermute | solution.py:97
  108.9 6.3 %collective-permute-start.9 = (bf16[56,512]{1,0:T(8,128)(2,1)S(1)}, bf16[56,512]{1,0:T(8,128)(2,1)S(1)}, u32[]{:S(2)}, u32[]{:S(2)}) collective-permute-start(bf16[56,512]{1,0:T(8,128)(2,1)S(1)} %collective-permute-done.7), channel_id=1, source_target_pairs={{0,2},{1,5},{2,0},{3,7},{4,6},{5,1},{6,4},{7,3},{8,10},{9,13},{10,... | collective-permute-start | bytes 172040 | tf_op jit(solution)/shard_map/ppermute | solution.py:97
  110.8 7.6 %collective-permute-start.22 = (bf16[56,896]{1,0:T(8,128)(2,1)S(1)}, bf16[56,896]{1,0:T(8,128)(2,1)S(1)}, u32[]{:S(2)}, u32[]{:S(2)}) collective-permute-start(bf16[56,896]{1,0:T(8,128)(2,1)S(1)} %subtract_convert_fusion), channel_id=1, source_target_pairs={{0,24},{1,25},{2,26},{3,27},{4,28},{5,29},{6,30},{7,31},{8,16},{9,... | collective-permute-start | bytes 301064 | tf_op jit(solution)/shard_map/ppermute | solution.py:97
  112.3 9.1 %collective-permute-start.21 = (bf16[56,896]{1,0:T(8,128)(2,1)S(1)}, bf16[56,896]{1,0:T(8,128)(2,1)S(1)}, u32[]{:S(2)}, u32[]{:S(2)}) collective-permute-start(bf16[56,896]{1,0:T(8,128)(2,1)S(1)} %subtract_convert_fusion), channel_id=1, source_target_pairs={{0,16},{1,17},{2,18},{3,19},{4,20},{5,21},{6,22},{7,23},{8,24},{9,... | collective-permute-start | bytes 301064 | tf_op jit(solution)/shard_map/ppermute | solution.py:97
  112.3 9.1 %collective-permute-start.20 = (bf16[56,896]{1,0:T(8,128)(2,1)S(1)}, bf16[56,896]{1,0:T(8,128)(2,1)S(1)}, u32[]{:S(2)}, u32[]{:S(2)}) collective-permute-start(bf16[56,896]{1,0:T(8,128)(2,1)S(1)} %subtract_convert_fusion), channel_id=1, source_target_pairs={{0,8},{1,9},{2,10},{3,11},{4,12},{5,13},{6,14},{7,15},{8,0},{9,1},... | collective-permute-start | bytes 301064 | tf_op jit(solution)/shard_map/ppermute | solution.py:97
  121.6 10.2 %collective-permute-start.23 = (bf16[208,896]{1,0:T(8,128)(2,1)S(1)}, bf16[208,896]{1,0:T(8,128)(2,1)S(1)}, u32[]{:S(2)}, u32[]{:S(2)}) collective-permute-start(bf16[208,896]{1,0:T(8,128)(2,1)S(1)} %pad_maximum_fusion.1.refs_4_), channel_id=1, source_target_pairs={{0,4},{1,3},{2,6},{3,1},{4,0},{5,7},{6,2},{7,5},{8,12},{9,11},{10,... | collective-permute-start | bytes 1118216 | tf_op jit(solution)/shard_map/ppermute | solution.py:97
  123.0 11.3 %collective-permute-start.10 = (bf16[208,512]{1,0:T(8,128)(2,1)S(1)}, bf16[208,512]{1,0:T(8,128)(2,1)S(1)}, u32[]{:S(2)}, u32[]{:S(2)}) collective-permute-start(bf16[208,512]{1,0:T(8,128)(2,1)S(1)} %pad_maximum_fusion.2.refs_0_), channel_id=1, source_target_pairs={{0,8},{1,9},{2,10},{3,11},{4,12},{5,13},{6,14},{7,15},{8,0},{9,1},... | collective-permute-start | bytes 638984 | tf_op jit(solution)/shard_map/ppermute | solution.py:97
  123.1 17.9 %collective-permute-start.11 = (bf16[208,512]{1,0:T(8,128)(2,1)S(1)}, bf16[208,512]{1,0:T(8,128)(2,1)S(1)}, u32[]{:S(2)}, u32[]{:S(2)}) collective-permute-start(bf16[208,512]{1,0:T(8,128)(2,1)S(1)} %pad_maximum_fusion.2.refs_0_), channel_id=1, source_target_pairs={{0,16},{1,17},{2,18},{3,19},{4,20},{5,21},{6,22},{7,23},{8,24},{9,... | collective-permute-start | bytes 638984 | tf_op jit(solution)/shard_map/ppermute | solution.py:97
  125.9 18.1 %collective-permute-start.24 = (bf16[208,896]{1,0:T(8,128)(2,1)S(1)}, bf16[208,896]{1,0:T(8,128)(2,1)S(1)}, u32[]{:S(2)}, u32[]{:S(2)}) collective-permute-start(bf16[208,896]{1,0:T(8,128)(2,1)S(1)} %pad_maximum_fusion.1.refs_4_), channel_id=1, source_target_pairs={{0,2},{1,5},{2,0},{3,7},{4,6},{5,1},{6,4},{7,3},{8,10},{9,13},{10,... | collective-permute-start | bytes 1118216 | tf_op jit(solution)/shard_map/ppermute | solution.py:97
  131.8 12.2 %collective-permute-start.25 = (bf16[208,896]{1,0:T(8,128)(2,1)S(1)}, bf16[208,896]{1,0:T(8,128)(2,1)S(1)}, u32[]{:S(2)}, u32[]{:S(2)}) collective-permute-start(bf16[208,896]{1,0:T(8,128)(2,1)S(1)} %collective-permute-done.23.refs_5_), channel_id=1, source_target_pairs={{0,2},{1,5},{2,0},{3,7},{4,6},{5,1},{6,4},{7,3},{8,10},{9,13},{10,... | collective-permute-start | bytes 1118216 | tf_op jit(solution)/shard_map/ppermute | solution.py:97
  132.9 8.1 %collective-permute-start.12 = (bf16[208,512]{1,0:T(8,128)(2,1)S(1)}, bf16[208,512]{1,0:T(8,128)(2,1)}, u32[]{:S(2)}, u32[]{:S(2)}) collective-permute-start(bf16[208,512]{1,0:T(8,128)(2,1)S(1)} %pad_maximum_fusion.2.refs_0_), channel_id=1, source_target_pairs={{0,24},{1,25},{2,26},{3,27},{4,28},{5,29},{6,30},{7,31},{8,16},{9,... | collective-permute-start | bytes 638984 | tf_op jit(solution)/shard_map/ppermute | solution.py:97
  134.3 7.8 %collective-permute-start.26 = (bf16[208,512]{1,0:T(8,128)(2,1)S(1)}, bf16[208,512]{1,0:T(8,128)(2,1)S(1)}, u32[]{:S(2)}, u32[]{:S(2)}) collective-permute-start(bf16[208,512]{1,0:T(8,128)(2,1)S(1)} %pad_maximum_fusion.2.refs_0_), channel_id=1, source_target_pairs={{0,1},{1,0},{2,3},{3,2},{4,5},{5,4},{6,7},{7,6},{8,9},{9,8},{10,11... | collective-permute-start | bytes 638984 | tf_op jit(solution)/shard_map/ppermute | solution.py:97
  140.9 1.9 %collective-permute-start.27 = (bf16[208,512]{1,0:T(8,128)(2,1)S(1)}, bf16[208,512]{1,0:T(8,128)(2,1)S(1)}, u32[]{:S(2)}, u32[]{:S(2)}) collective-permute-start(bf16[208,512]{1,0:T(8,128)(2,1)S(1)} %collective-permute-done.10.refs_1_), channel_id=1, source_target_pairs={{0,1},{1,0},{2,3},{3,2},{4,5},{5,4},{6,7},{7,6},{8,9},{9,8},{10,11... | collective-permute-start | bytes 638984 | tf_op jit(solution)/shard_map/ppermute | solution.py:97
  140.9 3.6 %collective-permute-start.28 = (bf16[208,512]{1,0:T(8,128)(2,1)S(1)}, bf16[208,512]{1,0:T(8,128)(2,1)S(1)}, u32[]{:S(2)}, u32[]{:S(2)}) collective-permute-start(bf16[208,512]{1,0:T(8,128)(2,1)S(1)} %collective-permute-done.11.refs_2_), channel_id=1, source_target_pairs={{0,1},{1,0},{2,3},{3,2},{4,5},{5,4},{6,7},{7,6},{8,9},{9,8},{10,11... | collective-permute-start | bytes 638984 | tf_op jit(solution)/shard_map/ppermute | solution.py:97
  141.5 0.7 copy-start
  142.1 0.7 copy-start.2
  142.8 4.2 %collective-permute-start.30 = (bf16[208,896]{1,0:T(8,128)(2,1)S(1)}, bf16[208,896]{1,0:T(8,128)(2,1)S(1)}, u32[]{:S(2)}, u32[]{:S(2)}) collective-permute-start(bf16[208,896]{1,0:T(8,128)(2,1)S(1)} %pad_maximum_fusion.1.refs_4_), channel_id=1, source_target_pairs={{0,1},{1,0},{2,3},{3,2},{4,5},{5,4},{6,7},{7,6},{8,9},{9,8},{10,11... | collective-permute-start | bytes 1118216 | tf_op jit(solution)/shard_map/ppermute | solution.py:97
  142.8 0.7 copy-start.4
  143.5 3.5 %collective-permute-start.31 = (bf16[208,896]{1,0:T(8,128)(2,1)S(1)}, bf16[208,896]{1,0:T(8,128)(2,1)S(1)}, u32[]{:S(2)}, u32[]{:S(2)}) collective-permute-start(bf16[208,896]{1,0:T(8,128)(2,1)S(1)} %collective-permute-done.23.refs_5_), channel_id=1, source_target_pairs={{0,1},{1,0},{2,3},{3,2},{4,5},{5,4},{6,7},{7,6},{8,9},{9,8},{10,11... | collective-permute-start | bytes 1118216 | tf_op jit(solution)/shard_map/ppermute | solution.py:97
  144.0 3.0 %collective-permute-start.32 = (bf16[208,896]{1,0:T(8,128)(2,1)S(1)}, bf16[208,896]{1,0:T(8,128)(2,1)S(1)}, u32[]{:S(2)}, u32[]{:S(2)}) collective-permute-start(bf16[208,896]{1,0:T(8,128)(2,1)S(1)} %collective-permute-done.24.refs_6_), channel_id=1, source_target_pairs={{0,1},{1,0},{2,3},{3,2},{4,5},{5,4},{6,7},{7,6},{8,9},{9,8},{10,11... | collective-permute-start | bytes 1118216 | tf_op jit(solution)/shard_map/ppermute | solution.py:97
  144.0 3.0 %collective-permute-start.33 = (bf16[208,896]{1,0:T(8,128)(2,1)S(1)}, bf16[208,896]{1,0:T(8,128)(2,1)S(1)}, u32[]{:S(2)}, u32[]{:S(2)}) collective-permute-start(bf16[208,896]{1,0:T(8,128)(2,1)S(1)} %collective-permute-done.25.refs_7_), channel_id=1, source_target_pairs={{0,1},{1,0},{2,3},{3,2},{4,5},{5,4},{6,7},{7,6},{8,9},{9,8},{10,11... | collective-permute-start | bytes 1118216 | tf_op jit(solution)/shard_map/ppermute | solution.py:97
  144.6 0.7 copy-start.6
  145.2 1.8 %collective-permute-start.29 = (bf16[208,512]{1,0:T(8,128)(2,1)}, bf16[208,512]{1,0:T(8,128)(2,1)}, u32[]{:S(2)}, u32[]{:S(2)}) collective-permute-start(bf16[208,512]{1,0:T(8,128)(2,1)} %collective-permute-done.12.refs_3_), channel_id=1, source_target_pairs={{0,1},{1,0},{2,3},{3,2},{4,5},{5,4},{6,7},{7,6},{8,9},{9,8},{10,11... | collective-permute-start | bytes 638984 | tf_op jit(solution)/shard_map/ppermute | solution.py:97
  147.1 0.9 copy-start.1
  148.0 0.9 copy-start.3
  148.9 0.9 copy-start.5
  149.9 0.9 copy-start.7

commit v3 on v0

v3 whole, which is shorter than its diff:
```python
import functools

import jax
import jax.numpy as jnp
from jax import lax
from jax.experimental import pallas as pl
from jax.experimental.pallas import tpu as pltpu
from jax.sharding import PartitionSpec as P


CLIP = 48.0
SIDES = 4
ROW, LANE = 8, 128


def coefficients(features, labels, weight):
    cls_width = weight.shape[1]
    logits = jnp.dot(features, weight, preferred_element_type=jnp.float32)
    offset = lax.axis_index("cls") * cls_width
    local_lab = labels - offset
    columns = lax.broadcasted_iota(jnp.int32, (1, cls_width), 1)
    onehot = columns == local_lab[:, None]
    label_part = jnp.sum(jnp.where(onehot, logits, 0.0), axis=1)
    top = lax.pmax(jnp.max(logits, axis=1), "cls")
    expo = jnp.exp(logits - top[:, None])
    total, squares, label_logit = lax.psum(
        (jnp.sum(expo, axis=1), jnp.sum(expo * expo, axis=1), label_part), "cls"
    )
    probs = expo / total[:, None]
    label_prob = jnp.exp(label_logit - top) / total
    resid_sq = squares / (total * total) - 2.0 * label_prob + 1.0
    resid_norm = jnp.sqrt(jnp.maximum(resid_sq, 0.0))
    feat = features.astype(jnp.float32)
    feat_norm = jnp.sqrt(jnp.sum(feat * feat, axis=1))
    factor = CLIP / jnp.maximum(feat_norm * resid_norm, CLIP)
    resid = probs - onehot.astype(jnp.float32)
    return (factor[:, None] * resid).astype(jnp.bfloat16)


def coefficient_rows(logits, rows, label):
    f32 = jnp.float32
    top = jnp.max(logits, axis=1, keepdims=True)
    expo = jnp.exp(logits - top)
    onehot = lax.broadcasted_iota(jnp.int32, logits.shape, 1) == label
    rest = jnp.where(onehot, 0.0, expo)
    total = jnp.sum(expo, axis=1, keepdims=True)
    others = jnp.sum(rest, axis=1, keepdims=True)
    squares = jnp.sum(rest * rest, axis=1, keepdims=True)
    feat = rows.astype(f32)
    feat_sq = jnp.sum(feat * feat, axis=1, keepdims=True)
    norm = jnp.sqrt(feat_sq) * jnp.sqrt(squares + others * others) / total
    gain = CLIP / jnp.maximum(norm, CLIP) / total
    return (jnp.where(onehot, -others, expo) * gain).astype(jnp.bfloat16)


def head_kernel(shape, core_ref, feat_ref, label_ref, weight_ref, *refs):
    block, part, slab, skip, columns, cuts = shape
    groups = len(columns)
    outs = refs[:groups], refs[groups : 2 * groups]
    feat, wgt, coef, even, odd, sent, kept, feat_sem, wgt_sem, out_sem = refs[2 * groups :]
    blocks = feat.shape[0] // block
    logits = even, odd

    def load_rows(i):
        at = pl.ds(i * block, block)
        return pltpu.make_async_copy(feat_ref.at[at], feat.at[at], feat_sem.at[i])

    def load_columns(i):
        at = pl.ds(cuts[i], cuts[i + 1] - cuts[i])
        return pltpu.make_async_copy(weight_ref.at[:, at], wgt.at[:, at], wgt_sem.at[i])

    load_rows(0).start()
    for i in range(len(cuts) - 1):
        load_columns(i).start()
    for i in range(1, blocks):
        load_rows(i).start()
    load_rows(0).wait()
    for i in range(len(cuts) - 1):
        load_columns(i).wait()
        even[:, cuts[i] : cuts[i + 1]] = jnp.dot(
            feat[:block, :], wgt[:, cuts[i] : cuts[i + 1]], preferred_element_type=jnp.float32
        )
    for i in range(1, blocks):
        load_rows(i).wait()

    def residuals(i):
        for j in range(block // part):
            r = i * block + j * part
            line = label_ref[r // LANE : r // LANE + 1, :]
            label = jnp.broadcast_to(line, (LANE, LANE)).T[:, :1]
            coef[r : r + part, :] = coefficient_rows(
                logits[i % 2][j * part : (j + 1) * part, :], feat[r : r + part, :], label
            )

    for i in range(1, blocks):
        logits[i % 2][...] = jnp.dot(
            feat[i * block : (i + 1) * block, :], wgt[...], preferred_element_type=jnp.float32
        )
        residuals(i - 1)
    residuals(blocks - 1)

    tiles = slab // LANE
    copies = []
    for side, buf in enumerate((sent, kept)):
        which = core_ref[0] if side else 1 - core_ref[0]
        base = which * (feat_ref.shape[1] - slab)
        for m in range(tiles):
            off = pl.multiple_of(base + m * LANE, LANE)
            buf[m * LANE : (m + 1) * LANE, :] = lax.dot_general(
                feat[:, pl.ds(off, LANE)],
                coef[...],
                (((0,), (0,)), ((), ())),
                preferred_element_type=jnp.float32,
            ).astype(buf.dtype)
            low, high = max(0, m * LANE - skip), (m + 1) * LANE - skip
            source = pl.ds(pl.multiple_of(which * skip + low, ROW), high - low)
            for g, (first, width) in enumerate(columns):
                copies.append(
                    pltpu.make_async_copy(
                        buf.at[source, pl.ds(first, width)],
                        outs[side][g].at[pl.ds(low, high - low)],
                        out_sem.at[len(copies)],
                    )
                )
                copies[-1].start()
    for copy in copies:
        copy.wait()


def halves(features, labels, weight, core, columns):
    n, depth = features.shape
    width = weight.shape[1]
    half = depth // 2
    slab = -(-half // LANE) * LANE
    bf16, f32 = jnp.bfloat16, jnp.float32
    block = 2 * LANE if n % (2 * LANE) == 0 else LANE
    chunks = min(4, width // LANE)
    cuts = [round(width // LANE * i / chunks) * LANE for i in range(chunks + 1)]
    shape = block, LANE, slab, slab - half, columns, cuts
    anywhere = pl.BlockSpec(memory_space=pl.ANY)
    return pl.pallas_call(
        functools.partial(head_kernel, shape),
        in_specs=[
            pl.BlockSpec(memory_space=pltpu.SMEM),
            anywhere,
            pl.BlockSpec(memory_space=pltpu.VMEM),
            anywhere,
        ],
        out_specs=[anywhere] * (2 * len(columns)),
        out_shape=[jax.ShapeDtypeStruct((half, w), bf16) for _, w in columns]
        + [jax.ShapeDtypeStruct((half, w), f32) for _, w in columns],
        scratch_shapes=[
            pltpu.VMEM((n, depth), bf16),
            pltpu.VMEM((depth, width), bf16),
            pltpu.VMEM((n, width), bf16),
            pltpu.VMEM((block, width), f32),
            pltpu.VMEM((block, width), f32),
            pltpu.VMEM((slab, width), bf16),
            pltpu.VMEM((slab, width), f32),
            pltpu.SemaphoreType.DMA((n // block,)),
            pltpu.SemaphoreType.DMA((chunks,)),
            pltpu.SemaphoreType.DMA((2 * slab // LANE * len(columns),)),
        ],
        compiler_params=pltpu.CompilerParams(vmem_limit_bytes=60 << 20),
        cost_estimate=pl.CostEstimate(
            flops=4 * n * depth * width,
            bytes_accessed=2 * n * depth + 5 * depth * width,
            transcendentals=n * width,
        ),
        name="halves",
    )(core.reshape(1), features, labels.reshape(n // LANE, LANE), weight)


def place(blocks, rows, columns, shape, into=None):
    count = len(blocks)

    def kernel(rows_ref, *refs):
        out_ref = refs[-count - 3]
        held, load_sem, save_sem = refs[-count - 2 : -2], refs[-2], refs[-1]
        loads, saves = [], []
        for i in range(count):
            start = pl.multiple_of(rows_ref[i], ROW)
            at = out_ref.at[pl.ds(start, blocks[i].shape[0]), pl.ds(columns[i], blocks[i].shape[1])]
            loads.append(pltpu.make_async_copy(refs[i], held[i], load_sem.at[i]))
            saves.append(pltpu.make_async_copy(held[i], at, save_sem.at[i]))
        for load in loads:
            load.start()
        for load, save in zip(loads, saves):
            load.wait()
            save.start()
        for save in saves:
            save.wait()

    extra = () if into is None else (into,)
    anywhere = pl.BlockSpec(memory_space=pl.ANY)
    return pl.pallas_call(
        kernel,
        in_specs=[pl.BlockSpec(memory_space=pltpu.SMEM)] + [anywhere] * (count + len(extra)),
        out_specs=anywhere,
        out_shape=jax.ShapeDtypeStruct(shape, blocks[0].dtype),
        scratch_shapes=[pltpu.VMEM(b.shape, b.dtype) for b in blocks]
        + [pltpu.SemaphoreType.DMA((count,)), pltpu.SemaphoreType.DMA((count,))],
        input_output_aliases={count + 1: 0} if extra else {},
        compiler_params=pltpu.CompilerParams(vmem_limit_bytes=16 << 20),
        name="place",
    )(jnp.stack(rows).astype(jnp.int32), *blocks, *extra)


def cut(total, pieces):
    own = total // pieces
    starts = [own * k // ROW * ROW for k in range(pieces)]
    window = max(-(-own * (k + 1) // ROW) * ROW - starts[k] for k in range(pieces))
    return [min(s, total - window) for s in starts], window


def rows_of(x, start, count):
    return lax.dynamic_slice_in_dim(x, start, count, 0)


def narrow_share(width):
    tiles = width // LANE
    return max(1, round(tiles * 4 / 11)) * LANE


class Group:
    def __init__(self, stride, count):
        n = lax.axis_size("ex")
        self.count = count
        self.index = lax.axis_index("ex") // stride % count
        self.pairs = [[(i, i ^ (stride * d)) for i in range(n)] for d in range(count)]

    def swap(self, x, d):
        return lax.ppermute(x, "ex", self.pairs[d])

    def sum(self, rows_at, starts):
        got = []
        for d in range(1, self.count):
            sent = rows_at(starts[self.index ^ d]).astype(jnp.bfloat16)
            got.append(self.swap(sent, d))
        total = rows_at(starts[self.index])
        for part in got:
            total = total + part.astype(jnp.float32)
        return total

    def spread(self, x):
        return [x] + [self.swap(x, d) for d in range(1, self.count)]


def two_way(core):
    return [jnp.where(core == 0, 2, 1), jnp.where(core == 0, 1, 2), 3]


def two_way_swaps():
    n = lax.axis_size("ex")
    first = [(i, i ^ (4 if i % 2 else 2)) for i in range(n)]
    second = [(i, i ^ (2 if i % 2 else 4)) for i in range(n)]
    return first, second


def two_way_sum(core, side, rows_at, starts):
    bf16, f32 = jnp.bfloat16, jnp.float32
    first, second = two_way_swaps()
    second_d, first_d, far_d = two_way(core)

    def at(d):
        return rows_at(starts[side.index ^ d])

    sent = jnp.concatenate([at(far_d).astype(bf16), at(first_d).astype(bf16)], axis=0)
    got = lax.ppermute(sent, "ex", first)
    count = sent.shape[0] // 2
    passed = (at(second_d) + got[:count].astype(f32)).astype(bf16)
    last = lax.ppermute(passed, "ex", second)
    return at(0) + got[count:].astype(f32) + last.astype(f32)


def two_way_spread(x, out):
    first, second = two_way_swaps()
    from_second = lax.ppermute(x, "ex", second)
    from_first = lax.ppermute(x, "ex", first)
    from_second, out = lax.optimization_barrier((from_second, out))
    far = lax.ppermute(from_second, "ex", first)
    return [from_second, from_first, far], out


def join(parts, index, own, starts):
    ordered = []
    for k, start in enumerate(starts):
        which = jnp.broadcast_to(index ^ k, parts[0].shape)
        piece = lax.select_n(which.astype(jnp.int32), *parts)
        skip = own * k - start
        ordered.append(piece[skip : skip + own])
    return jnp.concatenate(ordered, axis=0)


def by_rows(features, labels, weight, noise):
    bf16, f32 = jnp.bfloat16, jnp.float32
    n = lax.axis_size("ex")
    layers = n // (2 * SIDES)
    core, side, layer = Group(1, 2), Group(2, SIDES), Group(2 * SIDES, layers)
    depth, width = weight.shape
    half, own = depth // 2, depth // n
    by_side, by_layer = half // SIDES, half // layers
    narrow = narrow_share(width)
    wide = width - narrow
    classes = width * lax.axis_size("cls")
    batch = features.shape[0] * n
    scale = 0.1 * classes / batch

    to_wide, to_narrow = [], []
    for d in range(n):
        c, rest = d // (SIDES * layers), d % (SIDES * layers)
        q, k = rest // layers, rest % layers
        to_wide.append((d, (k * SIDES + q) * 2 + c))
        k, q = rest // SIDES, rest % SIDES
        to_narrow.append((d, (k * SIDES + q) * 2 + c))

    def shifted(noise_own, starts, index):
        count = wide_count if starts is wide_starts else narrow_count
        shapes = []
        for k, start in enumerate(starts):
            skip = own * k - start
            shapes.append(jnp.pad(noise_own, ((skip, count - own - skip), (0, 0))))
        which = jnp.broadcast_to(index, shapes[0].shape)
        return lax.select_n(which.astype(jnp.int32), *shapes)

    def updated(grad, noise_rows, begin, columns):
        rows = lax.dynamic_slice(weight, (begin, jnp.int32(columns)), grad.shape)
        return (
            rows.astype(f32) - scale * (grad + 0.96 * CLIP * noise_rows.astype(f32))
        ).astype(bf16)

    columns = [(wide, narrow), (0, wide)]
    if lax.axis_size("cls") == 1 and features.shape[0] % LANE == 0:
        sent_n, sent_w, kept_n, kept_w = halves(
            features, labels, weight, core.index, columns
        )
    else:
        coef = coefficients(features, labels, weight)
        grad = lax.dot_general(
            features, coef, (((0,), (0,)), ((), ())), preferred_element_type=f32
        )
        sent = rows_of(grad, half * (1 - core.index), half).astype(bf16)
        kept = rows_of(grad, half * core.index, half)
        sent_n, sent_w = sent[:, wide:], sent[:, :wide]
        kept_n, kept_w = kept[:, wide:], kept[:, :wide]

    side_rows = jnp.arange(SIDES, dtype=jnp.int32) * by_side
    layer_rows = jnp.arange(layers, dtype=jnp.int32) * by_layer
    wide_starts, wide_count = cut(by_side, layers)
    narrow_starts, narrow_count = cut(by_layer, SIDES)
    wide_table = jnp.asarray(wide_starts, jnp.int32)
    narrow_table = jnp.asarray(narrow_starts, jnp.int32)

    got_n, got_w = core.swap(sent_n, 1), core.swap(sent_w, 1)
    noise, kept_n, kept_w = lax.optimization_barrier((noise, kept_n, kept_w))
    noise_n = lax.ppermute(noise[:, wide:], "ex", to_narrow)
    noise_w = lax.ppermute(noise[:, :wide], "ex", to_wide)

    def narrow_rows(start):
        return rows_of(kept_n, start, by_layer) + rows_of(got_n, start, by_layer).astype(f32)

    def wide_rows(start):
        return rows_of(kept_w, start, by_side) + rows_of(got_w, start, by_side).astype(f32)

    layer_sum = layer.sum(narrow_rows, layer_rows)
    side_sum = two_way_sum(core.index, side, wide_rows, side_rows)
    noise_n = shifted(noise_n, narrow_starts, side.index)
    noise_w = shifted(noise_w, wide_starts, layer.index)
    layer_sum, side_sum, noise_n, noise_w = lax.optimization_barrier(
        (layer_sum, side_sum, noise_n, noise_w)
    )
    grad_n = side.sum(lambda start: rows_of(layer_sum, start, narrow_count), narrow_table)
    grad_w = layer.sum(lambda start: rows_of(side_sum, start, wide_count), wide_table)

    begin = half * core.index + by_layer * layer.index + narrow_table[side.index]
    new_narrow = updated(grad_n, noise_n, begin, wide)
    begin = half * core.index + by_side * side.index + wide_table[layer.index]
    new_wide = updated(grad_w, noise_w, begin, 0)
    new_narrow, new_wide = lax.optimization_barrier((new_narrow, new_wide))
    layer_parts, side_parts = lax.optimization_barrier(
        (side.spread(new_narrow), layer.spread(new_wide))
    )
    layer_block = join(layer_parts, side.index, own, narrow_starts)
    side_block = join(side_parts, layer.index, own, wide_starts)
    near = [layer_block, side_block]
    near += [core.swap(b, 1) for b in near]
    mine, other = half * core.index, half * (1 - core.index)
    narrow_at = [by_layer * (layer.index ^ d) for d in range(layers)]
    wide_at = [by_side * (side.index ^ d) for d in range(SIDES)]
    rows = [mine + narrow_at[0], mine + wide_at[0], other + narrow_at[0], other + wide_at[0]]
    out = place(near, rows, [wide, 0] * 2, weight.shape)

    blocks = layer.spread(layer_block)[1:]
    side_blocks, out = two_way_spread(side_block, out)
    side_rows = [mine + by_side * (side.index ^ d) for d in two_way(core.index)]
    side_blocks += [core.swap(b, 1) for b in side_blocks]
    side_rows += [other + by_side * (side.index ^ d) for d in two_way(1 - core.index)]
    early = [0, 1, 3, 4]
    out = place(
        [side_blocks[i] for i in early], [side_rows[i] for i in early], [0] * 4, weight.shape, out
    )
    blocks += [core.swap(b, 1) for b in blocks]
    rows = [mine + r for r in narrow_at[1:]] + [other + r for r in narrow_at[1:]]
    columns = [wide] * len(rows) + [0] * 2
    return place(
        blocks + [side_blocks[2], side_blocks[5]],
        rows + [side_rows[2], side_rows[5]],
        columns,
        weight.shape,
        out,
    )


def by_columns(features, labels, weight, noise):
    coef = coefficients(features, labels, weight)
    partial_grad = lax.dot_general(
        features, coef, (((0,), (0,)), ((), ())), preferred_element_type=jnp.float32
    )
    classes = weight.shape[1] * lax.axis_size("cls")
    batch = features.shape[0] * lax.axis_size("ex")
    scale = 0.1 * classes / batch
    grad_part = lax.psum_scatter(partial_grad, "ex", scatter_dimension=0, tiled=True)
    span = grad_part.shape[0]
    own_weight = lax.dynamic_slice_in_dim(weight, lax.axis_index("ex") * span, span, 0)
    updated = own_weight.astype(jnp.float32) - scale * (
        grad_part + 0.96 * CLIP * noise.astype(jnp.float32)
    )
    return lax.all_gather(updated.astype(jnp.bfloat16), "ex", axis=0, tiled=True)


def local(features, labels, weight, noise):
    n = lax.axis_size("ex")
    depth, width = weight.shape
    layers = n // (2 * SIDES)
    fits = n % (2 * SIDES) == 0 and layers > 1 and layers & (layers - 1) == 0
    fits = fits and depth % n == 0 and width % LANE == 0 and width > LANE
    fits = fits and depth % (2 * ROW * SIDES) == 0 and depth % (2 * ROW * layers) == 0
    if not fits:
        return by_columns(features, labels, weight, noise)
    return by_rows(features, labels, weight, noise)


def solution(mesh):
    in_specs = (P("ex", None), P("ex"), P(None, "cls"), P("ex", "cls"))
    out_specs = P(None, "cls")
    return jax.shard_map(
        local, mesh=mesh, in_specs=in_specs, out_specs=out_specs, check_vma=False
    )
```

time: 268 us -> 151 us (0.56)
  the two profiles are of different devices: /device:TPU:0 before, /device:TPU:11 now
where the time goes in v3:
time: 151 us; the launch traced here: 150 us
  waiting for transfers between devices  47.9 us (32%)
  starting transfers between devices  45 us (30%)
  Pallas kernels  28.2 us (19%)
  between operations  16.8 us (11%)
  other arithmetic  10.3 us (7%)
  local copies, waits for them, and re-layouts  2.01 us (1%)
    ppermute x28, waiting for transfers between devices, swap(): return lax.ppermute(x, 'ex', self.pairs[d])  44.9 us
    ppermute x28, starting transfers between devices, swap(): return lax.ppermute(x, 'ex', self.pairs[d])  31.4 us
    pallas_call x1, Pallas kernels, halves(): pl.pallas_call(functools.partial(head_kernel, shape), in_specs=[pl.BlockS...  19.4 us
    pallas_call x3, Pallas kernels, place(): pl.pallas_call(kernel, in_specs=[pl.BlockSpec(memory_space=pltpu.SMEM)] +...  8.78 us
    ppermute x1, starting transfers between devices, by_rows(): noise_w = lax.ppermute(noise[:, :wide], 'ex', to_wide)  5.65 us
  transfers between devices with their start and end apart: 35, of which 13 were waited for; matrix products, arithmetic and copies ran while one was open for 6% of the time, Pallas kernels for 3%

profile of v3, /device:TPU:11, one launch (start us, length us, event | category | flops | bytes accessed | tf_op | source)
XLA Modules:
  0.0 150.2 jit_solution(13569133868756626619)
XLA Ops:
  0.0 19.4 %halves.1 = (bf16[832,512]{1,0:T(8,128)(2,1)}, bf16[832,896]{1,0:T(8,128)(2,1)}, f32[832,512]{1,0:T(8,128)}, f32[832,896]{1,0:T(8,128)}) custom-call(s32[1]{0:T(128)} %bitcast.9.core_ref, bf16[1024,1664]{1,0:T(8,128)(2,1)} %feat_ref.1, s32[8,128]{1,0:T(8,128)} %bitcast.26, bf16[1664,1408]{1,0:T(8,128)(2,1)} %weight_ref.1), custom_call_target="tpu_custom_call" | custom-call | flops 9596567552 | bytes 15122432 | tf_op jit(solution)/shard_map/halves/pallas_call | solution.py:141
  19.4 0.7 collective-permute-start.4
  20.1 0.1 collective-permute-start
  20.2 3.1 %collective-permute-done.4 = bf16[832,896]{1,0:T(8,128)(2,1)S(1)} collective-permute-done((bf16[832,896]{1,0:T(8,128)(2,1)}, bf16[832,896]{1,0:T(8,128)(2,1)S(1)}, u32[]{:S(2)}, u32[]{:S(2)}) %collective-permute-start.4) | collective-permute-done | bytes 1490976 | tf_op jit(solution)/shard_map/ppermute | solution.py:233
  23.3 1.1 copy-done.1
  24.4 1.5 %add_convert_fusion.2 = (bf16[208,896]{1,0:T(8,128)(2,1)S(1)}, bf16[208,896]{1,0:T(8,128)(2,1)S(1)}) fusion(f32[832,896]{1,0:T(8,128)} %get-tuple-element.32, s32[]{:T(128)S(6)} %select_n.349, bf16[832,896]{1,0:T(8,128)(2,1)S(1)} %collective-permute-done.4, s32[]{:T(128)S(6)} %select_n.352), kind=kLoop, calls=%fused_computation.4 | loop fusion | flops 1118208 | bytes 2981896 | tf_op jit(solution)/shard_map/convert_element_type | solution.py:268
  25.9 0.9 pad_maximum_fusion
  26.9 1.2 collective-permute-start.5
  28.1 5.7 %collective-permute-start.8 = (bf16[52,896]{1,0:T(8,128)(2,1)S(1)}, bf16[52,896]{1,0:T(8,128)(2,1)S(1)}, u32[]{:S(2)}, u32[]{:S(2)}) collective-permute-start(bf16[52,896]{1,0:T(8,128)(2,1)S(1)} %slice.39), channel_id=1, source_target_pairs={{0,0},{1,8},{2,16},{3,24},{4,2},{5,10},{6,18},{7,26},{8,4},{9,12},... | collective-permute-start | bytes 279560 | tf_op jit(solution)/shard_map/ppermute | solution.py:357
  33.8 1.9 %collective-permute-start.7 = (bf16[52,512]{1,0:T(8,128)(2,1)S(1)}, bf16[52,512]{1,0:T(8,128)(2,1)S(1)}, u32[]{:S(2)}, u32[]{:S(2)}) collective-permute-start(bf16[52,512]{1,0:T(8,128)(2,1)S(1)} %slice.38), channel_id=1, source_target_pairs={{0,0},{1,2},{2,4},{3,6},{4,8},{5,10},{6,12},{7,14},{8,16},{9,18},{... | collective-permute-start | bytes 159752 | tf_op jit(solution)/shard_map/ppermute | solution.py:356
  35.9 0.7 fusion
  52.8 1.7 %add_convert_fusion.5 = (bf16[208,512]{1,0:T(8,128)(2,1)S(1)}, bf16[208,512]{1,0:T(8,128)(2,1)S(1)}, bf16[208,512]{1,0:T(8,128)(2,1)S(1)}) fusion(f32[832,512]{1,0:T(8,128)} %get-tuple-element.30, s32[]{:T(128)S(6)} %select_n.342, bf16[832,512]{1,0:T(8,128)(2,1)} %collective-permute-done, s32[]{:T(128)S(6)} %select_n.346, s32[]{:T(128)S(6)} %select_n.344), kind=kLoop, calls=%fused_computation.8 | loop fusion | flops 958464 | bytes 2555916 | tf_op jit(solution)/shard_map/convert_element_type | solution.py:238
  54.5 0.3 collective-permute-start.1
  54.8 2.3 %collective-permute-start.2 = (bf16[208,512]{1,0:T(8,128)(2,1)S(1)}, bf16[208,512]{1,0:T(8,128)(2,1)S(1)}, u32[]{:S(2)}, u32[]{:S(2)}) collective-permute-start(bf16[208,512]{1,0:T(8,128)(2,1)S(1)} %get-tuple-element.55), channel_id=1, source_target_pairs={{0,16},{1,17},{2,18},{3,19},{4,20},{5,21},{6,22},{7,23},{8,24},{9,... | collective-permute-start | bytes 638984 | tf_op jit(solution)/shard_map/ppermute | solution.py:233
  57.1 0.1 collective-permute-start.3
  57.2 1.2 add_convert_fusion
  58.4 1.2 collective-permute-start.6
  59.8 4.1 %collective-permute-done.1 = bf16[208,512]{1,0:T(8,128)(2,1)S(1)} collective-permute-done((bf16[208,512]{1,0:T(8,128)(2,1)S(1)}, bf16[208,512]{1,0:T(8,128)(2,1)S(1)}, u32[]{:S(2)}, u32[]{:S(2)}) %collective-permute-start.1) | collective-permute-done | bytes 213024 | tf_op jit(solution)/shard_map/ppermute | solution.py:233
  63.8 7.5 %collective-permute-done.2 = bf16[208,512]{1,0:T(8,128)(2,1)S(1)} collective-permute-done((bf16[208,512]{1,0:T(8,128)(2,1)S(1)}, bf16[208,512]{1,0:T(8,128)(2,1)S(1)}, u32[]{:S(2)}, u32[]{:S(2)}) %collective-permute-start.2) | collective-permute-done | bytes 213024 | tf_op jit(solution)/shard_map/ppermute | solution.py:233
  71.4 4.6 %collective-permute-done.3 = bf16[208,512]{1,0:T(8,128)(2,1)S(1)} collective-permute-done((bf16[208,512]{1,0:T(8,128)(2,1)S(1)}, bf16[208,512]{1,0:T(8,128)(2,1)S(1)}, u32[]{:S(2)}, u32[]{:S(2)}) %collective-permute-start.3) | collective-permute-done | bytes 213024 | tf_op jit(solution)/shard_map/ppermute | solution.py:233
  75.9 1.2 convert_add_fusion.1
  77.1 1.3 convert_add_fusion
  78.5 0.1 collective-permute-start.10
  78.5 2.2 %collective-permute-start.11 = (bf16[56,512]{1,0:T(8,128)(2,1)S(1)}, bf16[56,512]{1,0:T(8,128)(2,1)S(1)}, u32[]{:S(2)}, u32[]{:S(2)}) collective-permute-start(bf16[56,512]{1,0:T(8,128)(2,1)S(1)} %get-tuple-element.60), channel_id=1, source_target_pairs={{0,6},{1,7},{2,4},{3,5},{4,2},{5,3},{6,0},{7,1},{8,14},{9,15},{10,... | collective-permute-start | bytes 172040 | tf_op jit(solution)/shard_map/ppermute | solution.py:233
  80.7 0.5 collective-permute-start.9
  81.2 0.1 collective-permute-start.12
  81.3 3.4 %collective-permute-start.13 = (bf16[56,896]{1,0:T(8,128)(2,1)S(1)}, bf16[56,896]{1,0:T(8,128)(2,1)S(1)}, u32[]{:S(2)}, u32[]{:S(2)}) collective-permute-start(bf16[56,896]{1,0:T(8,128)(2,1)S(1)} %get-tuple-element.58), channel_id=1, source_target_pairs={{0,16},{1,17},{2,18},{3,19},{4,20},{5,21},{6,22},{7,23},{8,24},{9,... | collective-permute-start | bytes 301064 | tf_op jit(solution)/shard_map/ppermute | solution.py:233
  84.7 0.9 subtract_convert_fusion.1
  85.6 2.6 %collective-permute-done.13 = bf16[56,896]{1,0:T(8,128)(2,1)S(1)} collective-permute-done((bf16[56,896]{1,0:T(8,128)(2,1)S(1)}, bf16[56,896]{1,0:T(8,128)(2,1)S(1)}, u32[]{:S(2)}, u32[]{:S(2)}) %collective-permute-start.13) | collective-permute-done | bytes 100384 | tf_op jit(solution)/shard_map/ppermute | solution.py:233
  88.2 4.8 %collective-permute-done.14 = bf16[56,896]{1,0:T(8,128)(2,1)S(1)} collective-permute-done((bf16[56,896]{1,0:T(8,128)(2,1)S(1)}, bf16[56,896]{1,0:T(8,128)(2,1)S(1)}, u32[]{:S(2)}, u32[]{:S(2)}) %collective-permute-start.14) | collective-permute-done | bytes 100384 | tf_op jit(solution)/shard_map/ppermute | solution.py:233
  93.0 1.0 subtract_convert_fusion
  94.0 0.8 collective-permute-start.15
  94.8 2.6 %collective-permute-start.19 = (bf16[56,896]{1,0:T(8,128)(2,1)S(1)}, bf16[56,896]{1,0:T(8,128)(2,1)S(1)}, u32[]{:S(2)}, u32[]{:S(2)}) collective-permute-start(bf16[56,896]{1,0:T(8,128)(2,1)S(1)} %subtract_convert_fusion), channel_id=1, source_target_pairs={{0,16},{1,17},{2,18},{3,19},{4,20},{5,21},{6,22},{7,23},{8,24},{9,... | collective-permute-start | bytes 301064 | tf_op jit(solution)/shard_map/ppermute | solution.py:233
  97.4 0.1 collective-permute-start.20
  97.4 1.3 collective-permute-start.16
  98.7 1.1 collective-permute-start.17
  99.8 0.9 collective-permute-done.16
  100.8 2.2 %collective-permute-done.17 = bf16[56,512]{1,0:T(8,128)(2,1)S(1)} collective-permute-done((bf16[56,512]{1,0:T(8,128)(2,1)S(1)}, bf16[56,512]{1,0:T(8,128)(2,1)S(1)}, u32[]{:S(2)}, u32[]{:S(2)}) %collective-permute-start.17) | collective-permute-done | bytes 57376 | tf_op jit(solution)/shard_map/ppermute | solution.py:233
  103.0 3.1 %collective-permute-done.20 = bf16[56,896]{1,0:T(8,128)(2,1)S(1)} collective-permute-done((bf16[56,896]{1,0:T(8,128)(2,1)S(1)}, bf16[56,896]{1,0:T(8,128)(2,1)S(1)}, u32[]{:S(2)}, u32[]{:S(2)}) %collective-permute-start.20) | collective-permute-done | bytes 100384 | tf_op jit(solution)/shard_map/ppermute | solution.py:233
  106.1 0.1 select_select_fusion.2
  106.2 0.1 pad_maximum_fusion.1.refs_1_
  106.3 1.8 %collective-permute-start.29 = (bf16[208,896]{1,0:T(8,128)(2,1)S(1)}, bf16[208,896]{1,0:T(8,128)(2,1)S(1)}, u32[]{:S(2)}, u32[]{:S(2)}) collective-permute-start(bf16[208,896]{1,0:T(8,128)(2,1)S(1)} %pad_maximum_fusion.1.refs_1_), channel_id=1, source_target_pairs={{0,1},{1,0},{2,3},{3,2},{4,5},{5,4},{6,7},{7,6},{8,9},{9,8},{10,11... | collective-permute-start | bytes 1118216 | tf_op jit(solution)/shard_map/ppermute | solution.py:233
  108.0 1.2 collective-permute-start.27
  109.2 0.1 select_select_fusion.7
  109.4 0.4 collective-permute-start.28
  109.7 0.1 pad_add_fusion.rows_ref
  109.8 0.3 collective-permute-start.32
  110.2 0.7 collective-permute-done.28.refs_2_
  110.9 2.5 %place.3.refs_4_ = bf16[1664,1408]{1,0:T(8,128)(2,1)} custom-call(s32[4]{0:T(128)S(1)} %pad_add_fusion.rows_ref, bf16[208,512]{1,0:T(8,128)(2,1)S(1)} %pad_maximum_fusion.2.refs_0_, bf16[208,896]{1,0:T(8,128)(2,1)S(1)} %pad_maximum_fusion.1.refs_1_, bf16[208,512]{1,0:T(8,128)(2,1)S(1)} %collective-permute-done.28.refs_2_, ...), custom_call_target="tpu_custom_call" | custom-call | tf_op jit(solution)/shard_map/place/pallas_call | solution.py:196
  113.4 2.9 %collective-permute-done.27.refs_0_ = bf16[208,896]{1,0:T(8,128)(2,1)S(1)} collective-permute-done((bf16[208,896]{1,0:T(8,128)(2,1)S(1)}, bf16[208,896]{1,0:T(8,128)(2,1)S(1)}, u32[]{:S(2)}, u32[]{:S(2)}) %collective-permute-start.27) | collective-permute-done | bytes 372768 | tf_op jit(solution)/shard_map/ppermute | solution.py:278
  116.3 2.0 %collective-permute-start.30 = (bf16[208,896]{1,0:T(8,128)(2,1)S(1)}, bf16[208,896]{1,0:T(8,128)(2,1)S(1)}, u32[]{:S(2)}, u32[]{:S(2)}) collective-permute-start(bf16[208,896]{1,0:T(8,128)(2,1)S(1)} %collective-permute-done.27.refs_0_), channel_id=1, source_target_pairs={{0,2},{1,5},{2,0},{3,7},{4,6},{5,1},{6,4},{7,3},{8,10},{9,13},{10,... | collective-permute-start | bytes 1118216 | tf_op jit(solution)/shard_map/ppermute | solution.py:281
  118.4 2.8 %collective-permute-start.33 = (bf16[208,896]{1,0:T(8,128)(2,1)S(1)}, bf16[208,896]{1,0:T(8,128)(2,1)S(1)}, u32[]{:S(2)}, u32[]{:S(2)}) collective-permute-start(bf16[208,896]{1,0:T(8,128)(2,1)S(1)} %collective-permute-done.27.refs_0_), channel_id=1, source_target_pairs={{0,1},{1,0},{2,3},{3,2},{4,5},{5,4},{6,7},{7,6},{8,9},{9,8},{10,11... | collective-permute-start | bytes 1118216 | tf_op jit(solution)/shard_map/ppermute | solution.py:233
  121.2 2.4 %collective-permute-start.22 = (bf16[208,512]{1,0:T(8,128)(2,1)S(1)}, bf16[208,512]{1,0:T(8,128)(2,1)S(1)}, u32[]{:S(2)}, u32[]{:S(2)}) collective-permute-start(bf16[208,512]{1,0:T(8,128)(2,1)S(1)} %pad_maximum_fusion.2.refs_0_), channel_id=1, source_target_pairs={{0,16},{1,17},{2,18},{3,19},{4,20},{5,21},{6,22},{7,23},{8,24},{9,... | collective-permute-start | bytes 638984 | tf_op jit(solution)/shard_map/ppermute | solution.py:233
  123.6 0.2 collective-permute-start.23
  123.8 6.8 %collective-permute-start.34 = (bf16[208,896]{1,0:T(8,128)(2,1)S(1)}, bf16[208,896]{1,0:T(8,128)(2,1)S(1)}, u32[]{:S(2)}, u32[]{:S(2)}) collective-permute-start(bf16[208,896]{1,0:T(8,128)(2,1)S(1)} %collective-permute-done.32.refs_1_), channel_id=1, source_target_pairs={{0,1},{1,0},{2,3},{3,2},{4,5},{5,4},{6,7},{7,6},{8,9},{9,8},{10,11... | collective-permute-start | bytes 1118216 | tf_op jit(solution)/shard_map/ppermute | solution.py:233
  130.5 0.1 collective-permute-start.31
  130.6 6.7 %collective-permute-done.22.refs_1_ = bf16[208,512]{1,0:T(8,128)(2,1)S(1)} collective-permute-done((bf16[208,512]{1,0:T(8,128)(2,1)S(1)}, bf16[208,512]{1,0:T(8,128)(2,1)S(1)}, u32[]{:S(2)}, u32[]{:S(2)}) %collective-permute-start.22) | collective-permute-done | bytes 213024 | tf_op jit(solution)/shard_map/ppermute | solution.py:233
  137.3 0.9 collective-permute-start.24
  138.1 4.7 %collective-permute-done.23.refs_2_ = bf16[208,512]{1,0:T(8,128)(2,1)S(1)} collective-permute-done((bf16[208,512]{1,0:T(8,128)(2,1)S(1)}, bf16[208,512]{1,0:T(8,128)(2,1)S(1)}, u32[]{:S(2)}, u32[]{:S(2)}) %collective-permute-start.23) | collective-permute-done | bytes 213024 | tf_op jit(solution)/shard_map/ppermute | solution.py:233
  142.8 0.6 collective-permute-start.25
  143.5 0.1 stack.65.rows_ref
  143.6 0.1 pad_add_fusion.1.rows_ref
  143.6 2.4 %place.4.refs_8_ = bf16[1664,1408]{1,0:T(8,128)(2,1)} custom-call(s32[4]{0:T(128)S(1)} %pad_add_fusion.1.rows_ref, bf16[208,896]{1,0:T(8,128)(2,1)S(1)} %collective-permute-done.27.refs_0_, bf16[208,896]{1,0:T(8,128)(2,1)S(1)} %collective-permute-done.32.refs_1_, ...), custom_call_target="tpu_custom_call", output_to_operand_aliasing={{}: (5, {})} | custom-call | tf_op jit(solution)/shard_map/place/pallas_call | solution.py:196
  146.1 3.9 %place.5 = bf16[1664,1408]{1,0:T(8,128)(2,1)} custom-call(s32[8]{0:T(128)S(1)} %stack.65.rows_ref, bf16[208,512]{1,0:T(8,128)(2,1)S(1)} %collective-permute-done.21.refs_0_, bf16[208,512]{1,0:T(8,128)(2,1)S(1)} %collective-permute-done.22.refs_1_, bf16[208,512]{1,0:T(8,128)(2,1)S(1)} %collective-permute-done.23.refs_2_, ...), custom_call_target="tpu_custom_call", output_to_operand_aliasing={{}: (9, {})} | custom-call | tf_op jit(solution)/shard_map/place/pallas_call | solution.py:196
  (42 shorter events, 0.4 us)
Async XLA Ops:
  19.4 8.7 %copy-start.2 = (bf16[52,1408]{1,0:T(8,128)(2,1)S(1)}, bf16[52,1408]{1,0:T(8,128)(2,1)}, u32[]{:S(2)}) copy-start(bf16[52,1408]{1,0:T(8,128)(2,1)} %param.9) | copy-start | bytes 439300
  19.4 16.5 %copy-start.3 = (s32[4]{0:T(128)S(1)}, s32[4]{0:T(128)}, u32[]{:S(2)}) copy-start(s32[4]{0:T(128)} %constant.104.clone) | copy-start | bytes 52
  19.4 3.9 %collective-permute-start.4 = (bf16[832,896]{1,0:T(8,128)(2,1)}, bf16[832,896]{1,0:T(8,128)(2,1)S(1)}, u32[]{:S(2)}, u32[]{:S(2)}) collective-permute-start(bf16[832,896]{1,0:T(8,128)(2,1)} %get-tuple-element.33), channel_id=1, source_target_pairs={{0,1},{1,0},{2,3},{3,2},{4,5},{5,4},{6,7},{7,6},{8,9},{9,8},{10,11... | collective-permute-start | bytes 4472840 | tf_op jit(solution)/shard_map/ppermute | solution.py:233
  20.1 32.6 %collective-permute-start = (bf16[832,512]{1,0:T(8,128)(2,1)}, bf16[832,512]{1,0:T(8,128)(2,1)}, u32[]{:S(2)}, u32[]{:S(2)}) collective-permute-start(bf16[832,512]{1,0:T(8,128)(2,1)} %get-tuple-element.31), channel_id=1, source_target_pairs={{0,1},{1,0},{2,3},{3,2},{4,5},{5,4},{6,7},{7,6},{8,9},{9,8},{10,11... | collective-permute-start | bytes 2555912 | tf_op jit(solution)/shard_map/ppermute | solution.py:233
  23.3 1.1 copy-start.1
  25.9 31.3 %copy-start = (f32[832,896]{1,0:T(8,128)S(1)}, f32[832,896]{1,0:T(8,128)}, u32[]{:S(2)}) copy-start(f32[832,896]{1,0:T(8,128)} %get-tuple-element.32) | copy-start | bytes 8945668
  26.9 30.2 %collective-permute-start.5 = (bf16[416,896]{1,0:T(8,128)(2,1)}, bf16[416,896]{1,0:T(8,128)(2,1)}, u32[]{:S(2)}, u32[]{:S(2)}) collective-permute-start(bf16[416,896]{1,0:T(8,128)(2,1)} %pad_maximum_fusion), channel_id=1, source_target_pairs={{0,2},{1,5},{2,0},{3,7},{4,6},{5,1},{6,4},{7,3},{8,10},{9,13},{10,... | collective-permute-start | bytes 2236424 | tf_op jit(solution)/shard_map/ppermute | solution.py:269
  28.1 31.6 %collective-permute-start.8 = (bf16[52,896]{1,0:T(8,128)(2,1)S(1)}, bf16[52,896]{1,0:T(8,128)(2,1)S(1)}, u32[]{:S(2)}, u32[]{:S(2)}) collective-permute-start(bf16[52,896]{1,0:T(8,128)(2,1)S(1)} %slice.39), channel_id=1, source_target_pairs={{0,0},{1,8},{2,16},{3,24},{4,2},{5,10},{6,18},{7,26},{8,4},{9,12},... | collective-permute-start | bytes 279560 | tf_op jit(solution)/shard_map/ppermute | solution.py:357
  33.8 24.6 %collective-permute-start.7 = (bf16[52,512]{1,0:T(8,128)(2,1)S(1)}, bf16[52,512]{1,0:T(8,128)(2,1)S(1)}, u32[]{:S(2)}, u32[]{:S(2)}) collective-permute-start(bf16[52,512]{1,0:T(8,128)(2,1)S(1)} %slice.38), channel_id=1, source_target_pairs={{0,0},{1,2},{2,4},{3,6},{4,8},{5,10},{6,12},{7,14},{8,16},{9,18},{... | collective-permute-start | bytes 159752 | tf_op jit(solution)/shard_map/ppermute | solution.py:356
  54.5 9.3 %collective-permute-start.1 = (bf16[208,512]{1,0:T(8,128)(2,1)S(1)}, bf16[208,512]{1,0:T(8,128)(2,1)S(1)}, u32[]{:S(2)}, u32[]{:S(2)}) collective-permute-start(bf16[208,512]{1,0:T(8,128)(2,1)S(1)} %get-tuple-element.53), channel_id=1, source_target_pairs={{0,8},{1,9},{2,10},{3,11},{4,12},{5,13},{6,14},{7,15},{8,0},{9,1},... | collective-permute-start | bytes 638984 | tf_op jit(solution)/shard_map/ppermute | solution.py:233
  54.8 16.6 %collective-permute-start.2 = (bf16[208,512]{1,0:T(8,128)(2,1)S(1)}, bf16[208,512]{1,0:T(8,128)(2,1)S(1)}, u32[]{:S(2)}, u32[]{:S(2)}) collective-permute-start(bf16[208,512]{1,0:T(8,128)(2,1)S(1)} %get-tuple-element.55), channel_id=1, source_target_pairs={{0,16},{1,17},{2,18},{3,19},{4,20},{5,21},{6,22},{7,23},{8,24},{9,... | collective-permute-start | bytes 638984 | tf_op jit(solution)/shard_map/ppermute | solution.py:233
  57.1 18.8 %collective-permute-start.3 = (bf16[208,512]{1,0:T(8,128)(2,1)S(1)}, bf16[208,512]{1,0:T(8,128)(2,1)S(1)}, u32[]{:S(2)}, u32[]{:S(2)}) collective-permute-start(bf16[208,512]{1,0:T(8,128)(2,1)S(1)} %get-tuple-element.54), channel_id=1, source_target_pairs={{0,24},{1,25},{2,26},{3,27},{4,28},{5,29},{6,30},{7,31},{8,16},{9,... | collective-permute-start | bytes 638984 | tf_op jit(solution)/shard_map/ppermute | solution.py:233
  58.4 18.7 %collective-permute-start.6 = (bf16[208,896]{1,0:T(8,128)(2,1)S(1)}, bf16[208,896]{1,0:T(8,128)(2,1)S(1)}, u32[]{:S(2)}, u32[]{:S(2)}) collective-permute-start(bf16[208,896]{1,0:T(8,128)(2,1)S(1)} %add_convert_fusion), channel_id=1, source_target_pairs={{0,4},{1,3},{2,6},{3,1},{4,0},{5,7},{6,2},{7,5},{8,12},{9,11},{10,... | collective-permute-start | bytes 1118216 | tf_op jit(solution)/shard_map/ppermute | solution.py:272
  78.5 6.2 %collective-permute-start.10 = (bf16[56,512]{1,0:T(8,128)(2,1)S(1)}, bf16[56,512]{1,0:T(8,128)(2,1)S(1)}, u32[]{:S(2)}, u32[]{:S(2)}) collective-permute-start(bf16[56,512]{1,0:T(8,128)(2,1)S(1)} %get-tuple-element.61), channel_id=1, source_target_pairs={{0,4},{1,5},{2,6},{3,7},{4,0},{5,1},{6,2},{7,3},{8,12},{9,13},{10,... | collective-permute-start | bytes 172040 | tf_op jit(solution)/shard_map/ppermute | solution.py:233
  78.5 6.1 %collective-permute-start.11 = (bf16[56,512]{1,0:T(8,128)(2,1)S(1)}, bf16[56,512]{1,0:T(8,128)(2,1)S(1)}, u32[]{:S(2)}, u32[]{:S(2)}) collective-permute-start(bf16[56,512]{1,0:T(8,128)(2,1)S(1)} %get-tuple-element.60), channel_id=1, source_target_pairs={{0,6},{1,7},{2,4},{3,5},{4,2},{5,3},{6,0},{7,1},{8,14},{9,15},{10,... | collective-permute-start | bytes 172040 | tf_op jit(solution)/shard_map/ppermute | solution.py:233
  80.7 4.0 %collective-permute-start.9 = (bf16[56,512]{1,0:T(8,128)(2,1)S(1)}, bf16[56,512]{1,0:T(8,128)(2,1)S(1)}, u32[]{:S(2)}, u32[]{:S(2)}) collective-permute-start(bf16[56,512]{1,0:T(8,128)(2,1)S(1)} %get-tuple-element.59), channel_id=1, source_target_pairs={{0,2},{1,3},{2,0},{3,1},{4,6},{5,7},{6,4},{7,5},{8,10},{9,11},{10,... | collective-permute-start | bytes 172040 | tf_op jit(solution)/shard_map/ppermute | solution.py:233
  81.2 4.4 %collective-permute-start.12 = (bf16[56,896]{1,0:T(8,128)(2,1)S(1)}, bf16[56,896]{1,0:T(8,128)(2,1)S(1)}, u32[]{:S(2)}, u32[]{:S(2)}) collective-permute-start(bf16[56,896]{1,0:T(8,128)(2,1)S(1)} %get-tuple-element.56), channel_id=1, source_target_pairs={{0,8},{1,9},{2,10},{3,11},{4,12},{5,13},{6,14},{7,15},{8,0},{9,1},... | collective-permute-start | bytes 301064 | tf_op jit(solution)/shard_map/ppermute | solution.py:233
  81.3 6.9 %collective-permute-start.13 = (bf16[56,896]{1,0:T(8,128)(2,1)S(1)}, bf16[56,896]{1,0:T(8,128)(2,1)S(1)}, u32[]{:S(2)}, u32[]{:S(2)}) collective-permute-start(bf16[56,896]{1,0:T(8,128)(2,1)S(1)} %get-tuple-element.58), channel_id=1, source_target_pairs={{0,16},{1,17},{2,18},{3,19},{4,20},{5,21},{6,22},{7,23},{8,24},{9,... | collective-permute-start | bytes 301064 | tf_op jit(solution)/shard_map/ppermute | solution.py:233
  84.7 8.3 %collective-permute-start.14 = (bf16[56,896]{1,0:T(8,128)(2,1)S(1)}, bf16[56,896]{1,0:T(8,128)(2,1)S(1)}, u32[]{:S(2)}, u32[]{:S(2)}) collective-permute-start(bf16[56,896]{1,0:T(8,128)(2,1)S(1)} %get-tuple-element.57), channel_id=1, source_target_pairs={{0,24},{1,25},{2,26},{3,27},{4,28},{5,29},{6,30},{7,31},{8,16},{9,... | collective-permute-start | bytes 301064 | tf_op jit(solution)/shard_map/ppermute | solution.py:233
  94.0 4.8 %collective-permute-start.15 = (bf16[56,512]{1,0:T(8,128)(2,1)S(1)}, bf16[56,512]{1,0:T(8,128)(2,1)S(1)}, u32[]{:S(2)}, u32[]{:S(2)}) collective-permute-start(bf16[56,512]{1,0:T(8,128)(2,1)S(1)} %subtract_convert_fusion.1), channel_id=1, source_target_pairs={{0,2},{1,3},{2,0},{3,1},{4,6},{5,7},{6,4},{7,5},{8,10},{9,11},{10,... | collective-permute-start | bytes 172040 | tf_op jit(solution)/shard_map/ppermute | solution.py:233
  94.8 8.2 %collective-permute-start.18 = (bf16[56,896]{1,0:T(8,128)(2,1)S(1)}, bf16[56,896]{1,0:T(8,128)(2,1)S(1)}, u32[]{:S(2)}, u32[]{:S(2)}) collective-permute-start(bf16[56,896]{1,0:T(8,128)(2,1)S(1)} %subtract_convert_fusion), channel_id=1, source_target_pairs={{0,8},{1,9},{2,10},{3,11},{4,12},{5,13},{6,14},{7,15},{8,0},{9,1},... | collective-permute-start | bytes 301064 | tf_op jit(solution)/shard_map/ppermute | solution.py:233
  94.8 8.2 %collective-permute-start.19 = (bf16[56,896]{1,0:T(8,128)(2,1)S(1)}, bf16[56,896]{1,0:T(8,128)(2,1)S(1)}, u32[]{:S(2)}, u32[]{:S(2)}) collective-permute-start(bf16[56,896]{1,0:T(8,128)(2,1)S(1)} %subtract_convert_fusion), channel_id=1, source_target_pairs={{0,16},{1,17},{2,18},{3,19},{4,20},{5,21},{6,22},{7,23},{8,24},{9,... | collective-permute-start | bytes 301064 | tf_op jit(solution)/shard_map/ppermute | solution.py:233
  97.4 8.6 %collective-permute-start.20 = (bf16[56,896]{1,0:T(8,128)(2,1)S(1)}, bf16[56,896]{1,0:T(8,128)(2,1)S(1)}, u32[]{:S(2)}, u32[]{:S(2)}) collective-permute-start(bf16[56,896]{1,0:T(8,128)(2,1)S(1)} %subtract_convert_fusion), channel_id=1, source_target_pairs={{0,24},{1,25},{2,26},{3,27},{4,28},{5,29},{6,30},{7,31},{8,16},{9,... | collective-permute-start | bytes 301064 | tf_op jit(solution)/shard_map/ppermute | solution.py:233
  97.4 3.3 %collective-permute-start.16 = (bf16[56,512]{1,0:T(8,128)(2,1)S(1)}, bf16[56,512]{1,0:T(8,128)(2,1)S(1)}, u32[]{:S(2)}, u32[]{:S(2)}) collective-permute-start(bf16[56,512]{1,0:T(8,128)(2,1)S(1)} %subtract_convert_fusion.1), channel_id=1, source_target_pairs={{0,4},{1,5},{2,6},{3,7},{4,0},{5,1},{6,2},{7,3},{8,12},{9,13},{10,... | collective-permute-start | bytes 172040 | tf_op jit(solution)/shard_map/ppermute | solution.py:233
  98.7 4.2 %collective-permute-start.17 = (bf16[56,512]{1,0:T(8,128)(2,1)S(1)}, bf16[56,512]{1,0:T(8,128)(2,1)S(1)}, u32[]{:S(2)}, u32[]{:S(2)}) collective-permute-start(bf16[56,512]{1,0:T(8,128)(2,1)S(1)} %subtract_convert_fusion.1), channel_id=1, source_target_pairs={{0,6},{1,7},{2,4},{3,5},{4,2},{5,3},{6,0},{7,1},{8,14},{9,15},{10,... | collective-permute-start | bytes 172040 | tf_op jit(solution)/shard_map/ppermute | solution.py:233
  106.3 4.6 %collective-permute-start.29 = (bf16[208,896]{1,0:T(8,128)(2,1)S(1)}, bf16[208,896]{1,0:T(8,128)(2,1)S(1)}, u32[]{:S(2)}, u32[]{:S(2)}) collective-permute-start(bf16[208,896]{1,0:T(8,128)(2,1)S(1)} %pad_maximum_fusion.1.refs_1_), channel_id=1, source_target_pairs={{0,1},{1,0},{2,3},{3,2},{4,5},{5,4},{6,7},{7,6},{8,9},{9,8},{10,11... | collective-permute-start | bytes 1118216 | tf_op jit(solution)/shard_map/ppermute | solution.py:233
  108.0 8.3 %collective-permute-start.27 = (bf16[208,896]{1,0:T(8,128)(2,1)S(1)}, bf16[208,896]{1,0:T(8,128)(2,1)S(1)}, u32[]{:S(2)}, u32[]{:S(2)}) collective-permute-start(bf16[208,896]{1,0:T(8,128)(2,1)S(1)} %pad_maximum_fusion.1.refs_1_), channel_id=1, source_target_pairs={{0,4},{1,3},{2,6},{3,1},{4,0},{5,7},{6,2},{7,5},{8,12},{9,11},{10,... | collective-permute-start | bytes 1118216 | tf_op jit(solution)/shard_map/ppermute | solution.py:278
  109.4 1.5 %collective-permute-start.28 = (bf16[208,512]{1,0:T(8,128)(2,1)S(1)}, bf16[208,512]{1,0:T(8,128)(2,1)S(1)}, u32[]{:S(2)}, u32[]{:S(2)}) collective-permute-start(bf16[208,512]{1,0:T(8,128)(2,1)S(1)} %pad_maximum_fusion.2.refs_0_), channel_id=1, source_target_pairs={{0,1},{1,0},{2,3},{3,2},{4,5},{5,4},{6,7},{7,6},{8,9},{9,8},{10,11... | collective-permute-start | bytes 638984 | tf_op jit(solution)/shard_map/ppermute | solution.py:233
  109.8 13.9 %collective-permute-start.32 = (bf16[208,896]{1,0:T(8,128)(2,1)S(1)}, bf16[208,896]{1,0:T(8,128)(2,1)S(1)}, u32[]{:S(2)}, u32[]{:S(2)}) collective-permute-start(bf16[208,896]{1,0:T(8,128)(2,1)S(1)} %pad_maximum_fusion.1.refs_1_), channel_id=1, source_target_pairs={{0,2},{1,5},{2,0},{3,7},{4,6},{5,1},{6,4},{7,3},{8,10},{9,13},{10,... | collective-permute-start | bytes 1118216 | tf_op jit(solution)/shard_map/ppermute | solution.py:279
  116.3 14.2 %collective-permute-start.30 = (bf16[208,896]{1,0:T(8,128)(2,1)S(1)}, bf16[208,896]{1,0:T(8,128)(2,1)S(1)}, u32[]{:S(2)}, u32[]{:S(2)}) collective-permute-start(bf16[208,896]{1,0:T(8,128)(2,1)S(1)} %collective-permute-done.27.refs_0_), channel_id=1, source_target_pairs={{0,2},{1,5},{2,0},{3,7},{4,6},{5,1},{6,4},{7,3},{8,10},{9,13},{10,... | collective-permute-start | bytes 1118216 | tf_op jit(solution)/shard_map/ppermute | solution.py:281
  118.4 5.2 %collective-permute-start.21 = (bf16[208,512]{1,0:T(8,128)(2,1)S(1)}, bf16[208,512]{1,0:T(8,128)(2,1)S(1)}, u32[]{:S(2)}, u32[]{:S(2)}) collective-permute-start(bf16[208,512]{1,0:T(8,128)(2,1)S(1)} %pad_maximum_fusion.2.refs_0_), channel_id=1, source_target_pairs={{0,8},{1,9},{2,10},{3,11},{4,12},{5,13},{6,14},{7,15},{8,0},{9,1},... | collective-permute-start | bytes 638984 | tf_op jit(solution)/shard_map/ppermute | solution.py:233
  118.4 25.1 %collective-permute-start.33 = (bf16[208,896]{1,0:T(8,128)(2,1)S(1)}, bf16[208,896]{1,0:T(8,128)(2,1)S(1)}, u32[]{:S(2)}, u32[]{:S(2)}) collective-permute-start(bf16[208,896]{1,0:T(8,128)(2,1)S(1)} %collective-permute-done.27.refs_0_), channel_id=1, source_target_pairs={{0,1},{1,0},{2,3},{3,2},{4,5},{5,4},{6,7},{7,6},{8,9},{9,8},{10,11... | collective-permute-start | bytes 1118216 | tf_op jit(solution)/shard_map/ppermute | solution.py:233
  121.2 16.0 %collective-permute-start.22 = (bf16[208,512]{1,0:T(8,128)(2,1)S(1)}, bf16[208,512]{1,0:T(8,128)(2,1)S(1)}, u32[]{:S(2)}, u32[]{:S(2)}) collective-permute-start(bf16[208,512]{1,0:T(8,128)(2,1)S(1)} %pad_maximum_fusion.2.refs_0_), channel_id=1, source_target_pairs={{0,16},{1,17},{2,18},{3,19},{4,20},{5,21},{6,22},{7,23},{8,24},{9,... | collective-permute-start | bytes 638984 | tf_op jit(solution)/shard_map/ppermute | solution.py:233
  123.6 19.3 %collective-permute-start.23 = (bf16[208,512]{1,0:T(8,128)(2,1)S(1)}, bf16[208,512]{1,0:T(8,128)(2,1)S(1)}, u32[]{:S(2)}, u32[]{:S(2)}) collective-permute-start(bf16[208,512]{1,0:T(8,128)(2,1)S(1)} %pad_maximum_fusion.2.refs_0_), channel_id=1, source_target_pairs={{0,24},{1,25},{2,26},{3,27},{4,28},{5,29},{6,30},{7,31},{8,16},{9,... | collective-permute-start | bytes 638984 | tf_op jit(solution)/shard_map/ppermute | solution.py:233
  123.8 19.9 %collective-permute-start.34 = (bf16[208,896]{1,0:T(8,128)(2,1)S(1)}, bf16[208,896]{1,0:T(8,128)(2,1)S(1)}, u32[]{:S(2)}, u32[]{:S(2)}) collective-permute-start(bf16[208,896]{1,0:T(8,128)(2,1)S(1)} %collective-permute-done.32.refs_1_), channel_id=1, source_target_pairs={{0,1},{1,0},{2,3},{3,2},{4,5},{5,4},{6,7},{7,6},{8,9},{9,8},{10,11... | collective-permute-start | bytes 1118216 | tf_op jit(solution)/shard_map/ppermute | solution.py:233
  130.5 15.5 %collective-permute-start.31 = (bf16[208,896]{1,0:T(8,128)(2,1)S(1)}, bf16[208,896]{1,0:T(8,128)(2,1)S(1)}, u32[]{:S(2)}, u32[]{:S(2)}) collective-permute-start(bf16[208,896]{1,0:T(8,128)(2,1)S(1)} %collective-permute-done.30.refs_6_), channel_id=1, source_target_pairs={{0,1},{1,0},{2,3},{3,2},{4,5},{5,4},{6,7},{7,6},{8,9},{9,8},{10,11... | collective-permute-start | bytes 1118216 | tf_op jit(solution)/shard_map/ppermute | solution.py:233
  137.3 8.8 %collective-permute-start.24 = (bf16[208,512]{1,0:T(8,128)(2,1)S(1)}, bf16[208,512]{1,0:T(8,128)(2,1)S(1)}, u32[]{:S(2)}, u32[]{:S(2)}) collective-permute-start(bf16[208,512]{1,0:T(8,128)(2,1)S(1)} %collective-permute-done.21.refs_0_), channel_id=1, source_target_pairs={{0,1},{1,0},{2,3},{3,2},{4,5},{5,4},{6,7},{7,6},{8,9},{9,8},{10,11... | collective-permute-start | bytes 638984 | tf_op jit(solution)/shard_map/ppermute | solution.py:233
  142.8 3.2 %collective-permute-start.25 = (bf16[208,512]{1,0:T(8,128)(2,1)S(1)}, bf16[208,512]{1,0:T(8,128)(2,1)S(1)}, u32[]{:S(2)}, u32[]{:S(2)}) collective-permute-start(bf16[208,512]{1,0:T(8,128)(2,1)S(1)} %collective-permute-done.22.refs_1_), channel_id=1, source_target_pairs={{0,1},{1,0},{2,3},{3,2},{4,5},{5,4},{6,7},{7,6},{8,9},{9,8},{10,11... | collective-permute-start | bytes 638984 | tf_op jit(solution)/shard_map/ppermute | solution.py:233
  143.5 2.6 %collective-permute-start.26 = (bf16[208,512]{1,0:T(8,128)(2,1)S(1)}, bf16[208,512]{1,0:T(8,128)(2,1)S(1)}, u32[]{:S(2)}, u32[]{:S(2)}) collective-permute-start(bf16[208,512]{1,0:T(8,128)(2,1)S(1)} %collective-permute-done.23.refs_2_), channel_id=1, source_target_pairs={{0,1},{1,0},{2,3},{3,2},{4,5},{5,4},{6,7},{7,6},{8,9},{9,8},{10,11... | collective-permute-start | bytes 638984 | tf_op jit(solution)/shard_map/ppermute | solution.py:233

commit v4 on v3

--- a/solution.py
+++ b/solution.py
@@ -53,7 +53,7 @@
     return (jnp.where(onehot, -others, expo) * gain).astype(jnp.bfloat16)
 
 
-def head_kernel(shape, core_ref, feat_ref, label_ref, weight_ref, *refs):
+def head_kernel(shape, feat_ref, label_ref, weight_ref, *refs):
     block, part, slab, skip, columns, cuts = shape
     groups = len(columns)
     outs = refs[:groups], refs[groups : 2 * groups]
@@ -102,7 +102,8 @@
     tiles = slab // LANE
     copies = []
     for side, buf in enumerate((sent, kept)):
-        which = core_ref[0] if side else 1 - core_ref[0]
+        core = lax.axis_index("ex") % 2
+        which = core if side else 1 - core
         base = which * (feat_ref.shape[1] - slab)
         for m in range(tiles):
             off = pl.multiple_of(base + m * LANE, LANE)
@@ -127,7 +128,7 @@
         copy.wait()
 
 
-def halves(features, labels, weight, core, columns):
+def halves(features, labels, weight, columns):
     n, depth = features.shape
     width = weight.shape[1]
     half = depth // 2
@@ -140,12 +141,7 @@
     anywhere = pl.BlockSpec(memory_space=pl.ANY)
     return pl.pallas_call(
         functools.partial(head_kernel, shape),
-        in_specs=[
-            pl.BlockSpec(memory_space=pltpu.SMEM),
-            anywhere,
-            pl.BlockSpec(memory_space=pltpu.VMEM),
-            anywhere,
-        ],
+        in_specs=[anywhere, pl.BlockSpec(memory_space=pltpu.VMEM), anywhere],
         out_specs=[anywhere] * (2 * len(columns)),
         out_shape=[jax.ShapeDtypeStruct((half, w), bf16) for _, w in columns]
         + [jax.ShapeDtypeStruct((half, w), f32) for _, w in columns],
@@ -168,18 +164,19 @@
             transcendentals=n * width,
         ),
         name="halves",
-    )(core.reshape(1), features, labels.reshape(n // LANE, LANE), weight)
+    )(features, labels.reshape(n // LANE, LANE), weight)
 
 
 def place(blocks, rows, columns, shape, into=None):
     count = len(blocks)
 
-    def kernel(rows_ref, *refs):
+    def kernel(*refs):
+        firsts = rows()
         out_ref = refs[-count - 3]
         held, load_sem, save_sem = refs[-count - 2 : -2], refs[-2], refs[-1]
         loads, saves = [], []
         for i in range(count):
-            start = pl.multiple_of(rows_ref[i], ROW)
+            start = pl.multiple_of(firsts[i], ROW)
             at = out_ref.at[pl.ds(start, blocks[i].shape[0]), pl.ds(columns[i], blocks[i].shape[1])]
             loads.append(pltpu.make_async_copy(refs[i], held[i], load_sem.at[i]))
             saves.append(pltpu.make_async_copy(held[i], at, save_sem.at[i]))
@@ -195,22 +192,29 @@
     anywhere = pl.BlockSpec(memory_space=pl.ANY)
     return pl.pallas_call(
         kernel,
-        in_specs=[pl.BlockSpec(memory_space=pltpu.SMEM)] + [anywhere] * (count + len(extra)),
+        in_specs=[anywhere] * (count + len(extra)),
         out_specs=anywhere,
         out_shape=jax.ShapeDtypeStruct(shape, blocks[0].dtype),
         scratch_shapes=[pltpu.VMEM(b.shape, b.dtype) for b in blocks]
         + [pltpu.SemaphoreType.DMA((count,)), pltpu.SemaphoreType.DMA((count,))],
-        input_output_aliases={count + 1: 0} if extra else {},
+        input_output_aliases={count: 0} if extra else {},
         compiler_params=pltpu.CompilerParams(vmem_limit_bytes=16 << 20),
         name="place",
-    )(jnp.stack(rows).astype(jnp.int32), *blocks, *extra)
-
-
-def cut(total, pieces):
-    own = total // pieces
-    starts = [own * k // ROW * ROW for k in range(pieces)]
-    window = max(-(-own * (k + 1) // ROW) * ROW - starts[k] for k in range(pieces))
-    return [min(s, total - window) for s in starts], window
+    )(*blocks, *extra)
+
+
+class Cut:
+    def __init__(self, total, pieces):
+        self.own, self.pieces = total // pieces, pieces
+        firsts = [self.own * k // ROW * ROW for k in range(pieces)]
+        lasts = [-(-self.own * (k + 1) // ROW) * ROW for k in range(pieces)]
+        self.count = max(last - first for first, last in zip(firsts, lasts))
+        self.most = total - self.count
+        self.skips = [self.own * k - min(f, self.most) for k, f in enumerate(firsts)]
+
+    def start(self, k):
+        first = self.own * k
+        return lax.min(first - lax.rem(first, ROW), jnp.int32(self.most))
 
 
 def rows_of(x, start, count):
@@ -232,12 +236,12 @@
     def swap(self, x, d):
         return lax.ppermute(x, "ex", self.pairs[d])
 
-    def sum(self, rows_at, starts):
+    def sum(self, rows_at):
         got = []
-        for d in range(1, self.count):
-            sent = rows_at(starts[self.index ^ d]).astype(jnp.bfloat16)
+        for d in reversed(range(1, self.count)):
+            sent = rows_at(self.index ^ d).astype(jnp.bfloat16)
             got.append(self.swap(sent, d))
-        total = rows_at(starts[self.index])
+        total = rows_at(self.index)
         for part in got:
             total = total + part.astype(jnp.float32)
         return total
@@ -257,13 +261,13 @@
     return first, second
 
 
-def two_way_sum(core, side, rows_at, starts):
+def two_way_sum(core, side, rows_at):
     bf16, f32 = jnp.bfloat16, jnp.float32
     first, second = two_way_swaps()
     second_d, first_d, far_d = two_way(core)
 
     def at(d):
-        return rows_at(starts[side.index ^ d])
+        return rows_at(side.index ^ d)
 
     sent = jnp.concatenate([at(far_d).astype(bf16), at(first_d).astype(bf16)], axis=0)
     got = lax.ppermute(sent, "ex", first)
@@ -273,22 +277,20 @@
     return at(0) + got[count:].astype(f32) + last.astype(f32)
 
 
-def two_way_spread(x, out):
+def two_way_spread(x):
     first, second = two_way_swaps()
     from_second = lax.ppermute(x, "ex", second)
     from_first = lax.ppermute(x, "ex", first)
-    from_second, out = lax.optimization_barrier((from_second, out))
     far = lax.ppermute(from_second, "ex", first)
-    return [from_second, from_first, far], out
-
-
-def join(parts, index, own, starts):
+    return [from_second, from_first, far]
+
+
+def join(parts, index, cut):
     ordered = []
-    for k, start in enumerate(starts):
+    for k, skip in enumerate(cut.skips):
         which = jnp.broadcast_to(index ^ k, parts[0].shape)
         piece = lax.select_n(which.astype(jnp.int32), *parts)
-        skip = own * k - start
-        ordered.append(piece[skip : skip + own])
+        ordered.append(piece[skip : skip + cut.own])
     return jnp.concatenate(ordered, axis=0)
 
 
@@ -314,12 +316,12 @@
         k, q = rest // SIDES, rest % SIDES
         to_narrow.append((d, (k * SIDES + q) * 2 + c))
 
-    def shifted(noise_own, starts, index):
-        count = wide_count if starts is wide_starts else narrow_count
+    wide_cut, narrow_cut = Cut(by_side, layers), Cut(by_layer, SIDES)
+
+    def shifted(noise_own, cut, index):
         shapes = []
-        for k, start in enumerate(starts):
-            skip = own * k - start
-            shapes.append(jnp.pad(noise_own, ((skip, count - own - skip), (0, 0))))
+        for skip in cut.skips:
+            shapes.append(jnp.pad(noise_own, ((skip, cut.count - own - skip), (0, 0))))
         which = jnp.broadcast_to(index, shapes[0].shape)
         return lax.select_n(which.astype(jnp.int32), *shapes)
 
@@ -332,7 +334,7 @@
     columns = [(wide, narrow), (0, wide)]
     if lax.axis_size("cls") == 1 and features.shape[0] % LANE == 0:
         sent_n, sent_w, kept_n, kept_w = halves(
-            features, labels, weight, core.index, columns
+            features, labels, weight, columns
         )
     else:
         coef = coefficients(features, labels, weight)
@@ -344,71 +346,76 @@
         sent_n, sent_w = sent[:, wide:], sent[:, :wide]
         kept_n, kept_w = kept[:, wide:], kept[:, :wide]
 
-    side_rows = jnp.arange(SIDES, dtype=jnp.int32) * by_side
-    layer_rows = jnp.arange(layers, dtype=jnp.int32) * by_layer
-    wide_starts, wide_count = cut(by_side, layers)
-    narrow_starts, narrow_count = cut(by_layer, SIDES)
-    wide_table = jnp.asarray(wide_starts, jnp.int32)
-    narrow_table = jnp.asarray(narrow_starts, jnp.int32)
-
-    got_n, got_w = core.swap(sent_n, 1), core.swap(sent_w, 1)
+    got_n = core.swap(sent_n, 1)
+    got_w = core.swap(sent_w, 1)
     noise, kept_n, kept_w = lax.optimization_barrier((noise, kept_n, kept_w))
     noise_n = lax.ppermute(noise[:, wide:], "ex", to_narrow)
     noise_w = lax.ppermute(noise[:, :wide], "ex", to_wide)
 
-    def narrow_rows(start):
+    def narrow_rows(k):
+        start = by_layer * k
         return rows_of(kept_n, start, by_layer) + rows_of(got_n, start, by_layer).astype(f32)
 
-    def wide_rows(start):
+    def wide_rows(k):
+        start = by_side * k
         return rows_of(kept_w, start, by_side) + rows_of(got_w, start, by_side).astype(f32)
 
-    layer_sum = layer.sum(narrow_rows, layer_rows)
-    side_sum = two_way_sum(core.index, side, wide_rows, side_rows)
-    noise_n = shifted(noise_n, narrow_starts, side.index)
-    noise_w = shifted(noise_w, wide_starts, layer.index)
-    layer_sum, side_sum, noise_n, noise_w = lax.optimization_barrier(
-        (layer_sum, side_sum, noise_n, noise_w)
-    )
-    grad_n = side.sum(lambda start: rows_of(layer_sum, start, narrow_count), narrow_table)
-    grad_w = layer.sum(lambda start: rows_of(side_sum, start, wide_count), wide_table)
-
-    begin = half * core.index + by_layer * layer.index + narrow_table[side.index]
+    layer_sum = layer.sum(narrow_rows)
+    side_sum = two_way_sum(core.index, side, wide_rows)
+    layer_sum, side_sum = lax.optimization_barrier((layer_sum, side_sum))
+    noise_n = shifted(noise_n, narrow_cut, side.index)
+    noise_w = shifted(noise_w, wide_cut, layer.index)
+    noise_n, noise_w = lax.optimization_barrier((noise_n, noise_w))
+    grad_n = side.sum(lambda k: rows_of(layer_sum, narrow_cut.start(k), narrow_cut.count))
+    grad_w = layer.sum(lambda k: rows_of(side_sum, wide_cut.start(k), wide_cut.count))
+
+    begin = half * core.index + by_layer * layer.index + narrow_cut.start(side.index)
     new_narrow = updated(grad_n, noise_n, begin, wide)
-    begin = half * core.index + by_side * side.index + wide_table[layer.index]
+    begin = half * core.index + by_side * side.index + wide_cut.start(layer.index)
     new_wide = updated(grad_w, noise_w, begin, 0)
     new_narrow, new_wide = lax.optimization_barrier((new_narrow, new_wide))
     layer_parts, side_parts = lax.optimization_barrier(
         (side.spread(new_narrow), layer.spread(new_wide))
     )
-    layer_block = join(layer_parts, side.index, own, narrow_starts)
-    side_block = join(side_parts, layer.index, own, wide_starts)
+    layer_block = join(layer_parts, side.index, narrow_cut)
+    side_block = join(side_parts, layer.index, wide_cut)
     near = [layer_block, side_block]
     near += [core.swap(b, 1) for b in near]
-    mine, other = half * core.index, half * (1 - core.index)
-    narrow_at = [by_layer * (layer.index ^ d) for d in range(layers)]
-    wide_at = [by_side * (side.index ^ d) for d in range(SIDES)]
-    rows = [mine + narrow_at[0], mine + wide_at[0], other + narrow_at[0], other + wide_at[0]]
-    out = place(near, rows, [wide, 0] * 2, weight.shape)
+
+    def rows_in(of_core):
+        def rows():
+            at = lax.axis_index("ex")
+            c = at % 2 if of_core == 0 else 1 - at % 2
+            q, k = at // 2 % SIDES, at // (2 * SIDES)
+            narrow_at = [half * c + by_layer * (k ^ d) for d in range(layers)]
+            wide_at = [half * c + by_side * (q ^ d) for d in [0] + two_way(c)]
+            return narrow_at, wide_at
+
+        return rows
+
+    def near_rows():
+        (a, b), (c, d) = rows_in(0)(), rows_in(1)()
+        return [a[0], b[0], c[0], d[0]]
+
+    def early_rows():
+        (_, b), (_, d) = rows_in(0)(), rows_in(1)()
+        return b[1:3] + d[1:3]
+
+    def late_rows():
+        (a, b), (c, d) = rows_in(0)(), rows_in(1)()
+        return a[1:] + c[1:] + [b[3], d[3]]
+
+    out = place(near, near_rows, [wide, 0] * 2, weight.shape)
 
     blocks = layer.spread(layer_block)[1:]
-    side_blocks, out = two_way_spread(side_block, out)
-    side_rows = [mine + by_side * (side.index ^ d) for d in two_way(core.index)]
+    side_blocks = two_way_spread(side_block)
     side_blocks += [core.swap(b, 1) for b in side_blocks]
-    side_rows += [other + by_side * (side.index ^ d) for d in two_way(1 - core.index)]
-    early = [0, 1, 3, 4]
-    out = place(
-        [side_blocks[i] for i in early], [side_rows[i] for i in early], [0] * 4, weight.shape, out
-    )
+    early = [side_blocks[i] for i in (0, 1, 3, 4)]
+    out = place(early, early_rows, [0] * 4, weight.shape, out)
     blocks += [core.swap(b, 1) for b in blocks]
-    rows = [mine + r for r in narrow_at[1:]] + [other + r for r in narrow_at[1:]]
-    columns = [wide] * len(rows) + [0] * 2
-    return place(
-        blocks + [side_blocks[2], side_blocks[5]],
-        rows + [side_rows[2], side_rows[5]],
-        columns,
-        weight.shape,
-        out,
-    )
+    columns = [wide] * len(blocks) + [0] * 2
+    blocks += [side_blocks[2], side_blocks[5]]
+    return place(blocks, late_rows, columns, weight.shape, out)
 
 
 def by_columns(features, labels, weight, noise):

time: 151 us -> 131 us (0.87)
  the two profiles are of different devices: /device:TPU:11 before, /device:TPU:0 now
where the time goes in v4:
time: 131 us
  starting transfers between devices  47 us (36%)
  waiting for transfers between devices  45 us (34%)
  Pallas kernels  26.5 us (20%)
  other arithmetic  10.2 us (8%)
    ppermute x28, waiting for transfers between devices, swap(): return lax.ppermute(x, 'ex', self.pairs[d])  38.9 us
    ppermute x28, starting transfers between devices, swap(): return lax.ppermute(x, 'ex', self.pairs[d])  34.4 us
    pallas_call x1, Pallas kernels, halves(): pl.pallas_call(functools.partial(head_kernel, shape), in_specs=[anywhere,...  19.4 us
    pallas_call x3, Pallas kernels, place(): pl.pallas_call(kernel, in_specs=[anywhere] * (count + len(extra)), out_sp...  7.16 us
    ppermute x1, waiting for transfers between devices, two_way_spread(): from_second = lax.ppermute(x, 'ex', second)  6.12 us
    ppermute x1, starting transfers between devices, two_way_sum(): last = lax.ppermute(passed, 'ex', second)  6.11 us
    ppermute x1, starting transfers between devices, two_way_sum(): got = lax.ppermute(sent, 'ex', first)  2.84 us
  transfers between devices with their start and end apart: 35, of which 10 were waited for; matrix products, arithmetic and copies ran while one was open for 6% of the time, Pallas kernels for 3%

profile of v4, /device:TPU:0, one launch (start us, length us, event | category | flops | bytes accessed | tf_op | source)
XLA Modules:
  0.0 130.7 jit_solution(13685160242073488814)
XLA Ops:
  0.0 19.4 %halves.1 = (bf16[832,512]{1,0:T(8,128)(2,1)}, bf16[832,896]{1,0:T(8,128)(2,1)}, f32[832,512]{1,0:T(8,128)}, f32[832,896]{1,0:T(8,128)}) custom-call(bf16[1024,1664]{1,0:T(8,128)(2,1)} %feat_ref.1, s32[8,128]{1,0:T(8,128)} %bitcast.1, bf16[1664,1408]{1,0:T(8,128)(2,1)} %weight_ref.1), custom_call_target="tpu_custom_call" | custom-call | flops 9596567552 | bytes 15122432 | tf_op jit(solution)/shard_map/halves/pallas_call | solution.py:142
  19.4 0.0 copy-start.2
  19.4 0.6 collective-permute-start.4
  19.9 0.1 collective-permute-start
  20.0 3.1 %collective-permute-done.4 = bf16[832,896]{1,0:T(8,128)(2,1)S(1)} collective-permute-done((bf16[832,896]{1,0:T(8,128)(2,1)}, bf16[832,896]{1,0:T(8,128)(2,1)S(1)}, u32[]{:S(2)}, u32[]{:S(2)}) %collective-permute-start.4) | collective-permute-done | bytes 1490976 | tf_op jit(solution)/shard_map/ppermute | solution.py:237
  23.1 1.1 copy-done.1
  24.2 1.5 %add_convert_fusion.2 = (bf16[208,896]{1,0:T(8,128)(2,1)S(1)}, bf16[208,896]{1,0:T(8,128)(2,1)S(1)}) fusion(f32[832,896]{1,0:T(8,128)} %get-tuple-element.30, s32[]{:T(128)S(6)} %select_n.297, bf16[832,896]{1,0:T(8,128)(2,1)S(1)} %collective-permute-done.4, s32[]{:T(128)S(6)} %select_n.299), kind=kLoop, calls=%fused_computation.4 | loop fusion | flops 1118208 | bytes 2981896 | tf_op jit(solution)/shard_map/convert_element_type | solution.py:272
  25.7 0.0 copy-start
  25.7 0.9 pad_maximum_fusion
  26.7 2.8 %collective-permute-start.5 = (bf16[416,896]{1,0:T(8,128)(2,1)}, bf16[416,896]{1,0:T(8,128)(2,1)}, u32[]{:S(2)}, u32[]{:S(2)}) collective-permute-start(bf16[416,896]{1,0:T(8,128)(2,1)} %pad_maximum_fusion), channel_id=1, source_target_pairs={{0,2},{1,5},{2,0},{3,7},{4,6},{5,1},{6,4},{7,3},{8,10},{9,13},{10,... | collective-permute-start | bytes 2236424 | tf_op jit(solution)/shard_map/ppermute | solution.py:273
  29.5 0.7 collective-permute-start.11
  30.2 0.7 collective-permute-start.10
  31.1 0.0 collective-permute-done
  31.1 1.7 %add_convert_fusion.5 = (bf16[208,512]{1,0:T(8,128)(2,1)S(1)}, bf16[208,512]{1,0:T(8,128)(2,1)S(1)}, bf16[208,512]{1,0:T(8,128)(2,1)S(1)}) fusion(f32[832,512]{1,0:T(8,128)} %get-tuple-element.28, s32[]{:T(128)S(6)} %select_n.293, bf16[832,512]{1,0:T(8,128)(2,1)} %collective-permute-done, s32[]{:T(128)S(6)} %select_n.295, s32[]{:T(128)S(6)} %select_n.294), kind=kLoop, calls=%fused_computation.8 | loop fusion | flops 958464 | bytes 2555916 | tf_op jit(solution)/shard_map/convert_element_type | solution.py:242
  32.8 6.3 %collective-permute-start.1 = (bf16[208,512]{1,0:T(8,128)(2,1)S(1)}, bf16[208,512]{1,0:T(8,128)(2,1)S(1)}, u32[]{:S(2)}, u32[]{:S(2)}) collective-permute-start(bf16[208,512]{1,0:T(8,128)(2,1)S(1)} %get-tuple-element.49), channel_id=1, source_target_pairs={{0,24},{1,25},{2,26},{3,27},{4,28},{5,29},{6,30},{7,31},{8,16},{9,... | collective-permute-start | bytes 638984 | tf_op jit(solution)/shard_map/ppermute | solution.py:237
  39.1 0.9 collective-permute-start.2
  40.0 1.4 %collective-permute-start.3 = (bf16[208,512]{1,0:T(8,128)(2,1)S(1)}, bf16[208,512]{1,0:T(8,128)(2,1)S(1)}, u32[]{:S(2)}, u32[]{:S(2)}) collective-permute-start(bf16[208,512]{1,0:T(8,128)(2,1)S(1)} %get-tuple-element.50), channel_id=1, source_target_pairs={{0,8},{1,9},{2,10},{3,11},{4,12},{5,13},{6,14},{7,15},{8,0},{9,1},... | collective-permute-start | bytes 638984 | tf_op jit(solution)/shard_map/ppermute | solution.py:237
  41.5 1.2 add_convert_fusion
  42.7 6.1 %collective-permute-start.6 = (bf16[208,896]{1,0:T(8,128)(2,1)S(1)}, bf16[208,896]{1,0:T(8,128)(2,1)S(1)}, u32[]{:S(2)}, u32[]{:S(2)}) collective-permute-start(bf16[208,896]{1,0:T(8,128)(2,1)S(1)} %add_convert_fusion), channel_id=1, source_target_pairs={{0,4},{1,3},{2,6},{3,1},{4,0},{5,7},{6,2},{7,5},{8,12},{9,11},{10,... | collective-permute-start | bytes 1118216 | tf_op jit(solution)/shard_map/ppermute | solution.py:276
  48.8 0.0 collective-permute-done.11
  48.9 0.1 select_select_fusion.4
  48.9 0.0 collective-permute-done.1
  48.9 10.0 %collective-permute-done.2 = bf16[208,512]{1,0:T(8,128)(2,1)S(1)} collective-permute-done((bf16[208,512]{1,0:T(8,128)(2,1)S(1)}, bf16[208,512]{1,0:T(8,128)(2,1)S(1)}, u32[]{:S(2)}, u32[]{:S(2)}) %collective-permute-start.2) | collective-permute-done | bytes 213024 | tf_op jit(solution)/shard_map/ppermute | solution.py:237
  58.9 0.0 collective-permute-done.3
  58.9 1.2 convert_add_fusion.1
  60.1 1.3 convert_add_fusion
  61.5 2.6 %collective-permute-start.7 = (bf16[56,512]{1,0:T(8,128)(2,1)S(1)}, bf16[56,512]{1,0:T(8,128)(2,1)S(1)}, u32[]{:S(2)}, u32[]{:S(2)}) collective-permute-start(bf16[56,512]{1,0:T(8,128)(2,1)S(1)} %get-tuple-element.55), channel_id=1, source_target_pairs={{0,6},{1,7},{2,4},{3,5},{4,2},{5,3},{6,0},{7,1},{8,14},{9,15},{10,... | collective-permute-start | bytes 172040 | tf_op jit(solution)/shard_map/ppermute | solution.py:237
  64.1 2.4 %collective-permute-start.8 = (bf16[56,512]{1,0:T(8,128)(2,1)S(1)}, bf16[56,512]{1,0:T(8,128)(2,1)S(1)}, u32[]{:S(2)}, u32[]{:S(2)}) collective-permute-start(bf16[56,512]{1,0:T(8,128)(2,1)S(1)} %get-tuple-element.57), channel_id=1, source_target_pairs={{0,4},{1,5},{2,6},{3,7},{4,0},{5,1},{6,2},{7,3},{8,12},{9,13},{10,... | collective-permute-start | bytes 172040 | tf_op jit(solution)/shard_map/ppermute | solution.py:237
  66.5 0.1 dynamic-slice_convert_fusion.2
  66.5 2.1 %collective-permute-start.12 = (bf16[56,896]{1,0:T(8,128)(2,1)S(1)}, bf16[56,896]{1,0:T(8,128)(2,1)S(1)}, u32[]{:S(2)}, u32[]{:S(2)}) collective-permute-start(bf16[56,896]{1,0:T(8,128)(2,1)S(1)} %get-tuple-element.52), channel_id=1, source_target_pairs={{0,24},{1,25},{2,26},{3,27},{4,28},{5,29},{6,30},{7,31},{8,16},{9,... | collective-permute-start | bytes 301064 | tf_op jit(solution)/shard_map/ppermute | solution.py:237
  68.6 0.0 collective-permute-start.13
  68.6 2.4 %collective-permute-start.14 = (bf16[56,896]{1,0:T(8,128)(2,1)S(1)}, bf16[56,896]{1,0:T(8,128)(2,1)S(1)}, u32[]{:S(2)}, u32[]{:S(2)}) collective-permute-start(bf16[56,896]{1,0:T(8,128)(2,1)S(1)} %get-tuple-element.53), channel_id=1, source_target_pairs={{0,8},{1,9},{2,10},{3,11},{4,12},{5,13},{6,14},{7,15},{8,0},{9,1},... | collective-permute-start | bytes 301064 | tf_op jit(solution)/shard_map/ppermute | solution.py:237
  71.0 0.9 subtract_convert_fusion.1
  71.9 2.2 %collective-permute-done.12 = bf16[56,896]{1,0:T(8,128)(2,1)S(1)} collective-permute-done((bf16[56,896]{1,0:T(8,128)(2,1)S(1)}, bf16[56,896]{1,0:T(8,128)(2,1)S(1)}, u32[]{:S(2)}, u32[]{:S(2)}) %collective-permute-start.12) | collective-permute-done | bytes 100384 | tf_op jit(solution)/shard_map/ppermute | solution.py:237
  74.1 2.5 %collective-permute-done.13 = bf16[56,896]{1,0:T(8,128)(2,1)S(1)} collective-permute-done((bf16[56,896]{1,0:T(8,128)(2,1)S(1)}, bf16[56,896]{1,0:T(8,128)(2,1)S(1)}, u32[]{:S(2)}, u32[]{:S(2)}) %collective-permute-start.13) | collective-permute-done | bytes 100384 | tf_op jit(solution)/shard_map/ppermute | solution.py:237
  76.6 1.0 subtract_convert_fusion
  77.6 1.8 %collective-permute-start.15 = (bf16[56,512]{1,0:T(8,128)(2,1)S(1)}, bf16[56,512]{1,0:T(8,128)(2,1)S(1)}, u32[]{:S(2)}, u32[]{:S(2)}) collective-permute-start(bf16[56,512]{1,0:T(8,128)(2,1)S(1)} %subtract_convert_fusion.1), channel_id=1, source_target_pairs={{0,2},{1,3},{2,0},{3,1},{4,6},{5,7},{6,4},{7,5},{8,10},{9,11},{10,... | collective-permute-start | bytes 172040 | tf_op jit(solution)/shard_map/ppermute | solution.py:237
  79.4 0.6 collective-permute-start.18
  80.1 2.4 %collective-permute-start.19 = (bf16[56,896]{1,0:T(8,128)(2,1)S(1)}, bf16[56,896]{1,0:T(8,128)(2,1)S(1)}, u32[]{:S(2)}, u32[]{:S(2)}) collective-permute-start(bf16[56,896]{1,0:T(8,128)(2,1)S(1)} %subtract_convert_fusion), channel_id=1, source_target_pairs={{0,16},{1,17},{2,18},{3,19},{4,20},{5,21},{6,22},{7,23},{8,24},{9,... | collective-permute-start | bytes 301064 | tf_op jit(solution)/shard_map/ppermute | solution.py:237
  82.5 1.4 %collective-permute-start.20 = (bf16[56,896]{1,0:T(8,128)(2,1)S(1)}, bf16[56,896]{1,0:T(8,128)(2,1)S(1)}, u32[]{:S(2)}, u32[]{:S(2)}) collective-permute-start(bf16[56,896]{1,0:T(8,128)(2,1)S(1)} %subtract_convert_fusion), channel_id=1, source_target_pairs={{0,24},{1,25},{2,26},{3,27},{4,28},{5,29},{6,30},{7,31},{8,16},{9,... | collective-permute-start | bytes 301064 | tf_op jit(solution)/shard_map/ppermute | solution.py:237
  83.8 0.3 collective-permute-start.16
  84.1 1.5 %collective-permute-start.17 = (bf16[56,512]{1,0:T(8,128)(2,1)S(1)}, bf16[56,512]{1,0:T(8,128)(2,1)S(1)}, u32[]{:S(2)}, u32[]{:S(2)}) collective-permute-start(bf16[56,512]{1,0:T(8,128)(2,1)S(1)} %subtract_convert_fusion.1), channel_id=1, source_target_pairs={{0,6},{1,7},{2,4},{3,5},{4,2},{5,3},{6,0},{7,1},{8,14},{9,15},{10,... | collective-permute-start | bytes 172040 | tf_op jit(solution)/shard_map/ppermute | solution.py:237
  85.6 2.4 %collective-permute-done.16 = bf16[56,512]{1,0:T(8,128)(2,1)S(1)} collective-permute-done((bf16[56,512]{1,0:T(8,128)(2,1)S(1)}, bf16[56,512]{1,0:T(8,128)(2,1)S(1)}, u32[]{:S(2)}, u32[]{:S(2)}) %collective-permute-start.16) | collective-permute-done | bytes 57376 | tf_op jit(solution)/shard_map/ppermute | solution.py:237
  88.0 1.2 collective-permute-done.17
  89.2 1.1 collective-permute-done.19
  90.3 0.1 select_select_fusion.2
  90.5 0.1 pad_maximum_fusion.1.refs_1_
  90.6 0.7 collective-permute-start.27
  91.3 0.1 select_select_fusion.7
  91.4 0.1 collective-permute-start.33
  91.5 1.4 %collective-permute-start.21 = (bf16[208,512]{1,0:T(8,128)(2,1)S(1)}, bf16[208,512]{1,0:T(8,128)(2,1)S(1)}, u32[]{:S(2)}, u32[]{:S(2)}) collective-permute-start(bf16[208,512]{1,0:T(8,128)(2,1)S(1)} %pad_maximum_fusion.2.refs_0_), channel_id=1, source_target_pairs={{0,8},{1,9},{2,10},{3,11},{4,12},{5,13},{6,14},{7,15},{8,0},{9,1},... | collective-permute-start | bytes 638984 | tf_op jit(solution)/shard_map/ppermute | solution.py:237
  92.9 1.6 %collective-permute-start.30 = (bf16[208,896]{1,0:T(8,128)(2,1)S(1)}, bf16[208,896]{1,0:T(8,128)(2,1)S(1)}, u32[]{:S(2)}, u32[]{:S(2)}) collective-permute-start(bf16[208,896]{1,0:T(8,128)(2,1)S(1)} %pad_maximum_fusion.1.refs_1_), channel_id=1, source_target_pairs={{0,2},{1,5},{2,0},{3,7},{4,6},{5,1},{6,4},{7,3},{8,10},{9,13},{10,... | collective-permute-start | bytes 1118216 | tf_op jit(solution)/shard_map/ppermute | solution.py:283
  94.5 6.1 %collective-permute-done.27.refs_0_ = bf16[208,896]{1,0:T(8,128)(2,1)S(1)} collective-permute-done((bf16[208,896]{1,0:T(8,128)(2,1)S(1)}, bf16[208,896]{1,0:T(8,128)(2,1)S(1)}, u32[]{:S(2)}, u32[]{:S(2)}) %collective-permute-start.27) | collective-permute-done | bytes 372768 | tf_op jit(solution)/shard_map/ppermute | solution.py:282
  100.7 3.9 %collective-permute-start.22 = (bf16[208,512]{1,0:T(8,128)(2,1)S(1)}, bf16[208,512]{1,0:T(8,128)(2,1)S(1)}, u32[]{:S(2)}, u32[]{:S(2)}) collective-permute-start(bf16[208,512]{1,0:T(8,128)(2,1)S(1)} %pad_maximum_fusion.2.refs_0_), channel_id=1, source_target_pairs={{0,16},{1,17},{2,18},{3,19},{4,20},{5,21},{6,22},{7,23},{8,24},{9,... | collective-permute-start | bytes 638984 | tf_op jit(solution)/shard_map/ppermute | solution.py:237
  104.6 0.5 collective-permute-start.31
  105.1 9.9 %collective-permute-done.22.refs_1_ = bf16[208,512]{1,0:T(8,128)(2,1)S(1)} collective-permute-done((bf16[208,512]{1,0:T(8,128)(2,1)S(1)}, bf16[208,512]{1,0:T(8,128)(2,1)S(1)}, u32[]{:S(2)}, u32[]{:S(2)}) %collective-permute-start.22) | collective-permute-done | bytes 213024 | tf_op jit(solution)/shard_map/ppermute | solution.py:237
  115.1 0.7 collective-permute-start.23
  115.7 0.5 collective-permute-start.29
  116.2 6.5 %collective-permute-done.23.refs_2_ = bf16[208,512]{1,0:T(8,128)(2,1)S(1)} collective-permute-done((bf16[208,512]{1,0:T(8,128)(2,1)S(1)}, bf16[208,512]{1,0:T(8,128)(2,1)S(1)}, u32[]{:S(2)}, u32[]{:S(2)}) %collective-permute-start.23) | collective-permute-done | bytes 213024 | tf_op jit(solution)/shard_map/ppermute | solution.py:237
  122.7 0.5 collective-permute-start.25
  123.2 0.1 collective-permute-start.26
  123.3 1.9 %place.3.refs_4_ = bf16[1664,1408]{1,0:T(8,128)(2,1)} custom-call(bf16[208,512]{1,0:T(8,128)(2,1)S(1)} %pad_maximum_fusion.2.refs_0_, bf16[208,896]{1,0:T(8,128)(2,1)S(1)} %pad_maximum_fusion.1.refs_1_, bf16[208,512]{1,0:T(8,128)(2,1)S(1)} %collective-permute-done.33.refs_2_, bf16[208,896]{1,0:T(8,128)(2,1)S(1)} %collective-permute-done.34.refs_3_), custom_call_target="tpu_custom_call" | custom-call | tf_op jit(solution)/shard_map/place/pallas_call | solution.py:193
  125.2 1.8 %place.4.refs_8_ = bf16[1664,1408]{1,0:T(8,128)(2,1)} custom-call(bf16[208,896]{1,0:T(8,128)(2,1)S(1)} %collective-permute-done.27.refs_0_, bf16[208,896]{1,0:T(8,128)(2,1)S(1)} %collective-permute-done.30.refs_1_, bf16[208,896]{1,0:T(8,128)(2,1)S(1)} %collective-permute-done.31.refs_2_, ...), custom_call_target="tpu_custom_call", output_to_operand_aliasing={{}: (4, {})} | custom-call | tf_op jit(solution)/shard_map/place/pallas_call | solution.py:193
  127.1 3.4 %place.5 = bf16[1664,1408]{1,0:T(8,128)(2,1)} custom-call(bf16[208,512]{1,0:T(8,128)(2,1)S(1)} %collective-permute-done.21.refs_0_, bf16[208,512]{1,0:T(8,128)(2,1)S(1)} %collective-permute-done.22.refs_1_, bf16[208,512]{1,0:T(8,128)(2,1)S(1)} %collective-permute-done.23.refs_2_, ...), custom_call_target="tpu_custom_call", output_to_operand_aliasing={{}: (8, {})} | custom-call | tf_op jit(solution)/shard_map/place/pallas_call | solution.py:193
  (36 shorter events, 0.3 us)
Async XLA Ops:
  19.4 10.1 %copy-start.2 = (bf16[52,1408]{1,0:T(8,128)(2,1)S(1)}, bf16[52,1408]{1,0:T(8,128)(2,1)}, u32[]{:S(2)}) copy-start(bf16[52,1408]{1,0:T(8,128)(2,1)} %param.7) | copy-start | bytes 439300
  19.4 3.7 %collective-permute-start.4 = (bf16[832,896]{1,0:T(8,128)(2,1)}, bf16[832,896]{1,0:T(8,128)(2,1)S(1)}, u32[]{:S(2)}, u32[]{:S(2)}) collective-permute-start(bf16[832,896]{1,0:T(8,128)(2,1)} %get-tuple-element.31), channel_id=1, source_target_pairs={{0,1},{1,0},{2,3},{3,2},{4,5},{5,4},{6,7},{7,6},{8,9},{9,8},{10,11... | collective-permute-start | bytes 4472840 | tf_op jit(solution)/shard_map/ppermute | solution.py:237
  19.9 11.2 %collective-permute-start = (bf16[832,512]{1,0:T(8,128)(2,1)}, bf16[832,512]{1,0:T(8,128)(2,1)}, u32[]{:S(2)}, u32[]{:S(2)}) collective-permute-start(bf16[832,512]{1,0:T(8,128)(2,1)} %get-tuple-element.29), channel_id=1, source_target_pairs={{0,1},{1,0},{2,3},{3,2},{4,5},{5,4},{6,7},{7,6},{8,9},{9,8},{10,11... | collective-permute-start | bytes 2555912 | tf_op jit(solution)/shard_map/ppermute | solution.py:237
  23.1 1.1 copy-start.1
  25.7 15.7 %copy-start = (f32[832,896]{1,0:T(8,128)S(1)}, f32[832,896]{1,0:T(8,128)}, u32[]{:S(2)}) copy-start(f32[832,896]{1,0:T(8,128)} %get-tuple-element.30) | copy-start | bytes 8945668
  26.7 13.4 %collective-permute-start.5 = (bf16[416,896]{1,0:T(8,128)(2,1)}, bf16[416,896]{1,0:T(8,128)(2,1)}, u32[]{:S(2)}, u32[]{:S(2)}) collective-permute-start(bf16[416,896]{1,0:T(8,128)(2,1)} %pad_maximum_fusion), channel_id=1, source_target_pairs={{0,2},{1,5},{2,0},{3,7},{4,6},{5,1},{6,4},{7,3},{8,10},{9,13},{10,... | collective-permute-start | bytes 2236424 | tf_op jit(solution)/shard_map/ppermute | solution.py:273
  29.5 19.3 %collective-permute-start.11 = (bf16[52,896]{1,0:T(8,128)(2,1)S(1)}, bf16[52,896]{1,0:T(8,128)(2,1)S(1)}, u32[]{:S(2)}, u32[]{:S(2)}) collective-permute-start(bf16[52,896]{1,0:T(8,128)(2,1)S(1)} %slice.39), channel_id=1, source_target_pairs={{0,0},{1,8},{2,16},{3,24},{4,2},{5,10},{6,18},{7,26},{8,4},{9,12},... | collective-permute-start | bytes 279560 | tf_op jit(solution)/shard_map/ppermute | solution.py:353
  30.2 12.5 %collective-permute-start.10 = (bf16[52,512]{1,0:T(8,128)(2,1)S(1)}, bf16[52,512]{1,0:T(8,128)(2,1)S(1)}, u32[]{:S(2)}, u32[]{:S(2)}) collective-permute-start(bf16[52,512]{1,0:T(8,128)(2,1)S(1)} %slice.38), channel_id=1, source_target_pairs={{0,0},{1,2},{2,4},{3,6},{4,8},{5,10},{6,12},{7,14},{8,16},{9,18},{... | collective-permute-start | bytes 159752 | tf_op jit(solution)/shard_map/ppermute | solution.py:352
  32.8 16.1 %collective-permute-start.1 = (bf16[208,512]{1,0:T(8,128)(2,1)S(1)}, bf16[208,512]{1,0:T(8,128)(2,1)S(1)}, u32[]{:S(2)}, u32[]{:S(2)}) collective-permute-start(bf16[208,512]{1,0:T(8,128)(2,1)S(1)} %get-tuple-element.49), channel_id=1, source_target_pairs={{0,24},{1,25},{2,26},{3,27},{4,28},{5,29},{6,30},{7,31},{8,16},{9,... | collective-permute-start | bytes 638984 | tf_op jit(solution)/shard_map/ppermute | solution.py:237
  39.1 19.8 %collective-permute-start.2 = (bf16[208,512]{1,0:T(8,128)(2,1)S(1)}, bf16[208,512]{1,0:T(8,128)(2,1)S(1)}, u32[]{:S(2)}, u32[]{:S(2)}) collective-permute-start(bf16[208,512]{1,0:T(8,128)(2,1)S(1)} %get-tuple-element.51), channel_id=1, source_target_pairs={{0,16},{1,17},{2,18},{3,19},{4,20},{5,21},{6,22},{7,23},{8,24},{9,... | collective-permute-start | bytes 638984 | tf_op jit(solution)/shard_map/ppermute | solution.py:237
  40.0 18.9 %collective-permute-start.3 = (bf16[208,512]{1,0:T(8,128)(2,1)S(1)}, bf16[208,512]{1,0:T(8,128)(2,1)S(1)}, u32[]{:S(2)}, u32[]{:S(2)}) collective-permute-start(bf16[208,512]{1,0:T(8,128)(2,1)S(1)} %get-tuple-element.50), channel_id=1, source_target_pairs={{0,8},{1,9},{2,10},{3,11},{4,12},{5,13},{6,14},{7,15},{8,0},{9,1},... | collective-permute-start | bytes 638984 | tf_op jit(solution)/shard_map/ppermute | solution.py:237
  42.7 17.4 %collective-permute-start.6 = (bf16[208,896]{1,0:T(8,128)(2,1)S(1)}, bf16[208,896]{1,0:T(8,128)(2,1)S(1)}, u32[]{:S(2)}, u32[]{:S(2)}) collective-permute-start(bf16[208,896]{1,0:T(8,128)(2,1)S(1)} %add_convert_fusion), channel_id=1, source_target_pairs={{0,4},{1,3},{2,6},{3,1},{4,0},{5,7},{6,2},{7,5},{8,12},{9,11},{10,... | collective-permute-start | bytes 1118216 | tf_op jit(solution)/shard_map/ppermute | solution.py:276
  61.5 7.2 %collective-permute-start.7 = (bf16[56,512]{1,0:T(8,128)(2,1)S(1)}, bf16[56,512]{1,0:T(8,128)(2,1)S(1)}, u32[]{:S(2)}, u32[]{:S(2)}) collective-permute-start(bf16[56,512]{1,0:T(8,128)(2,1)S(1)} %get-tuple-element.55), channel_id=1, source_target_pairs={{0,6},{1,7},{2,4},{3,5},{4,2},{5,3},{6,0},{7,1},{8,14},{9,15},{10,... | collective-permute-start | bytes 172040 | tf_op jit(solution)/shard_map/ppermute | solution.py:237
  64.1 6.9 %collective-permute-start.8 = (bf16[56,512]{1,0:T(8,128)(2,1)S(1)}, bf16[56,512]{1,0:T(8,128)(2,1)S(1)}, u32[]{:S(2)}, u32[]{:S(2)}) collective-permute-start(bf16[56,512]{1,0:T(8,128)(2,1)S(1)} %get-tuple-element.57), channel_id=1, source_target_pairs={{0,4},{1,5},{2,6},{3,7},{4,0},{5,1},{6,2},{7,3},{8,12},{9,13},{10,... | collective-permute-start | bytes 172040 | tf_op jit(solution)/shard_map/ppermute | solution.py:237
  66.5 4.5 %collective-permute-start.9 = (bf16[56,512]{1,0:T(8,128)(2,1)S(1)}, bf16[56,512]{1,0:T(8,128)(2,1)S(1)}, u32[]{:S(2)}, u32[]{:S(2)}) collective-permute-start(bf16[56,512]{1,0:T(8,128)(2,1)S(1)} %get-tuple-element.56), channel_id=1, source_target_pairs={{0,2},{1,3},{2,0},{3,1},{4,6},{5,7},{6,4},{7,5},{8,10},{9,11},{10,... | collective-permute-start | bytes 172040 | tf_op jit(solution)/shard_map/ppermute | solution.py:237
  66.5 7.6 %collective-permute-start.12 = (bf16[56,896]{1,0:T(8,128)(2,1)S(1)}, bf16[56,896]{1,0:T(8,128)(2,1)S(1)}, u32[]{:S(2)}, u32[]{:S(2)}) collective-permute-start(bf16[56,896]{1,0:T(8,128)(2,1)S(1)} %get-tuple-element.52), channel_id=1, source_target_pairs={{0,24},{1,25},{2,26},{3,27},{4,28},{5,29},{6,30},{7,31},{8,16},{9,... | collective-permute-start | bytes 301064 | tf_op jit(solution)/shard_map/ppermute | solution.py:237
  68.6 8.0 %collective-permute-start.13 = (bf16[56,896]{1,0:T(8,128)(2,1)S(1)}, bf16[56,896]{1,0:T(8,128)(2,1)S(1)}, u32[]{:S(2)}, u32[]{:S(2)}) collective-permute-start(bf16[56,896]{1,0:T(8,128)(2,1)S(1)} %get-tuple-element.54), channel_id=1, source_target_pairs={{0,16},{1,17},{2,18},{3,19},{4,20},{5,21},{6,22},{7,23},{8,24},{9,... | collective-permute-start | bytes 301064 | tf_op jit(solution)/shard_map/ppermute | solution.py:237
  68.6 8.0 %collective-permute-start.14 = (bf16[56,896]{1,0:T(8,128)(2,1)S(1)}, bf16[56,896]{1,0:T(8,128)(2,1)S(1)}, u32[]{:S(2)}, u32[]{:S(2)}) collective-permute-start(bf16[56,896]{1,0:T(8,128)(2,1)S(1)} %get-tuple-element.53), channel_id=1, source_target_pairs={{0,8},{1,9},{2,10},{3,11},{4,12},{5,13},{6,14},{7,15},{8,0},{9,1},... | collective-permute-start | bytes 301064 | tf_op jit(solution)/shard_map/ppermute | solution.py:237
  77.6 6.5 %collective-permute-start.15 = (bf16[56,512]{1,0:T(8,128)(2,1)S(1)}, bf16[56,512]{1,0:T(8,128)(2,1)S(1)}, u32[]{:S(2)}, u32[]{:S(2)}) collective-permute-start(bf16[56,512]{1,0:T(8,128)(2,1)S(1)} %subtract_convert_fusion.1), channel_id=1, source_target_pairs={{0,2},{1,3},{2,0},{3,1},{4,6},{5,7},{6,4},{7,5},{8,10},{9,11},{10,... | collective-permute-start | bytes 172040 | tf_op jit(solution)/shard_map/ppermute | solution.py:237
  79.4 9.8 %collective-permute-start.18 = (bf16[56,896]{1,0:T(8,128)(2,1)S(1)}, bf16[56,896]{1,0:T(8,128)(2,1)S(1)}, u32[]{:S(2)}, u32[]{:S(2)}) collective-permute-start(bf16[56,896]{1,0:T(8,128)(2,1)S(1)} %subtract_convert_fusion), channel_id=1, source_target_pairs={{0,8},{1,9},{2,10},{3,11},{4,12},{5,13},{6,14},{7,15},{8,0},{9,1},... | collective-permute-start | bytes 301064 | tf_op jit(solution)/shard_map/ppermute | solution.py:237
  80.1 10.2 %collective-permute-start.19 = (bf16[56,896]{1,0:T(8,128)(2,1)S(1)}, bf16[56,896]{1,0:T(8,128)(2,1)S(1)}, u32[]{:S(2)}, u32[]{:S(2)}) collective-permute-start(bf16[56,896]{1,0:T(8,128)(2,1)S(1)} %subtract_convert_fusion), channel_id=1, source_target_pairs={{0,16},{1,17},{2,18},{3,19},{4,20},{5,21},{6,22},{7,23},{8,24},{9,... | collective-permute-start | bytes 301064 | tf_op jit(solution)/shard_map/ppermute | solution.py:237
  82.5 7.8 %collective-permute-start.20 = (bf16[56,896]{1,0:T(8,128)(2,1)S(1)}, bf16[56,896]{1,0:T(8,128)(2,1)S(1)}, u32[]{:S(2)}, u32[]{:S(2)}) collective-permute-start(bf16[56,896]{1,0:T(8,128)(2,1)S(1)} %subtract_convert_fusion), channel_id=1, source_target_pairs={{0,24},{1,25},{2,26},{3,27},{4,28},{5,29},{6,30},{7,31},{8,16},{9,... | collective-permute-start | bytes 301064 | tf_op jit(solution)/shard_map/ppermute | solution.py:237
  83.8 4.2 %collective-permute-start.16 = (bf16[56,512]{1,0:T(8,128)(2,1)S(1)}, bf16[56,512]{1,0:T(8,128)(2,1)S(1)}, u32[]{:S(2)}, u32[]{:S(2)}) collective-permute-start(bf16[56,512]{1,0:T(8,128)(2,1)S(1)} %subtract_convert_fusion.1), channel_id=1, source_target_pairs={{0,4},{1,5},{2,6},{3,7},{4,0},{5,1},{6,2},{7,3},{8,12},{9,13},{10,... | collective-permute-start | bytes 172040 | tf_op jit(solution)/shard_map/ppermute | solution.py:237
  84.1 5.1 %collective-permute-start.17 = (bf16[56,512]{1,0:T(8,128)(2,1)S(1)}, bf16[56,512]{1,0:T(8,128)(2,1)S(1)}, u32[]{:S(2)}, u32[]{:S(2)}) collective-permute-start(bf16[56,512]{1,0:T(8,128)(2,1)S(1)} %subtract_convert_fusion.1), channel_id=1, source_target_pairs={{0,6},{1,7},{2,4},{3,5},{4,2},{5,3},{6,0},{7,1},{8,14},{9,15},{10,... | collective-permute-start | bytes 172040 | tf_op jit(solution)/shard_map/ppermute | solution.py:237
  90.6 10.1 %collective-permute-start.27 = (bf16[208,896]{1,0:T(8,128)(2,1)S(1)}, bf16[208,896]{1,0:T(8,128)(2,1)S(1)}, u32[]{:S(2)}, u32[]{:S(2)}) collective-permute-start(bf16[208,896]{1,0:T(8,128)(2,1)S(1)} %pad_maximum_fusion.1.refs_1_), channel_id=1, source_target_pairs={{0,4},{1,3},{2,6},{3,1},{4,0},{5,7},{6,2},{7,5},{8,12},{9,11},{10,... | collective-permute-start | bytes 1118216 | tf_op jit(solution)/shard_map/ppermute | solution.py:282
  91.4 13.2 %collective-permute-start.33 = (bf16[208,512]{1,0:T(8,128)(2,1)S(1)}, bf16[208,512]{1,0:T(8,128)(2,1)S(1)}, u32[]{:S(2)}, u32[]{:S(2)}) collective-permute-start(bf16[208,512]{1,0:T(8,128)(2,1)S(1)} %pad_maximum_fusion.2.refs_0_), channel_id=1, source_target_pairs={{0,1},{1,0},{2,3},{3,2},{4,5},{5,4},{6,7},{7,6},{8,9},{9,8},{10,11... | collective-permute-start | bytes 638984 | tf_op jit(solution)/shard_map/ppermute | solution.py:237
  91.5 13.1 %collective-permute-start.21 = (bf16[208,512]{1,0:T(8,128)(2,1)S(1)}, bf16[208,512]{1,0:T(8,128)(2,1)S(1)}, u32[]{:S(2)}, u32[]{:S(2)}) collective-permute-start(bf16[208,512]{1,0:T(8,128)(2,1)S(1)} %pad_maximum_fusion.2.refs_0_), channel_id=1, source_target_pairs={{0,8},{1,9},{2,10},{3,11},{4,12},{5,13},{6,14},{7,15},{8,0},{9,1},... | collective-permute-start | bytes 638984 | tf_op jit(solution)/shard_map/ppermute | solution.py:237
  92.9 22.8 %collective-permute-start.30 = (bf16[208,896]{1,0:T(8,128)(2,1)S(1)}, bf16[208,896]{1,0:T(8,128)(2,1)S(1)}, u32[]{:S(2)}, u32[]{:S(2)}) collective-permute-start(bf16[208,896]{1,0:T(8,128)(2,1)S(1)} %pad_maximum_fusion.1.refs_1_), channel_id=1, source_target_pairs={{0,2},{1,5},{2,0},{3,7},{4,6},{5,1},{6,4},{7,3},{8,10},{9,13},{10,... | collective-permute-start | bytes 1118216 | tf_op jit(solution)/shard_map/ppermute | solution.py:283
  100.7 15.1 %collective-permute-start.28 = (bf16[208,896]{1,0:T(8,128)(2,1)S(1)}, bf16[208,896]{1,0:T(8,128)(2,1)S(1)}, u32[]{:S(2)}, u32[]{:S(2)}) collective-permute-start(bf16[208,896]{1,0:T(8,128)(2,1)S(1)} %collective-permute-done.27.refs_0_), channel_id=1, source_target_pairs={{0,2},{1,5},{2,0},{3,7},{4,6},{5,1},{6,4},{7,3},{8,10},{9,13},{10,... | collective-permute-start | bytes 1118216 | tf_op jit(solution)/shard_map/ppermute | solution.py:284
  100.7 14.4 %collective-permute-start.22 = (bf16[208,512]{1,0:T(8,128)(2,1)S(1)}, bf16[208,512]{1,0:T(8,128)(2,1)S(1)}, u32[]{:S(2)}, u32[]{:S(2)}) collective-permute-start(bf16[208,512]{1,0:T(8,128)(2,1)S(1)} %pad_maximum_fusion.2.refs_0_), channel_id=1, source_target_pairs={{0,16},{1,17},{2,18},{3,19},{4,20},{5,21},{6,22},{7,23},{8,24},{9,... | collective-permute-start | bytes 638984 | tf_op jit(solution)/shard_map/ppermute | solution.py:237
  104.6 18.1 %collective-permute-start.34 = (bf16[208,896]{1,0:T(8,128)(2,1)S(1)}, bf16[208,896]{1,0:T(8,128)(2,1)S(1)}, u32[]{:S(2)}, u32[]{:S(2)}) collective-permute-start(bf16[208,896]{1,0:T(8,128)(2,1)S(1)} %pad_maximum_fusion.1.refs_1_), channel_id=1, source_target_pairs={{0,1},{1,0},{2,3},{3,2},{4,5},{5,4},{6,7},{7,6},{8,9},{9,8},{10,11... | collective-permute-start | bytes 1118216 | tf_op jit(solution)/shard_map/ppermute | solution.py:237
  104.6 18.6 %collective-permute-start.31 = (bf16[208,896]{1,0:T(8,128)(2,1)S(1)}, bf16[208,896]{1,0:T(8,128)(2,1)S(1)}, u32[]{:S(2)}, u32[]{:S(2)}) collective-permute-start(bf16[208,896]{1,0:T(8,128)(2,1)S(1)} %collective-permute-done.27.refs_0_), channel_id=1, source_target_pairs={{0,1},{1,0},{2,3},{3,2},{4,5},{5,4},{6,7},{7,6},{8,9},{9,8},{10,11... | collective-permute-start | bytes 1118216 | tf_op jit(solution)/shard_map/ppermute | solution.py:237
  115.1 7.6 %collective-permute-start.23 = (bf16[208,512]{1,0:T(8,128)(2,1)S(1)}, bf16[208,512]{1,0:T(8,128)(2,1)S(1)}, u32[]{:S(2)}, u32[]{:S(2)}) collective-permute-start(bf16[208,512]{1,0:T(8,128)(2,1)S(1)} %pad_maximum_fusion.2.refs_0_), channel_id=1, source_target_pairs={{0,24},{1,25},{2,26},{3,27},{4,28},{5,29},{6,30},{7,31},{8,16},{9,... | collective-permute-start | bytes 638984 | tf_op jit(solution)/shard_map/ppermute | solution.py:237
  115.7 9.5 %collective-permute-start.32 = (bf16[208,896]{1,0:T(8,128)(2,1)S(1)}, bf16[208,896]{1,0:T(8,128)(2,1)S(1)}, u32[]{:S(2)}, u32[]{:S(2)}) collective-permute-start(bf16[208,896]{1,0:T(8,128)(2,1)S(1)} %collective-permute-done.30.refs_1_), channel_id=1, source_target_pairs={{0,1},{1,0},{2,3},{3,2},{4,5},{5,4},{6,7},{7,6},{8,9},{9,8},{10,11... | collective-permute-start | bytes 1118216 | tf_op jit(solution)/shard_map/ppermute | solution.py:237
  115.7 11.4 %collective-permute-start.29 = (bf16[208,896]{1,0:T(8,128)(2,1)S(1)}, bf16[208,896]{1,0:T(8,128)(2,1)S(1)}, u32[]{:S(2)}, u32[]{:S(2)}) collective-permute-start(bf16[208,896]{1,0:T(8,128)(2,1)S(1)} %collective-permute-done.28.refs_6_), channel_id=1, source_target_pairs={{0,1},{1,0},{2,3},{3,2},{4,5},{5,4},{6,7},{7,6},{8,9},{9,8},{10,11... | collective-permute-start | bytes 1118216 | tf_op jit(solution)/shard_map/ppermute | solution.py:237
  122.7 4.4 %collective-permute-start.24 = (bf16[208,512]{1,0:T(8,128)(2,1)S(1)}, bf16[208,512]{1,0:T(8,128)(2,1)S(1)}, u32[]{:S(2)}, u32[]{:S(2)}) collective-permute-start(bf16[208,512]{1,0:T(8,128)(2,1)S(1)} %collective-permute-done.21.refs_0_), channel_id=1, source_target_pairs={{0,1},{1,0},{2,3},{3,2},{4,5},{5,4},{6,7},{7,6},{8,9},{9,8},{10,11... | collective-permute-start | bytes 638984 | tf_op jit(solution)/shard_map/ppermute | solution.py:237
  122.7 4.4 %collective-permute-start.25 = (bf16[208,512]{1,0:T(8,128)(2,1)S(1)}, bf16[208,512]{1,0:T(8,128)(2,1)S(1)}, u32[]{:S(2)}, u32[]{:S(2)}) collective-permute-start(bf16[208,512]{1,0:T(8,128)(2,1)S(1)} %collective-permute-done.22.refs_1_), channel_id=1, source_target_pairs={{0,1},{1,0},{2,3},{3,2},{4,5},{5,4},{6,7},{7,6},{8,9},{9,8},{10,11... | collective-permute-start | bytes 638984 | tf_op jit(solution)/shard_map/ppermute | solution.py:237
  123.2 3.9 %collective-permute-start.26 = (bf16[208,512]{1,0:T(8,128)(2,1)S(1)}, bf16[208,512]{1,0:T(8,128)(2,1)S(1)}, u32[]{:S(2)}, u32[]{:S(2)}) collective-permute-start(bf16[208,512]{1,0:T(8,128)(2,1)S(1)} %collective-permute-done.23.refs_2_), channel_id=1, source_target_pairs={{0,1},{1,0},{2,3},{3,2},{4,5},{5,4},{6,7},{7,6},{8,9},{9,8},{10,11... | collective-permute-start | bytes 638984 | tf_op jit(solution)/shard_map/ppermute | solution.py:237

commit v5 on v4

--- a/solution.py
+++ b/solution.py
@@ -223,7 +223,7 @@
 
 def narrow_share(width):
     tiles = width // LANE
-    return max(1, round(tiles * 4 / 11)) * LANE
+    return max(1, round(tiles * 3 / 11)) * LANE
 
 
 class Group:
@@ -401,21 +401,26 @@
         (_, b), (_, d) = rows_in(0)(), rows_in(1)()
         return b[1:3] + d[1:3]
 
-    def late_rows():
-        (a, b), (c, d) = rows_in(0)(), rows_in(1)()
-        return a[1:] + c[1:] + [b[3], d[3]]
+    def narrow_rows_late():
+        (a, _), (c, _) = rows_in(0)(), rows_in(1)()
+        return a[1:] + c[1:]
+
+    def last_rows():
+        (_, b), (_, d) = rows_in(0)(), rows_in(1)()
+        return [b[3], d[3]]
 
     out = place(near, near_rows, [wide, 0] * 2, weight.shape)
 
     blocks = layer.spread(layer_block)[1:]
     side_blocks = two_way_spread(side_block)
-    side_blocks += [core.swap(b, 1) for b in side_blocks]
+    last_far = core.swap(side_blocks[2], 1)
+    side_blocks += [core.swap(b, 1) for b in side_blocks[:2]] + [last_far]
     early = [side_blocks[i] for i in (0, 1, 3, 4)]
     out = place(early, early_rows, [0] * 4, weight.shape, out)
     blocks += [core.swap(b, 1) for b in blocks]
-    columns = [wide] * len(blocks) + [0] * 2
-    blocks += [side_blocks[2], side_blocks[5]]
-    return place(blocks, late_rows, columns, weight.shape, out)
+    out = place(blocks, narrow_rows_late, [wide] * len(blocks), weight.shape, out)
+    last = [side_blocks[2], side_blocks[5]]
+    return place(last, last_rows, [0] * 2, weight.shape, out)
 
 
 def by_columns(features, labels, weight, noise):

time: 131 us -> 138 us (1.053)
  waiting for transfers between devices: 45 us -> 51.6 us
  starting transfers between devices: 47 us -> 43.4 us
  local copies, waits for them, and re-layouts: 1.27 us -> 3.05 us
    ppermute x28, starting transfers between devices: 34.4 us -> 29 us  [swap(): return lax.ppermute(x, 'ex', self.pairs[d])]
    ppermute x1, waiting for transfers between devices: 6.12 us -> 10.6 us  [two_way_spread(): from_second = lax.ppermute(x, 'ex', second)]
    ppermute x28, waiting for transfers between devices: 38.9 us -> 40.6 us  [swap(): return lax.ppermute(x, 'ex', self.pairs[d])]
    slice x1, local copies, waits for them, and re-layouts: 0.01 us -> 1.55 us  [by_rows(): noise_w = lax.ppermute(noise[:, :wide], 'ex', to_wide)]
    slice x1, local copies, waits for them, and re-layouts: 0.01 us -> 1.39 us  [by_rows(): noise_n = lax.ppermute(noise[:, wide:], 'ex', to_narrow)]
    ppermute x1, starting transfers between devices: 0.66 us -> 2.04 us  [by_rows(): noise_n = lax.ppermute(noise[:, wide:], 'ex', to_narrow)]
    pallas_call x3 -> x4, Pallas kernels: 7.16 us -> 7.79 us  [place(): pl.pallas_call(kernel, in_specs=[anywhere] * (count + len(extra)), out_sp...]
  transfers between devices with their start and end apart: 35 -> 35, of which waited for: 10 -> 11; matrix products, arithmetic and copies ran while one was open for 6% -> 6% of each run, Pallas kernels for 3% -> 5%
where the time goes in v5:
time: 138 us; the launch traced here: 137 us
  waiting for transfers between devices  51.6 us (37%)
  starting transfers between devices  43.4 us (31%)
  Pallas kernels  27.2 us (20%)
  other arithmetic  11.3 us (8%)
  local copies, waits for them, and re-layouts  3.05 us (2%)
    ppermute x28, waiting for transfers between devices, swap(): return lax.ppermute(x, 'ex', self.pairs[d])  40.6 us
    ppermute x28, starting transfers between devices, swap(): return lax.ppermute(x, 'ex', self.pairs[d])  29 us
    pallas_call x1, Pallas kernels, halves(): pl.pallas_call(functools.partial(head_kernel, shape), in_specs=[anywhere,...  19.4 us
    ppermute x1, waiting for transfers between devices, two_way_spread(): from_second = lax.ppermute(x, 'ex', second)  10.6 us
    pallas_call x4, Pallas kernels, place(): pl.pallas_call(kernel, in_specs=[anywhere] * (count + len(extra)), out_sp...  7.79 us
    ppermute x1, starting transfers between devices, two_way_sum(): last = lax.ppermute(passed, 'ex', second)  5.45 us
    ppermute x1, starting transfers between devices, two_way_sum(): got = lax.ppermute(sent, 'ex', first)  2.85 us
  transfers between devices with their start and end apart: 35, of which 11 were waited for; matrix products, arithmetic and copies ran while one was open for 6% of the time, Pallas kernels for 5%

profile of v5, /device:TPU:0, one launch (start us, length us, event | category | flops | bytes accessed | tf_op | source)
XLA Modules:
  0.0 137.0 jit_solution(12121571326875886562)
XLA Ops:
  0.0 19.4 %halves.1 = (bf16[832,384]{1,0:T(8,128)(2,1)}, bf16[832,1024]{1,0:T(8,128)(2,1)}, f32[832,384]{1,0:T(8,128)}, f32[832,1024]{1,0:T(8,128)}) custom-call(bf16[1024,1664]{1,0:T(8,128)(2,1)} %feat_ref.1, s32[8,128]{1,0:T(8,128)} %bitcast.1, bf16[1664,1408]{1,0:T(8,128)(2,1)} %weight_ref.1), custom_call_target="tpu_custom_call" | custom-call | flops 9596567552 | bytes 15122432 | tf_op jit(solution)/shard_map/halves/pallas_call | solution.py:142
  19.4 0.6 collective-permute-start.4
  19.9 3.6 %collective-permute-done.4 = bf16[832,1024]{1,0:T(8,128)(2,1)} collective-permute-done((bf16[832,1024]{1,0:T(8,128)(2,1)}, bf16[832,1024]{1,0:T(8,128)(2,1)}, u32[]{:S(2)}, u32[]{:S(2)}) %collective-permute-start.4) | collective-permute-done | bytes 1703968 | tf_op jit(solution)/shard_map/ppermute | solution.py:237
  23.5 1.9 %add_convert_fusion.2 = (bf16[208,1024]{1,0:T(8,128)(2,1)S(1)}, bf16[208,1024]{1,0:T(8,128)(2,1)S(1)}) fusion(f32[832,1024]{1,0:T(8,128)} %get-tuple-element.30, s32[]{:T(128)S(6)} %select_n.297, bf16[832,1024]{1,0:T(8,128)(2,1)} %collective-permute-done.4, s32[]{:T(128)S(6)} %select_n.299), kind=kLoop, calls=%fused_computation.4 | loop fusion | flops 1277952 | bytes 3407880 | tf_op jit(solution)/shard_map/convert_element_type | solution.py:272
  25.4 1.0 pad_maximum_fusion
  26.4 2.8 %collective-permute-start.5 = (bf16[416,1024]{1,0:T(8,128)(2,1)}, bf16[416,1024]{1,0:T(8,128)(2,1)}, u32[]{:S(2)}, u32[]{:S(2)}) collective-permute-start(bf16[416,1024]{1,0:T(8,128)(2,1)} %pad_maximum_fusion), channel_id=1, source_target_pairs={{0,2},{1,5},{2,0},{3,7},{4,6},{5,1},{6,4},{7,3},{8,10},{9,13},{10,... | collective-permute-start | bytes 2555912 | tf_op jit(solution)/shard_map/ppermute | solution.py:273
  29.3 1.5 %slice.39 = bf16[52,1024]{1,0:T(8,128)(2,1)} slice(bf16[52,1408]{1,0:T(8,128)(2,1)} %param.7), slice={[0:52], [0:1024]} | slice | bytes 212992 | tf_op jit(solution)/shard_map/slice | solution.py:353
  30.8 1.5 %collective-permute-start.11 = (bf16[52,1024]{1,0:T(8,128)(2,1)}, bf16[52,1024]{1,0:T(8,128)(2,1)S(1)}, u32[]{:S(2)}, u32[]{:S(2)}) collective-permute-start(bf16[52,1024]{1,0:T(8,128)(2,1)} %slice.39), channel_id=1, source_target_pairs={{0,0},{1,8},{2,16},{3,24},{4,2},{5,10},{6,18},{7,26},{8,4},{9,12},... | collective-permute-start | bytes 319496 | tf_op jit(solution)/shard_map/ppermute | solution.py:353
  32.4 1.4 %slice.38 = bf16[52,384]{1,0:T(8,128)(2,1)} slice(bf16[52,1408]{1,0:T(8,128)(2,1)} %param.7), slice={[0:52], [1024:1408]} | slice | bytes 79872 | tf_op jit(solution)/shard_map/slice | solution.py:352
  33.7 2.0 %collective-permute-start.10 = (bf16[52,384]{1,0:T(8,128)(2,1)}, bf16[52,384]{1,0:T(8,128)(2,1)}, u32[]{:S(2)}, u32[]{:S(2)}) collective-permute-start(bf16[52,384]{1,0:T(8,128)(2,1)} %slice.38), channel_id=1, source_target_pairs={{0,0},{1,2},{2,4},{3,6},{4,8},{5,10},{6,12},{7,14},{8,16},{9,18},{... | collective-permute-start | bytes 119816 | tf_op jit(solution)/shard_map/ppermute | solution.py:352
  35.8 0.0 collective-permute-done
  35.8 1.4 %add_convert_fusion.5 = (bf16[208,384]{1,0:T(8,128)(2,1)S(1)}, bf16[208,384]{1,0:T(8,128)(2,1)S(1)}, bf16[208,384]{1,0:T(8,128)(2,1)S(1)}) fusion(f32[832,384]{1,0:T(8,128)} %get-tuple-element.28, s32[]{:T(128)S(6)} %select_n.293, bf16[832,384]{1,0:T(8,128)(2,1)} %collective-permute-done, s32[]{:T(128)S(6)} %select_n.295, s32[]{:T(128)S(6)} %select_n.294), kind=kLoop, calls=%fused_computation.9 | loop fusion | flops 718848 | bytes 1916940 | tf_op jit(solution)/shard_map/convert_element_type | solution.py:242
  37.2 5.5 %collective-permute-start.1 = (bf16[208,384]{1,0:T(8,128)(2,1)S(1)}, bf16[208,384]{1,0:T(8,128)(2,1)S(1)}, u32[]{:S(2)}, u32[]{:S(2)}) collective-permute-start(bf16[208,384]{1,0:T(8,128)(2,1)S(1)} %get-tuple-element.49), channel_id=1, source_target_pairs={{0,24},{1,25},{2,26},{3,27},{4,28},{5,29},{6,30},{7,31},{8,16},{9,... | collective-permute-start | bytes 479240 | tf_op jit(solution)/shard_map/ppermute | solution.py:237
  42.7 0.2 collective-permute-start.2
  42.8 0.5 collective-permute-start.3
  43.3 1.3 add_convert_fusion
  44.7 5.5 %collective-permute-start.6 = (bf16[208,1024]{1,0:T(8,128)(2,1)S(1)}, bf16[208,1024]{1,0:T(8,128)(2,1)S(1)}, u32[]{:S(2)}, u32[]{:S(2)}) collective-permute-start(bf16[208,1024]{1,0:T(8,128)(2,1)S(1)} %add_convert_fusion), channel_id=1, source_target_pairs={{0,4},{1,3},{2,6},{3,1},{4,0},{5,7},{6,2},{7,5},{8,12},{9,11},{10,... | collective-permute-start | bytes 1277960 | tf_op jit(solution)/shard_map/ppermute | solution.py:276
  50.1 0.9 select_select_fusion.9
  51.0 0.1 select_select_fusion.4
  51.1 6.8 %collective-permute-done.2 = bf16[208,384]{1,0:T(8,128)(2,1)S(1)} collective-permute-done((bf16[208,384]{1,0:T(8,128)(2,1)S(1)}, bf16[208,384]{1,0:T(8,128)(2,1)S(1)}, u32[]{:S(2)}, u32[]{:S(2)}) %collective-permute-start.2) | collective-permute-done | bytes 159776 | tf_op jit(solution)/shard_map/ppermute | solution.py:237
  57.9 1.1 convert_add_fusion.1
  59.0 1.4 %convert_add_fusion = f32[208,1024]{1,0:T(8,128)S(1)} fusion(bf16[208,1024]{1,0:T(8,128)(2,1)S(1)} %collective-permute-done.6, f32[832,1024]{1,0:T(8,128)S(1)} %copy-done, s32[]{:T(128)S(6)} %select_n.296, bf16[416,1024]{1,0:T(8,128)(2,1)} %collective-permute-done.5, bf16[832,1024]{1,0:T(8,128)(2,1)} %collective-permute-done.4), kind=kLoop, calls=%fused_computation.1 | loop fusion | flops 1277952 | bytes 2981892 | tf_op jit(solution)/shard_map/add | solution.py:277
  60.5 2.0 %collective-permute-start.7 = (bf16[56,384]{1,0:T(8,128)(2,1)S(1)}, bf16[56,384]{1,0:T(8,128)(2,1)S(1)}, u32[]{:S(2)}, u32[]{:S(2)}) collective-permute-start(bf16[56,384]{1,0:T(8,128)(2,1)S(1)} %get-tuple-element.59), channel_id=1, source_target_pairs={{0,6},{1,7},{2,4},{3,5},{4,2},{5,3},{6,0},{7,1},{8,14},{9,15},{10,... | collective-permute-start | bytes 129032 | tf_op jit(solution)/shard_map/ppermute | solution.py:237
  62.5 2.1 %collective-permute-start.8 = (bf16[56,384]{1,0:T(8,128)(2,1)S(1)}, bf16[56,384]{1,0:T(8,128)(2,1)S(1)}, u32[]{:S(2)}, u32[]{:S(2)}) collective-permute-start(bf16[56,384]{1,0:T(8,128)(2,1)S(1)} %get-tuple-element.61), channel_id=1, source_target_pairs={{0,4},{1,5},{2,6},{3,7},{4,0},{5,1},{6,2},{7,3},{8,12},{9,13},{10,... | collective-permute-start | bytes 129032 | tf_op jit(solution)/shard_map/ppermute | solution.py:237
  64.6 0.7 collective-permute-start.9
  65.4 0.1 dynamic-slice_convert_fusion.2
  65.4 2.0 %collective-permute-start.12 = (bf16[56,1024]{1,0:T(8,128)(2,1)S(1)}, bf16[56,1024]{1,0:T(8,128)(2,1)S(1)}, u32[]{:S(2)}, u32[]{:S(2)}) collective-permute-start(bf16[56,1024]{1,0:T(8,128)(2,1)S(1)} %get-tuple-element.52), channel_id=1, source_target_pairs={{0,24},{1,25},{2,26},{3,27},{4,28},{5,29},{6,30},{7,31},{8,16},{9,... | collective-permute-start | bytes 344072 | tf_op jit(solution)/shard_map/ppermute | solution.py:237
  67.4 2.5 %collective-permute-start.14 = (bf16[56,1024]{1,0:T(8,128)(2,1)S(1)}, bf16[56,1024]{1,0:T(8,128)(2,1)S(1)}, u32[]{:S(2)}, u32[]{:S(2)}) collective-permute-start(bf16[56,1024]{1,0:T(8,128)(2,1)S(1)} %get-tuple-element.53), channel_id=1, source_target_pairs={{0,8},{1,9},{2,10},{3,11},{4,12},{5,13},{6,14},{7,15},{8,0},{9,1},... | collective-permute-start | bytes 344072 | tf_op jit(solution)/shard_map/ppermute | solution.py:237
  69.9 0.9 subtract_convert_fusion.1
  70.7 2.6 %collective-permute-done.12 = bf16[56,1024]{1,0:T(8,128)(2,1)S(1)} collective-permute-done((bf16[56,1024]{1,0:T(8,128)(2,1)S(1)}, bf16[56,1024]{1,0:T(8,128)(2,1)S(1)}, u32[]{:S(2)}, u32[]{:S(2)}) %collective-permute-start.12) | collective-permute-done | bytes 114720 | tf_op jit(solution)/shard_map/ppermute | solution.py:237
  73.3 3.5 %collective-permute-done.13 = bf16[56,1024]{1,0:T(8,128)(2,1)S(1)} collective-permute-done((bf16[56,1024]{1,0:T(8,128)(2,1)S(1)}, bf16[56,1024]{1,0:T(8,128)(2,1)S(1)}, u32[]{:S(2)}, u32[]{:S(2)}) %collective-permute-start.13) | collective-permute-done | bytes 114720 | tf_op jit(solution)/shard_map/ppermute | solution.py:237
  76.8 1.0 subtract_convert_fusion
  77.9 0.2 collective-permute-start.18
  78.1 2.3 %collective-permute-start.19 = (bf16[56,1024]{1,0:T(8,128)(2,1)S(1)}, bf16[56,1024]{1,0:T(8,128)(2,1)S(1)}, u32[]{:S(2)}, u32[]{:S(2)}) collective-permute-start(bf16[56,1024]{1,0:T(8,128)(2,1)S(1)} %subtract_convert_fusion), channel_id=1, source_target_pairs={{0,16},{1,17},{2,18},{3,19},{4,20},{5,21},{6,22},{7,23},{8,24},{9,... | collective-permute-start | bytes 344072 | tf_op jit(solution)/shard_map/ppermute | solution.py:237
  80.4 1.9 %collective-permute-start.20 = (bf16[56,1024]{1,0:T(8,128)(2,1)S(1)}, bf16[56,1024]{1,0:T(8,128)(2,1)S(1)}, u32[]{:S(2)}, u32[]{:S(2)}) collective-permute-start(bf16[56,1024]{1,0:T(8,128)(2,1)S(1)} %subtract_convert_fusion), channel_id=1, source_target_pairs={{0,24},{1,25},{2,26},{3,27},{4,28},{5,29},{6,30},{7,31},{8,16},{9,... | collective-permute-start | bytes 344072 | tf_op jit(solution)/shard_map/ppermute | solution.py:237
  82.3 1.4 %collective-permute-start.15 = (bf16[56,384]{1,0:T(8,128)(2,1)S(1)}, bf16[56,384]{1,0:T(8,128)(2,1)S(1)}, u32[]{:S(2)}, u32[]{:S(2)}) collective-permute-start(bf16[56,384]{1,0:T(8,128)(2,1)S(1)} %subtract_convert_fusion.1), channel_id=1, source_target_pairs={{0,2},{1,3},{2,0},{3,1},{4,6},{5,7},{6,4},{7,5},{8,10},{9,11},{10,... | collective-permute-start | bytes 129032 | tf_op jit(solution)/shard_map/ppermute | solution.py:237
  83.7 0.6 collective-permute-start.16
  84.3 2.0 %collective-permute-done.15 = bf16[56,384]{1,0:T(8,128)(2,1)S(1)} collective-permute-done((bf16[56,384]{1,0:T(8,128)(2,1)S(1)}, bf16[56,384]{1,0:T(8,128)(2,1)S(1)}, u32[]{:S(2)}, u32[]{:S(2)}) %collective-permute-start.15) | collective-permute-done | bytes 43040 | tf_op jit(solution)/shard_map/ppermute | solution.py:237
  86.3 1.5 %collective-permute-start.17 = (bf16[56,384]{1,0:T(8,128)(2,1)S(1)}, bf16[56,384]{1,0:T(8,128)(2,1)S(1)}, u32[]{:S(2)}, u32[]{:S(2)}) collective-permute-start(bf16[56,384]{1,0:T(8,128)(2,1)S(1)} %subtract_convert_fusion.1), channel_id=1, source_target_pairs={{0,6},{1,7},{2,4},{3,5},{4,2},{5,3},{6,0},{7,1},{8,14},{9,15},{10,... | collective-permute-start | bytes 129032 | tf_op jit(solution)/shard_map/ppermute | solution.py:237
  87.8 3.5 %collective-permute-done.17 = bf16[56,384]{1,0:T(8,128)(2,1)S(1)} collective-permute-done((bf16[56,384]{1,0:T(8,128)(2,1)S(1)}, bf16[56,384]{1,0:T(8,128)(2,1)S(1)}, u32[]{:S(2)}, u32[]{:S(2)}) %collective-permute-start.17) | collective-permute-done | bytes 43040 | tf_op jit(solution)/shard_map/ppermute | solution.py:237
  91.3 0.1 select_select_fusion.2
  91.5 0.1 pad_maximum_fusion.1.refs_1_
  91.6 1.4 %collective-permute-start.21 = (bf16[208,1024]{1,0:T(8,128)(2,1)S(1)}, bf16[208,1024]{1,0:T(8,128)(2,1)S(1)}, u32[]{:S(2)}, u32[]{:S(2)}) collective-permute-start(bf16[208,1024]{1,0:T(8,128)(2,1)S(1)} %pad_maximum_fusion.1.refs_1_), channel_id=1, source_target_pairs={{0,4},{1,3},{2,6},{3,1},{4,0},{5,7},{6,2},{7,5},{8,12},{9,11},{10,... | collective-permute-start | bytes 1277960 | tf_op jit(solution)/shard_map/ppermute | solution.py:282
  93.0 0.6 collective-permute-start.30
  93.7 0.1 select_select_fusion.7
  93.7 10.6 %collective-permute-done.21.refs_0_ = bf16[208,1024]{1,0:T(8,128)(2,1)S(1)} collective-permute-done((bf16[208,1024]{1,0:T(8,128)(2,1)S(1)}, bf16[208,1024]{1,0:T(8,128)(2,1)S(1)}, u32[]{:S(2)}, u32[]{:S(2)}) %collective-permute-start.21) | collective-permute-done | bytes 426016 | tf_op jit(solution)/shard_map/ppermute | solution.py:282
  104.3 0.4 collective-permute-start.22
  104.8 0.1 collective-permute-start.33
  104.8 1.5 %collective-permute-start.24 = (bf16[208,384]{1,0:T(8,128)(2,1)S(1)}, bf16[208,384]{1,0:T(8,128)(2,1)S(1)}, u32[]{:S(2)}, u32[]{:S(2)}) collective-permute-start(bf16[208,384]{1,0:T(8,128)(2,1)S(1)} %pad_maximum_fusion.2.refs_0_), channel_id=1, source_target_pairs={{0,8},{1,9},{2,10},{3,11},{4,12},{5,13},{6,14},{7,15},{8,0},{9,1},... | collective-permute-start | bytes 479240 | tf_op jit(solution)/shard_map/ppermute | solution.py:237
  106.4 0.2 collective-permute-start.34
  106.5 0.4 collective-permute-start.31
  106.9 4.5 %collective-permute-done.24.refs_0_ = bf16[208,384]{1,0:T(8,128)(2,1)S(1)} collective-permute-done((bf16[208,384]{1,0:T(8,128)(2,1)S(1)}, bf16[208,384]{1,0:T(8,128)(2,1)S(1)}, u32[]{:S(2)}, u32[]{:S(2)}) %collective-permute-start.24) | collective-permute-done | bytes 159776 | tf_op jit(solution)/shard_map/ppermute | solution.py:237
  111.3 0.7 collective-permute-start.25
  112.1 0.4 collective-permute-done.22.refs_0_
  112.4 0.2 collective-permute-start.23
  112.6 8.7 %collective-permute-done.25.refs_1_ = bf16[208,384]{1,0:T(8,128)(2,1)S(1)} collective-permute-done((bf16[208,384]{1,0:T(8,128)(2,1)S(1)}, bf16[208,384]{1,0:T(8,128)(2,1)S(1)}, u32[]{:S(2)}, u32[]{:S(2)}) %collective-permute-start.25) | collective-permute-done | bytes 159776 | tf_op jit(solution)/shard_map/ppermute | solution.py:237
  121.3 1.5 %collective-permute-start.26 = (bf16[208,384]{1,0:T(8,128)(2,1)S(1)}, bf16[208,384]{1,0:T(8,128)(2,1)S(1)}, u32[]{:S(2)}, u32[]{:S(2)}) collective-permute-start(bf16[208,384]{1,0:T(8,128)(2,1)S(1)} %pad_maximum_fusion.2.refs_0_), channel_id=1, source_target_pairs={{0,24},{1,25},{2,26},{3,27},{4,28},{5,29},{6,30},{7,31},{8,16},{9,... | collective-permute-start | bytes 479240 | tf_op jit(solution)/shard_map/ppermute | solution.py:237
  122.8 5.6 %collective-permute-done.26.refs_2_ = bf16[208,384]{1,0:T(8,128)(2,1)S(1)} collective-permute-done((bf16[208,384]{1,0:T(8,128)(2,1)S(1)}, bf16[208,384]{1,0:T(8,128)(2,1)S(1)}, u32[]{:S(2)}, u32[]{:S(2)}) %collective-permute-start.26) | collective-permute-done | bytes 159776 | tf_op jit(solution)/shard_map/ppermute | solution.py:237
  128.3 0.5 collective-permute-start.28
  128.8 0.1 collective-permute-start.29
  128.9 1.9 %place.4.refs_4_ = bf16[1664,1408]{1,0:T(8,128)(2,1)} custom-call(bf16[208,384]{1,0:T(8,128)(2,1)S(1)} %pad_maximum_fusion.2.refs_0_, bf16[208,1024]{1,0:T(8,128)(2,1)S(1)} %pad_maximum_fusion.1.refs_1_, bf16[208,384]{1,0:T(8,128)(2,1)S(1)} %collective-permute-done.33.refs_2_, bf16[208,1024]{1,0:T(8,128)(2,1)S(1)} %collective-permute-done.34.refs_3_), custom_call_target="tpu_custom_call" | custom-call | tf_op jit(solution)/shard_map/place/pallas_call | solution.py:193
  130.8 2.2 %place.5.refs_6_ = bf16[1664,1408]{1,0:T(8,128)(2,1)} custom-call(bf16[208,1024]{1,0:T(8,128)(2,1)S(1)} %collective-permute-done.21.refs_0_, bf16[208,1024]{1,0:T(8,128)(2,1)S(1)} %collective-permute-done.30.refs_1_, bf16[208,1024]{1,0:T(8,128)(2,1)S(1)} %collective-permute-done.31.refs_2_, ...), custom_call_target="tpu_custom_call", output_to_operand_aliasing={{}: (4, {})} | custom-call | tf_op jit(solution)/shard_map/place/pallas_call | solution.py:193
  133.1 2.3 %place.6.refs_2_ = bf16[1664,1408]{1,0:T(8,128)(2,1)} custom-call(bf16[208,384]{1,0:T(8,128)(2,1)S(1)} %collective-permute-done.24.refs_0_, bf16[208,384]{1,0:T(8,128)(2,1)S(1)} %collective-permute-done.25.refs_1_, bf16[208,384]{1,0:T(8,128)(2,1)S(1)} %collective-permute-done.26.refs_2_, ...), custom_call_target="tpu_custom_call", output_to_operand_aliasing={{}: (6, {})} | custom-call | tf_op jit(solution)/shard_map/place/pallas_call | solution.py:193
  135.4 1.4 %place.7 = bf16[1664,1408]{1,0:T(8,128)(2,1)} custom-call(bf16[208,1024]{1,0:T(8,128)(2,1)S(1)} %collective-permute-done.22.refs_0_, bf16[208,1024]{1,0:T(8,128)(2,1)S(1)} %collective-permute-done.23.refs_1_, bf16[1664,1408]{1,0:T(8,128)(2,1)} %place.6.refs_2_), custom_call_target="tpu_custom_call", output_to_operand_aliasing={{}: (2, {})} | custom-call | tf_op jit(solution)/shard_map/place/pallas_call | solution.py:193
  (33 shorter events, 0.2 us)
Async XLA Ops:
  19.4 4.1 %collective-permute-start.4 = (bf16[832,1024]{1,0:T(8,128)(2,1)}, bf16[832,1024]{1,0:T(8,128)(2,1)}, u32[]{:S(2)}, u32[]{:S(2)}) collective-permute-start(bf16[832,1024]{1,0:T(8,128)(2,1)} %get-tuple-element.31), channel_id=1, source_target_pairs={{0,1},{1,0},{2,3},{3,2},{4,5},{5,4},{6,7},{7,6},{8,9},{9,8},{10,11... | collective-permute-start | bytes 5111816 | tf_op jit(solution)/shard_map/ppermute | solution.py:237
  19.9 23.4 %copy-start = (f32[832,1024]{1,0:T(8,128)S(1)}, f32[832,1024]{1,0:T(8,128)}, u32[]{:S(2)}) copy-start(f32[832,1024]{1,0:T(8,128)} %get-tuple-element.30) | copy-start | bytes 10223620
  26.4 16.4 %collective-permute-start.5 = (bf16[416,1024]{1,0:T(8,128)(2,1)}, bf16[416,1024]{1,0:T(8,128)(2,1)}, u32[]{:S(2)}, u32[]{:S(2)}) collective-permute-start(bf16[416,1024]{1,0:T(8,128)(2,1)} %pad_maximum_fusion), channel_id=1, source_target_pairs={{0,2},{1,5},{2,0},{3,7},{4,6},{5,1},{6,4},{7,3},{8,10},{9,13},{10,... | collective-permute-start | bytes 2555912 | tf_op jit(solution)/shard_map/ppermute | solution.py:273
  29.3 6.5 %collective-permute-start = (bf16[832,384]{1,0:T(8,128)(2,1)}, bf16[832,384]{1,0:T(8,128)(2,1)}, u32[]{:S(2)}, u32[]{:S(2)}) collective-permute-start(bf16[832,384]{1,0:T(8,128)(2,1)} %get-tuple-element.29), channel_id=1, source_target_pairs={{0,1},{1,0},{2,3},{3,2},{4,5},{5,4},{6,7},{7,6},{8,9},{9,8},{10,11... | collective-permute-start | bytes 1916936 | tf_op jit(solution)/shard_map/ppermute | solution.py:237
  30.8 20.2 %collective-permute-start.11 = (bf16[52,1024]{1,0:T(8,128)(2,1)}, bf16[52,1024]{1,0:T(8,128)(2,1)S(1)}, u32[]{:S(2)}, u32[]{:S(2)}) collective-permute-start(bf16[52,1024]{1,0:T(8,128)(2,1)} %slice.39), channel_id=1, source_target_pairs={{0,0},{1,8},{2,16},{3,24},{4,2},{5,10},{6,18},{7,26},{8,4},{9,12},... | collective-permute-start | bytes 319496 | tf_op jit(solution)/shard_map/ppermute | solution.py:353
  33.7 10.9 %collective-permute-start.10 = (bf16[52,384]{1,0:T(8,128)(2,1)}, bf16[52,384]{1,0:T(8,128)(2,1)}, u32[]{:S(2)}, u32[]{:S(2)}) collective-permute-start(bf16[52,384]{1,0:T(8,128)(2,1)} %slice.38), channel_id=1, source_target_pairs={{0,0},{1,2},{2,4},{3,6},{4,8},{5,10},{6,12},{7,14},{8,16},{9,18},{... | collective-permute-start | bytes 119816 | tf_op jit(solution)/shard_map/ppermute | solution.py:352
  37.2 13.9 %collective-permute-start.1 = (bf16[208,384]{1,0:T(8,128)(2,1)S(1)}, bf16[208,384]{1,0:T(8,128)(2,1)S(1)}, u32[]{:S(2)}, u32[]{:S(2)}) collective-permute-start(bf16[208,384]{1,0:T(8,128)(2,1)S(1)} %get-tuple-element.49), channel_id=1, source_target_pairs={{0,24},{1,25},{2,26},{3,27},{4,28},{5,29},{6,30},{7,31},{8,16},{9,... | collective-permute-start | bytes 479240 | tf_op jit(solution)/shard_map/ppermute | solution.py:237
  42.7 15.2 %collective-permute-start.2 = (bf16[208,384]{1,0:T(8,128)(2,1)S(1)}, bf16[208,384]{1,0:T(8,128)(2,1)S(1)}, u32[]{:S(2)}, u32[]{:S(2)}) collective-permute-start(bf16[208,384]{1,0:T(8,128)(2,1)S(1)} %get-tuple-element.51), channel_id=1, source_target_pairs={{0,16},{1,17},{2,18},{3,19},{4,20},{5,21},{6,22},{7,23},{8,24},{9,... | collective-permute-start | bytes 479240 | tf_op jit(solution)/shard_map/ppermute | solution.py:237
  42.8 15.1 %collective-permute-start.3 = (bf16[208,384]{1,0:T(8,128)(2,1)S(1)}, bf16[208,384]{1,0:T(8,128)(2,1)S(1)}, u32[]{:S(2)}, u32[]{:S(2)}) collective-permute-start(bf16[208,384]{1,0:T(8,128)(2,1)S(1)} %get-tuple-element.50), channel_id=1, source_target_pairs={{0,8},{1,9},{2,10},{3,11},{4,12},{5,13},{6,14},{7,15},{8,0},{9,1},... | collective-permute-start | bytes 479240 | tf_op jit(solution)/shard_map/ppermute | solution.py:237
  44.7 14.4 %collective-permute-start.6 = (bf16[208,1024]{1,0:T(8,128)(2,1)S(1)}, bf16[208,1024]{1,0:T(8,128)(2,1)S(1)}, u32[]{:S(2)}, u32[]{:S(2)}) collective-permute-start(bf16[208,1024]{1,0:T(8,128)(2,1)S(1)} %add_convert_fusion), channel_id=1, source_target_pairs={{0,4},{1,3},{2,6},{3,1},{4,0},{5,7},{6,2},{7,5},{8,12},{9,11},{10,... | collective-permute-start | bytes 1277960 | tf_op jit(solution)/shard_map/ppermute | solution.py:276
  60.5 6.9 %collective-permute-start.7 = (bf16[56,384]{1,0:T(8,128)(2,1)S(1)}, bf16[56,384]{1,0:T(8,128)(2,1)S(1)}, u32[]{:S(2)}, u32[]{:S(2)}) collective-permute-start(bf16[56,384]{1,0:T(8,128)(2,1)S(1)} %get-tuple-element.59), channel_id=1, source_target_pairs={{0,6},{1,7},{2,4},{3,5},{4,2},{5,3},{6,0},{7,1},{8,14},{9,15},{10,... | collective-permute-start | bytes 129032 | tf_op jit(solution)/shard_map/ppermute | solution.py:237
  62.5 7.4 %collective-permute-start.8 = (bf16[56,384]{1,0:T(8,128)(2,1)S(1)}, bf16[56,384]{1,0:T(8,128)(2,1)S(1)}, u32[]{:S(2)}, u32[]{:S(2)}) collective-permute-start(bf16[56,384]{1,0:T(8,128)(2,1)S(1)} %get-tuple-element.61), channel_id=1, source_target_pairs={{0,4},{1,5},{2,6},{3,7},{4,0},{5,1},{6,2},{7,3},{8,12},{9,13},{10,... | collective-permute-start | bytes 129032 | tf_op jit(solution)/shard_map/ppermute | solution.py:237
  64.6 5.3 %collective-permute-start.9 = (bf16[56,384]{1,0:T(8,128)(2,1)S(1)}, bf16[56,384]{1,0:T(8,128)(2,1)S(1)}, u32[]{:S(2)}, u32[]{:S(2)}) collective-permute-start(bf16[56,384]{1,0:T(8,128)(2,1)S(1)} %get-tuple-element.60), channel_id=1, source_target_pairs={{0,2},{1,3},{2,0},{3,1},{4,6},{5,7},{6,4},{7,5},{8,10},{9,11},{10,... | collective-permute-start | bytes 129032 | tf_op jit(solution)/shard_map/ppermute | solution.py:237
  65.4 7.9 %collective-permute-start.12 = (bf16[56,1024]{1,0:T(8,128)(2,1)S(1)}, bf16[56,1024]{1,0:T(8,128)(2,1)S(1)}, u32[]{:S(2)}, u32[]{:S(2)}) collective-permute-start(bf16[56,1024]{1,0:T(8,128)(2,1)S(1)} %get-tuple-element.52), channel_id=1, source_target_pairs={{0,24},{1,25},{2,26},{3,27},{4,28},{5,29},{6,30},{7,31},{8,16},{9,... | collective-permute-start | bytes 344072 | tf_op jit(solution)/shard_map/ppermute | solution.py:237
  67.4 9.4 %collective-permute-start.13 = (bf16[56,1024]{1,0:T(8,128)(2,1)S(1)}, bf16[56,1024]{1,0:T(8,128)(2,1)S(1)}, u32[]{:S(2)}, u32[]{:S(2)}) collective-permute-start(bf16[56,1024]{1,0:T(8,128)(2,1)S(1)} %get-tuple-element.54), channel_id=1, source_target_pairs={{0,16},{1,17},{2,18},{3,19},{4,20},{5,21},{6,22},{7,23},{8,24},{9,... | collective-permute-start | bytes 344072 | tf_op jit(solution)/shard_map/ppermute | solution.py:237
  67.4 9.4 %collective-permute-start.14 = (bf16[56,1024]{1,0:T(8,128)(2,1)S(1)}, bf16[56,1024]{1,0:T(8,128)(2,1)S(1)}, u32[]{:S(2)}, u32[]{:S(2)}) collective-permute-start(bf16[56,1024]{1,0:T(8,128)(2,1)S(1)} %get-tuple-element.53), channel_id=1, source_target_pairs={{0,8},{1,9},{2,10},{3,11},{4,12},{5,13},{6,14},{7,15},{8,0},{9,1},... | collective-permute-start | bytes 344072 | tf_op jit(solution)/shard_map/ppermute | solution.py:237
  77.9 13.4 %collective-permute-start.18 = (bf16[56,1024]{1,0:T(8,128)(2,1)S(1)}, bf16[56,1024]{1,0:T(8,128)(2,1)S(1)}, u32[]{:S(2)}, u32[]{:S(2)}) collective-permute-start(bf16[56,1024]{1,0:T(8,128)(2,1)S(1)} %subtract_convert_fusion), channel_id=1, source_target_pairs={{0,8},{1,9},{2,10},{3,11},{4,12},{5,13},{6,14},{7,15},{8,0},{9,1},... | collective-permute-start | bytes 344072 | tf_op jit(solution)/shard_map/ppermute | solution.py:237
  78.1 13.2 %collective-permute-start.19 = (bf16[56,1024]{1,0:T(8,128)(2,1)S(1)}, bf16[56,1024]{1,0:T(8,128)(2,1)S(1)}, u32[]{:S(2)}, u32[]{:S(2)}) collective-permute-start(bf16[56,1024]{1,0:T(8,128)(2,1)S(1)} %subtract_convert_fusion), channel_id=1, source_target_pairs={{0,16},{1,17},{2,18},{3,19},{4,20},{5,21},{6,22},{7,23},{8,24},{9,... | collective-permute-start | bytes 344072 | tf_op jit(solution)/shard_map/ppermute | solution.py:237
  80.4 10.9 %collective-permute-start.20 = (bf16[56,1024]{1,0:T(8,128)(2,1)S(1)}, bf16[56,1024]{1,0:T(8,128)(2,1)S(1)}, u32[]{:S(2)}, u32[]{:S(2)}) collective-permute-start(bf16[56,1024]{1,0:T(8,128)(2,1)S(1)} %subtract_convert_fusion), channel_id=1, source_target_pairs={{0,24},{1,25},{2,26},{3,27},{4,28},{5,29},{6,30},{7,31},{8,16},{9,... | collective-permute-start | bytes 344072 | tf_op jit(solution)/shard_map/ppermute | solution.py:237
  82.3 4.0 %collective-permute-start.15 = (bf16[56,384]{1,0:T(8,128)(2,1)S(1)}, bf16[56,384]{1,0:T(8,128)(2,1)S(1)}, u32[]{:S(2)}, u32[]{:S(2)}) collective-permute-start(bf16[56,384]{1,0:T(8,128)(2,1)S(1)} %subtract_convert_fusion.1), channel_id=1, source_target_pairs={{0,2},{1,3},{2,0},{3,1},{4,6},{5,7},{6,4},{7,5},{8,10},{9,11},{10,... | collective-permute-start | bytes 129032 | tf_op jit(solution)/shard_map/ppermute | solution.py:237
  83.7 4.1 %collective-permute-start.16 = (bf16[56,384]{1,0:T(8,128)(2,1)S(1)}, bf16[56,384]{1,0:T(8,128)(2,1)S(1)}, u32[]{:S(2)}, u32[]{:S(2)}) collective-permute-start(bf16[56,384]{1,0:T(8,128)(2,1)S(1)} %subtract_convert_fusion.1), channel_id=1, source_target_pairs={{0,4},{1,5},{2,6},{3,7},{4,0},{5,1},{6,2},{7,3},{8,12},{9,13},{10,... | collective-permute-start | bytes 129032 | tf_op jit(solution)/shard_map/ppermute | solution.py:237
  86.3 4.9 %collective-permute-start.17 = (bf16[56,384]{1,0:T(8,128)(2,1)S(1)}, bf16[56,384]{1,0:T(8,128)(2,1)S(1)}, u32[]{:S(2)}, u32[]{:S(2)}) collective-permute-start(bf16[56,384]{1,0:T(8,128)(2,1)S(1)} %subtract_convert_fusion.1), channel_id=1, source_target_pairs={{0,6},{1,7},{2,4},{3,5},{4,2},{5,3},{6,0},{7,1},{8,14},{9,15},{10,... | collective-permute-start | bytes 129032 | tf_op jit(solution)/shard_map/ppermute | solution.py:237
  91.6 12.8 %collective-permute-start.21 = (bf16[208,1024]{1,0:T(8,128)(2,1)S(1)}, bf16[208,1024]{1,0:T(8,128)(2,1)S(1)}, u32[]{:S(2)}, u32[]{:S(2)}) collective-permute-start(bf16[208,1024]{1,0:T(8,128)(2,1)S(1)} %pad_maximum_fusion.1.refs_1_), channel_id=1, source_target_pairs={{0,4},{1,3},{2,6},{3,1},{4,0},{5,7},{6,2},{7,5},{8,12},{9,11},{10,... | collective-permute-start | bytes 1277960 | tf_op jit(solution)/shard_map/ppermute | solution.py:282
  93.0 19.1 %collective-permute-start.30 = (bf16[208,1024]{1,0:T(8,128)(2,1)S(1)}, bf16[208,1024]{1,0:T(8,128)(2,1)S(1)}, u32[]{:S(2)}, u32[]{:S(2)}) collective-permute-start(bf16[208,1024]{1,0:T(8,128)(2,1)S(1)} %pad_maximum_fusion.1.refs_1_), channel_id=1, source_target_pairs={{0,2},{1,5},{2,0},{3,7},{4,6},{5,1},{6,4},{7,3},{8,10},{9,13},{10,... | collective-permute-start | bytes 1277960 | tf_op jit(solution)/shard_map/ppermute | solution.py:283
  104.3 8.1 %collective-permute-start.22 = (bf16[208,1024]{1,0:T(8,128)(2,1)S(1)}, bf16[208,1024]{1,0:T(8,128)(2,1)S(1)}, u32[]{:S(2)}, u32[]{:S(2)}) collective-permute-start(bf16[208,1024]{1,0:T(8,128)(2,1)S(1)} %collective-permute-done.21.refs_0_), channel_id=1, source_target_pairs={{0,2},{1,5},{2,0},{3,7},{4,6},{5,1},{6,4},{7,3},{8,10},{9,13},{10,... | collective-permute-start | bytes 1277960 | tf_op jit(solution)/shard_map/ppermute | solution.py:284
  104.8 1.8 %collective-permute-start.33 = (bf16[208,384]{1,0:T(8,128)(2,1)S(1)}, bf16[208,384]{1,0:T(8,128)(2,1)S(1)}, u32[]{:S(2)}, u32[]{:S(2)}) collective-permute-start(bf16[208,384]{1,0:T(8,128)(2,1)S(1)} %pad_maximum_fusion.2.refs_0_), channel_id=1, source_target_pairs={{0,1},{1,0},{2,3},{3,2},{4,5},{5,4},{6,7},{7,6},{8,9},{9,8},{10,11... | collective-permute-start | bytes 479240 | tf_op jit(solution)/shard_map/ppermute | solution.py:237
  104.8 6.5 %collective-permute-start.24 = (bf16[208,384]{1,0:T(8,128)(2,1)S(1)}, bf16[208,384]{1,0:T(8,128)(2,1)S(1)}, u32[]{:S(2)}, u32[]{:S(2)}) collective-permute-start(bf16[208,384]{1,0:T(8,128)(2,1)S(1)} %pad_maximum_fusion.2.refs_0_), channel_id=1, source_target_pairs={{0,8},{1,9},{2,10},{3,11},{4,12},{5,13},{6,14},{7,15},{8,0},{9,1},... | collective-permute-start | bytes 479240 | tf_op jit(solution)/shard_map/ppermute | solution.py:237
  106.4 22.0 %collective-permute-start.34 = (bf16[208,1024]{1,0:T(8,128)(2,1)S(1)}, bf16[208,1024]{1,0:T(8,128)(2,1)S(1)}, u32[]{:S(2)}, u32[]{:S(2)}) collective-permute-start(bf16[208,1024]{1,0:T(8,128)(2,1)S(1)} %pad_maximum_fusion.1.refs_1_), channel_id=1, source_target_pairs={{0,1},{1,0},{2,3},{3,2},{4,5},{5,4},{6,7},{7,6},{8,9},{9,8},{10,11... | collective-permute-start | bytes 1277960 | tf_op jit(solution)/shard_map/ppermute | solution.py:237
  106.5 22.3 %collective-permute-start.31 = (bf16[208,1024]{1,0:T(8,128)(2,1)S(1)}, bf16[208,1024]{1,0:T(8,128)(2,1)S(1)}, u32[]{:S(2)}, u32[]{:S(2)}) collective-permute-start(bf16[208,1024]{1,0:T(8,128)(2,1)S(1)} %collective-permute-done.21.refs_0_), channel_id=1, source_target_pairs={{0,1},{1,0},{2,3},{3,2},{4,5},{5,4},{6,7},{7,6},{8,9},{9,8},{10,11... | collective-permute-start | bytes 1277960 | tf_op jit(solution)/shard_map/ppermute | solution.py:237
  111.3 9.9 %collective-permute-start.25 = (bf16[208,384]{1,0:T(8,128)(2,1)S(1)}, bf16[208,384]{1,0:T(8,128)(2,1)S(1)}, u32[]{:S(2)}, u32[]{:S(2)}) collective-permute-start(bf16[208,384]{1,0:T(8,128)(2,1)S(1)} %pad_maximum_fusion.2.refs_0_), channel_id=1, source_target_pairs={{0,16},{1,17},{2,18},{3,19},{4,20},{5,21},{6,22},{7,23},{8,24},{9,... | collective-permute-start | bytes 479240 | tf_op jit(solution)/shard_map/ppermute | solution.py:237
  112.1 18.8 %collective-permute-start.32 = (bf16[208,1024]{1,0:T(8,128)(2,1)S(1)}, bf16[208,1024]{1,0:T(8,128)(2,1)S(1)}, u32[]{:S(2)}, u32[]{:S(2)}) collective-permute-start(bf16[208,1024]{1,0:T(8,128)(2,1)S(1)} %collective-permute-done.30.refs_1_), channel_id=1, source_target_pairs={{0,1},{1,0},{2,3},{3,2},{4,5},{5,4},{6,7},{7,6},{8,9},{9,8},{10,11... | collective-permute-start | bytes 1277960 | tf_op jit(solution)/shard_map/ppermute | solution.py:237
  112.4 22.9 %collective-permute-start.23 = (bf16[208,1024]{1,0:T(8,128)(2,1)S(1)}, bf16[208,1024]{1,0:T(8,128)(2,1)S(1)}, u32[]{:S(2)}, u32[]{:S(2)}) collective-permute-start(bf16[208,1024]{1,0:T(8,128)(2,1)S(1)} %collective-permute-done.22.refs_0_), channel_id=1, source_target_pairs={{0,1},{1,0},{2,3},{3,2},{4,5},{5,4},{6,7},{7,6},{8,9},{9,8},{10,11... | collective-permute-start | bytes 1277960 | tf_op jit(solution)/shard_map/ppermute | solution.py:237
  121.3 7.1 %collective-permute-start.26 = (bf16[208,384]{1,0:T(8,128)(2,1)S(1)}, bf16[208,384]{1,0:T(8,128)(2,1)S(1)}, u32[]{:S(2)}, u32[]{:S(2)}) collective-permute-start(bf16[208,384]{1,0:T(8,128)(2,1)S(1)} %pad_maximum_fusion.2.refs_0_), channel_id=1, source_target_pairs={{0,24},{1,25},{2,26},{3,27},{4,28},{5,29},{6,30},{7,31},{8,16},{9,... | collective-permute-start | bytes 479240 | tf_op jit(solution)/shard_map/ppermute | solution.py:237
  128.3 4.7 %collective-permute-start.27 = (bf16[208,384]{1,0:T(8,128)(2,1)S(1)}, bf16[208,384]{1,0:T(8,128)(2,1)S(1)}, u32[]{:S(2)}, u32[]{:S(2)}) collective-permute-start(bf16[208,384]{1,0:T(8,128)(2,1)S(1)} %collective-permute-done.24.refs_0_), channel_id=1, source_target_pairs={{0,1},{1,0},{2,3},{3,2},{4,5},{5,4},{6,7},{7,6},{8,9},{9,8},{10,11... | collective-permute-start | bytes 479240 | tf_op jit(solution)/shard_map/ppermute | solution.py:237
  128.3 4.7 %collective-permute-start.28 = (bf16[208,384]{1,0:T(8,128)(2,1)S(1)}, bf16[208,384]{1,0:T(8,128)(2,1)S(1)}, u32[]{:S(2)}, u32[]{:S(2)}) collective-permute-start(bf16[208,384]{1,0:T(8,128)(2,1)S(1)} %collective-permute-done.25.refs_1_), channel_id=1, source_target_pairs={{0,1},{1,0},{2,3},{3,2},{4,5},{5,4},{6,7},{7,6},{8,9},{9,8},{10,11... | collective-permute-start | bytes 479240 | tf_op jit(solution)/shard_map/ppermute | solution.py:237
  128.8 4.2 %collective-permute-start.29 = (bf16[208,384]{1,0:T(8,128)(2,1)S(1)}, bf16[208,384]{1,0:T(8,128)(2,1)S(1)}, u32[]{:S(2)}, u32[]{:S(2)}) collective-permute-start(bf16[208,384]{1,0:T(8,128)(2,1)S(1)} %collective-permute-done.26.refs_2_), channel_id=1, source_target_pairs={{0,1},{1,0},{2,3},{3,2},{4,5},{5,4},{6,7},{7,6},{8,9},{9,8},{10,11... | collective-permute-start | bytes 479240 | tf_op jit(solution)/shard_map/ppermute | solution.py:237

commit v6 on v5

--- a/solution.py
+++ b/solution.py
@@ -269,12 +269,12 @@
     def at(d):
         return rows_at(side.index ^ d)
 
-    sent = jnp.concatenate([at(far_d).astype(bf16), at(first_d).astype(bf16)], axis=0)
-    got = lax.ppermute(sent, "ex", first)
-    count = sent.shape[0] // 2
-    passed = (at(second_d) + got[:count].astype(f32)).astype(bf16)
+    far, near = at(far_d).astype(bf16), at(first_d).astype(bf16)
+    got_far = lax.ppermute(far, "ex", first)
+    got_near = lax.ppermute(near, "ex", first)
+    passed = (at(second_d) + got_far.astype(f32)).astype(bf16)
     last = lax.ppermute(passed, "ex", second)
-    return at(0) + got[count:].astype(f32) + last.astype(f32)
+    return at(0) + got_near.astype(f32) + last.astype(f32)
 
 
 def two_way_spread(x):

time: 138 us -> 138 us (level)
  waiting for transfers between devices: 51.6 us -> 53.7 us
  starting transfers between devices: 43.4 us -> 42 us
    ppermute x1, starting transfers between devices: 5.45 us -> 0.91 us  [two_way_sum(): last = lax.ppermute(passed, 'ex', second)]
    ppermute x1 -> x2, starting transfers between devices: 2.85 us -> 6.58 us  [the longest x1 3.73 us: two_way_sum(): got_near = lax.ppermute(near, 'ex', first)]
    ppermute x28, waiting for transfers between devices: 40.6 us -> 42.5 us  [swap(): return lax.ppermute(x, 'ex', self.pairs[d])]
    ppermute x28, starting transfers between devices: 29 us -> 27.6 us  [swap(): return lax.ppermute(x, 'ex', self.pairs[d])]
  transfers between devices with their start and end apart: 35 -> 36, of which waited for: 11 -> 13; matrix products, arithmetic and copies ran while one was open for 6% -> 9% of each run, Pallas kernels for 5% -> 5%
where the time goes in v6:
time: 138 us
  waiting for transfers between devices  53.7 us (39%)
  starting transfers between devices  42 us (30%)
  Pallas kernels  27.2 us (20%)
  other arithmetic  11.2 us (8%)
  local copies, waits for them, and re-layouts  3.09 us (2%)
    ppermute x28, waiting for transfers between devices, swap(): return lax.ppermute(x, 'ex', self.pairs[d])  42.5 us
    ppermute x28, starting transfers between devices, swap(): return lax.ppermute(x, 'ex', self.pairs[d])  27.6 us
    pallas_call x1, Pallas kernels, halves(): pl.pallas_call(functools.partial(head_kernel, shape), in_specs=[anywhere,...  19.4 us
    ppermute x1, waiting for transfers between devices, two_way_spread(): from_second = lax.ppermute(x, 'ex', second)  9.91 us
    pallas_call x4, Pallas kernels, place(): pl.pallas_call(kernel, in_specs=[anywhere] * (count + len(extra)), out_sp...  7.79 us
    ppermute x1, starting transfers between devices, two_way_sum(): got_near = lax.ppermute(near, 'ex', first)  3.73 us
    ppermute x1, starting transfers between devices, two_way_sum(): got_far = lax.ppermute(far, 'ex', first)  2.85 us
    convert_element_type x1, other arithmetic, two_way_sum(): far, near = (at(far_d).astype(bf16), at(first_d).astype(bf16))  2.84 us
  transfers between devices with their start and end apart: 36, of which 13 were waited for; matrix products, arithmetic and copies ran while one was open for 9% of the time, Pallas kernels for 5%

profile of v6, /device:TPU:0, one launch (start us, length us, event | category | flops | bytes accessed | tf_op | source)
XLA Modules:
  0.0 137.5 jit_solution(1632425492430693704)
XLA Ops:
  0.0 19.4 %halves.1 = (bf16[832,384]{1,0:T(8,128)(2,1)}, bf16[832,1024]{1,0:T(8,128)(2,1)}, f32[832,384]{1,0:T(8,128)}, f32[832,1024]{1,0:T(8,128)}) custom-call(bf16[1024,1664]{1,0:T(8,128)(2,1)} %feat_ref.1, s32[8,128]{1,0:T(8,128)} %bitcast.1, bf16[1664,1408]{1,0:T(8,128)(2,1)} %weight_ref.1), custom_call_target="tpu_custom_call" | custom-call | flops 9596567552 | bytes 15122432 | tf_op jit(solution)/shard_map/halves/pallas_call | solution.py:142
  19.4 0.6 collective-permute-start.4
  19.9 0.1 collective-permute-start
  20.0 3.5 %collective-permute-done.4 = bf16[832,1024]{1,0:T(8,128)(2,1)} collective-permute-done((bf16[832,1024]{1,0:T(8,128)(2,1)}, bf16[832,1024]{1,0:T(8,128)(2,1)}, u32[]{:S(2)}, u32[]{:S(2)}) %collective-permute-start.4) | collective-permute-done | bytes 1703968 | tf_op jit(solution)/shard_map/ppermute | solution.py:237
  23.5 2.8 %add_convert_fusion.2 = (bf16[208,1024]{1,0:T(8,128)(2,1)}, bf16[208,1024]{1,0:T(8,128)(2,1)}) fusion(f32[832,1024]{1,0:T(8,128)} %get-tuple-element.30, s32[]{:T(128)S(6)} %select_n.298, bf16[832,1024]{1,0:T(8,128)(2,1)} %collective-permute-done.4, s32[]{:T(128)S(6)} %select_n.301), kind=kLoop, calls=%fused_computation.3 | loop fusion | flops 1277952 | bytes 3407880 | tf_op jit(solution)/shard_map/convert_element_type | solution.py:272
  26.4 2.8 %collective-permute-start.6 = (bf16[208,1024]{1,0:T(8,128)(2,1)}, bf16[208,1024]{1,0:T(8,128)(2,1)}, u32[]{:S(2)}, u32[]{:S(2)}) collective-permute-start(bf16[208,1024]{1,0:T(8,128)(2,1)} %get-tuple-element.48), channel_id=1, source_target_pairs={{0,2},{1,5},{2,0},{3,7},{4,6},{5,1},{6,4},{7,3},{8,10},{9,13},{10,... | collective-permute-start | bytes 1277960 | tf_op jit(solution)/shard_map/ppermute | solution.py:273
  29.2 1.6 %slice.31 = bf16[52,1024]{1,0:T(8,128)(2,1)} slice(bf16[52,1408]{1,0:T(8,128)(2,1)} %param.7), slice={[0:52], [0:1024]} | slice | bytes 212992 | tf_op jit(solution)/shard_map/slice | solution.py:353
  30.8 1.5 %collective-permute-start.12 = (bf16[52,1024]{1,0:T(8,128)(2,1)}, bf16[52,1024]{1,0:T(8,128)(2,1)S(1)}, u32[]{:S(2)}, u32[]{:S(2)}) collective-permute-start(bf16[52,1024]{1,0:T(8,128)(2,1)} %slice.31), channel_id=1, source_target_pairs={{0,0},{1,8},{2,16},{3,24},{4,2},{5,10},{6,18},{7,26},{8,4},{9,12},... | collective-permute-start | bytes 319496 | tf_op jit(solution)/shard_map/ppermute | solution.py:353
  32.3 1.4 %slice.30 = bf16[52,384]{1,0:T(8,128)(2,1)} slice(bf16[52,1408]{1,0:T(8,128)(2,1)} %param.7), slice={[0:52], [1024:1408]} | slice | bytes 79872 | tf_op jit(solution)/shard_map/slice | solution.py:352
  33.7 2.0 %collective-permute-start.11 = (bf16[52,384]{1,0:T(8,128)(2,1)}, bf16[52,384]{1,0:T(8,128)(2,1)}, u32[]{:S(2)}, u32[]{:S(2)}) collective-permute-start(bf16[52,384]{1,0:T(8,128)(2,1)} %slice.30), channel_id=1, source_target_pairs={{0,0},{1,2},{2,4},{3,6},{4,8},{5,10},{6,12},{7,14},{8,16},{9,18},{... | collective-permute-start | bytes 119816 | tf_op jit(solution)/shard_map/ppermute | solution.py:352
  35.8 1.5 %add_convert_fusion.5 = (bf16[208,384]{1,0:T(8,128)(2,1)S(1)}, bf16[208,384]{1,0:T(8,128)(2,1)S(1)}, bf16[208,384]{1,0:T(8,128)(2,1)S(1)}) fusion(f32[832,384]{1,0:T(8,128)} %get-tuple-element.28, s32[]{:T(128)S(6)} %select_n.293, bf16[832,384]{1,0:T(8,128)(2,1)} %collective-permute-done, s32[]{:T(128)S(6)} %select_n.295, s32[]{:T(128)S(6)} %select_n.294), kind=kLoop, calls=%fused_computation.8 | loop fusion | flops 718848 | bytes 1916940 | tf_op jit(solution)/shard_map/convert_element_type | solution.py:242
  37.2 4.3 %collective-permute-start.1 = (bf16[208,384]{1,0:T(8,128)(2,1)S(1)}, bf16[208,384]{1,0:T(8,128)(2,1)S(1)}, u32[]{:S(2)}, u32[]{:S(2)}) collective-permute-start(bf16[208,384]{1,0:T(8,128)(2,1)S(1)} %get-tuple-element.49), channel_id=1, source_target_pairs={{0,24},{1,25},{2,26},{3,27},{4,28},{5,29},{6,30},{7,31},{8,16},{9,... | collective-permute-start | bytes 479240 | tf_op jit(solution)/shard_map/ppermute | solution.py:237
  41.5 0.9 collective-permute-start.2
  42.4 0.2 collective-permute-start.3
  42.6 1.3 add_convert_fusion
  43.9 3.7 %collective-permute-start.5 = (bf16[208,1024]{1,0:T(8,128)(2,1)S(1)}, bf16[208,1024]{1,0:T(8,128)(2,1)S(1)}, u32[]{:S(2)}, u32[]{:S(2)}) collective-permute-start(bf16[208,1024]{1,0:T(8,128)(2,1)S(1)} %copy-done.1), channel_id=1, source_target_pairs={{0,2},{1,5},{2,0},{3,7},{4,6},{5,1},{6,4},{7,3},{8,10},{9,13},{10,... | collective-permute-start | bytes 1277960 | tf_op jit(solution)/shard_map/ppermute | solution.py:274
  47.7 0.9 collective-permute-start.7
  48.6 0.9 select_select_fusion.9
  49.6 7.5 %collective-permute-done.2 = bf16[208,384]{1,0:T(8,128)(2,1)S(1)} collective-permute-done((bf16[208,384]{1,0:T(8,128)(2,1)S(1)}, bf16[208,384]{1,0:T(8,128)(2,1)S(1)}, u32[]{:S(2)}, u32[]{:S(2)}) %collective-permute-start.2) | collective-permute-done | bytes 159776 | tf_op jit(solution)/shard_map/ppermute | solution.py:237
  57.0 1.1 convert_add_fusion.1
  58.1 1.2 collective-permute-done.7
  59.3 1.3 convert_add_fusion
  60.6 2.1 %collective-permute-start.10 = (bf16[56,384]{1,0:T(8,128)(2,1)S(1)}, bf16[56,384]{1,0:T(8,128)(2,1)S(1)}, u32[]{:S(2)}, u32[]{:S(2)}) collective-permute-start(bf16[56,384]{1,0:T(8,128)(2,1)S(1)} %get-tuple-element.60), channel_id=1, source_target_pairs={{0,2},{1,3},{2,0},{3,1},{4,6},{5,7},{6,4},{7,5},{8,10},{9,11},{10,... | collective-permute-start | bytes 129032 | tf_op jit(solution)/shard_map/ppermute | solution.py:237
  62.8 1.1 collective-permute-start.8
  63.9 0.4 collective-permute-start.9
  64.3 0.1 dynamic-slice_convert_fusion.2
  64.4 2.1 %collective-permute-start.13 = (bf16[56,1024]{1,0:T(8,128)(2,1)S(1)}, bf16[56,1024]{1,0:T(8,128)(2,1)S(1)}, u32[]{:S(2)}, u32[]{:S(2)}) collective-permute-start(bf16[56,1024]{1,0:T(8,128)(2,1)S(1)} %get-tuple-element.52), channel_id=1, source_target_pairs={{0,24},{1,25},{2,26},{3,27},{4,28},{5,29},{6,30},{7,31},{8,16},{9,... | collective-permute-start | bytes 344072 | tf_op jit(solution)/shard_map/ppermute | solution.py:237
  66.5 2.4 %collective-permute-start.15 = (bf16[56,1024]{1,0:T(8,128)(2,1)S(1)}, bf16[56,1024]{1,0:T(8,128)(2,1)S(1)}, u32[]{:S(2)}, u32[]{:S(2)}) collective-permute-start(bf16[56,1024]{1,0:T(8,128)(2,1)S(1)} %get-tuple-element.53), channel_id=1, source_target_pairs={{0,8},{1,9},{2,10},{3,11},{4,12},{5,13},{6,14},{7,15},{8,0},{9,1},... | collective-permute-start | bytes 344072 | tf_op jit(solution)/shard_map/ppermute | solution.py:237
  68.8 0.9 subtract_convert_fusion.1
  69.7 2.6 %collective-permute-done.13 = bf16[56,1024]{1,0:T(8,128)(2,1)S(1)} collective-permute-done((bf16[56,1024]{1,0:T(8,128)(2,1)S(1)}, bf16[56,1024]{1,0:T(8,128)(2,1)S(1)}, u32[]{:S(2)}, u32[]{:S(2)}) %collective-permute-start.13) | collective-permute-done | bytes 114720 | tf_op jit(solution)/shard_map/ppermute | solution.py:237
  72.3 4.1 %collective-permute-done.14 = bf16[56,1024]{1,0:T(8,128)(2,1)S(1)} collective-permute-done((bf16[56,1024]{1,0:T(8,128)(2,1)S(1)}, bf16[56,1024]{1,0:T(8,128)(2,1)S(1)}, u32[]{:S(2)}, u32[]{:S(2)}) %collective-permute-start.14) | collective-permute-done | bytes 114720 | tf_op jit(solution)/shard_map/ppermute | solution.py:237
  76.3 1.0 subtract_convert_fusion
  77.4 0.1 collective-permute-start.19
  77.5 3.1 %collective-permute-start.20 = (bf16[56,1024]{1,0:T(8,128)(2,1)S(1)}, bf16[56,1024]{1,0:T(8,128)(2,1)S(1)}, u32[]{:S(2)}, u32[]{:S(2)}) collective-permute-start(bf16[56,1024]{1,0:T(8,128)(2,1)S(1)} %subtract_convert_fusion), channel_id=1, source_target_pairs={{0,16},{1,17},{2,18},{3,19},{4,20},{5,21},{6,22},{7,23},{8,24},{9,... | collective-permute-start | bytes 344072 | tf_op jit(solution)/shard_map/ppermute | solution.py:237
  80.6 1.3 collective-permute-start.21
  81.8 1.6 %collective-permute-start.16 = (bf16[56,384]{1,0:T(8,128)(2,1)S(1)}, bf16[56,384]{1,0:T(8,128)(2,1)S(1)}, u32[]{:S(2)}, u32[]{:S(2)}) collective-permute-start(bf16[56,384]{1,0:T(8,128)(2,1)S(1)} %subtract_convert_fusion.1), channel_id=1, source_target_pairs={{0,2},{1,3},{2,0},{3,1},{4,6},{5,7},{6,4},{7,5},{8,10},{9,11},{10,... | collective-permute-start | bytes 129032 | tf_op jit(solution)/shard_map/ppermute | solution.py:237
  83.5 0.6 collective-permute-start.17
  84.1 1.7 %collective-permute-done.16 = bf16[56,384]{1,0:T(8,128)(2,1)S(1)} collective-permute-done((bf16[56,384]{1,0:T(8,128)(2,1)S(1)}, bf16[56,384]{1,0:T(8,128)(2,1)S(1)}, u32[]{:S(2)}, u32[]{:S(2)}) %collective-permute-start.16) | collective-permute-done | bytes 43040 | tf_op jit(solution)/shard_map/ppermute | solution.py:237
  85.9 1.7 %collective-permute-start.18 = (bf16[56,384]{1,0:T(8,128)(2,1)S(1)}, bf16[56,384]{1,0:T(8,128)(2,1)S(1)}, u32[]{:S(2)}, u32[]{:S(2)}) collective-permute-start(bf16[56,384]{1,0:T(8,128)(2,1)S(1)} %subtract_convert_fusion.1), channel_id=1, source_target_pairs={{0,6},{1,7},{2,4},{3,5},{4,2},{5,3},{6,0},{7,1},{8,14},{9,15},{10,... | collective-permute-start | bytes 129032 | tf_op jit(solution)/shard_map/ppermute | solution.py:237
  87.6 0.3 collective-permute-done.17
  87.8 2.9 %collective-permute-done.18 = bf16[56,384]{1,0:T(8,128)(2,1)S(1)} collective-permute-done((bf16[56,384]{1,0:T(8,128)(2,1)S(1)}, bf16[56,384]{1,0:T(8,128)(2,1)S(1)}, u32[]{:S(2)}, u32[]{:S(2)}) %collective-permute-start.18) | collective-permute-done | bytes 43040 | tf_op jit(solution)/shard_map/ppermute | solution.py:237
  90.8 0.1 select_select_fusion.2
  91.0 0.1 pad_maximum_fusion.refs_1_
  91.1 2.2 %collective-permute-start.22 = (bf16[208,1024]{1,0:T(8,128)(2,1)S(1)}, bf16[208,1024]{1,0:T(8,128)(2,1)S(1)}, u32[]{:S(2)}, u32[]{:S(2)}) collective-permute-start(bf16[208,1024]{1,0:T(8,128)(2,1)S(1)} %pad_maximum_fusion.refs_1_), channel_id=1, source_target_pairs={{0,4},{1,3},{2,6},{3,1},{4,0},{5,7},{6,2},{7,5},{8,12},{9,11},{10,... | collective-permute-start | bytes 1277960 | tf_op jit(solution)/shard_map/ppermute | solution.py:282
  93.3 0.1 collective-permute-start.31
  93.5 9.9 %collective-permute-done.22.refs_0_ = bf16[208,1024]{1,0:T(8,128)(2,1)S(1)} collective-permute-done((bf16[208,1024]{1,0:T(8,128)(2,1)S(1)}, bf16[208,1024]{1,0:T(8,128)(2,1)S(1)}, u32[]{:S(2)}, u32[]{:S(2)}) %collective-permute-start.22) | collective-permute-done | bytes 426016 | tf_op jit(solution)/shard_map/ppermute | solution.py:282
  103.4 1.0 collective-permute-start.23
  104.5 0.1 collective-permute-start.34
  104.5 0.1 collective-permute-start.25
  104.6 0.4 collective-permute-start.35
  105.1 0.9 collective-permute-done.34.refs_2_
  105.9 0.1 collective-permute-start.32
  106.1 5.0 %collective-permute-done.25.refs_0_ = bf16[208,384]{1,0:T(8,128)(2,1)S(1)} collective-permute-done((bf16[208,384]{1,0:T(8,128)(2,1)S(1)}, bf16[208,384]{1,0:T(8,128)(2,1)S(1)}, u32[]{:S(2)}, u32[]{:S(2)}) %collective-permute-start.25) | collective-permute-done | bytes 159776 | tf_op jit(solution)/shard_map/ppermute | solution.py:237
  111.1 1.0 collective-permute-start.26
  112.1 0.5 collective-permute-start.24
  112.6 8.4 %collective-permute-done.26.refs_1_ = bf16[208,384]{1,0:T(8,128)(2,1)S(1)} collective-permute-done((bf16[208,384]{1,0:T(8,128)(2,1)S(1)}, bf16[208,384]{1,0:T(8,128)(2,1)S(1)}, u32[]{:S(2)}, u32[]{:S(2)}) %collective-permute-start.26) | collective-permute-done | bytes 159776 | tf_op jit(solution)/shard_map/ppermute | solution.py:237
  121.0 2.2 %collective-permute-start.27 = (bf16[208,384]{1,0:T(8,128)(2,1)S(1)}, bf16[208,384]{1,0:T(8,128)(2,1)S(1)}, u32[]{:S(2)}, u32[]{:S(2)}) collective-permute-start(bf16[208,384]{1,0:T(8,128)(2,1)S(1)} %pad_maximum_fusion.1.refs_0_), channel_id=1, source_target_pairs={{0,24},{1,25},{2,26},{3,27},{4,28},{5,29},{6,30},{7,31},{8,16},{9,... | collective-permute-start | bytes 479240 | tf_op jit(solution)/shard_map/ppermute | solution.py:237
  123.2 5.7 %collective-permute-done.27.refs_2_ = bf16[208,384]{1,0:T(8,128)(2,1)S(1)} collective-permute-done((bf16[208,384]{1,0:T(8,128)(2,1)S(1)}, bf16[208,384]{1,0:T(8,128)(2,1)S(1)}, u32[]{:S(2)}, u32[]{:S(2)}) %collective-permute-start.27) | collective-permute-done | bytes 159776 | tf_op jit(solution)/shard_map/ppermute | solution.py:237
  128.9 0.5 collective-permute-start.29
  129.4 0.1 collective-permute-start.30
  129.5 1.9 %place.4.refs_4_ = bf16[1664,1408]{1,0:T(8,128)(2,1)} custom-call(bf16[208,384]{1,0:T(8,128)(2,1)S(1)} %pad_maximum_fusion.1.refs_0_, bf16[208,1024]{1,0:T(8,128)(2,1)S(1)} %pad_maximum_fusion.refs_1_, bf16[208,384]{1,0:T(8,128)(2,1)S(1)} %collective-permute-done.34.refs_2_, bf16[208,1024]{1,0:T(8,128)(2,1)S(1)} %collective-permute-done.35.refs_3_), custom_call_target="tpu_custom_call" | custom-call | tf_op jit(solution)/shard_map/place/pallas_call | solution.py:193
  131.4 2.2 %place.5.refs_6_ = bf16[1664,1408]{1,0:T(8,128)(2,1)} custom-call(bf16[208,1024]{1,0:T(8,128)(2,1)S(1)} %collective-permute-done.22.refs_0_, bf16[208,1024]{1,0:T(8,128)(2,1)S(1)} %collective-permute-done.31.refs_1_, bf16[208,1024]{1,0:T(8,128)(2,1)S(1)} %collective-permute-done.32.refs_2_, ...), custom_call_target="tpu_custom_call", output_to_operand_aliasing={{}: (4, {})} | custom-call | tf_op jit(solution)/shard_map/place/pallas_call | solution.py:193
  133.7 2.3 %place.6.refs_2_ = bf16[1664,1408]{1,0:T(8,128)(2,1)} custom-call(bf16[208,384]{1,0:T(8,128)(2,1)S(1)} %collective-permute-done.25.refs_0_, bf16[208,384]{1,0:T(8,128)(2,1)S(1)} %collective-permute-done.26.refs_1_, bf16[208,384]{1,0:T(8,128)(2,1)S(1)} %collective-permute-done.27.refs_2_, ...), custom_call_target="tpu_custom_call", output_to_operand_aliasing={{}: (6, {})} | custom-call | tf_op jit(solution)/shard_map/place/pallas_call | solution.py:193
  136.0 1.4 %place.7 = bf16[1664,1408]{1,0:T(8,128)(2,1)} custom-call(bf16[208,1024]{1,0:T(8,128)(2,1)S(1)} %collective-permute-done.23.refs_0_, bf16[208,1024]{1,0:T(8,128)(2,1)S(1)} %collective-permute-done.24.refs_1_, bf16[1664,1408]{1,0:T(8,128)(2,1)} %place.6.refs_2_), custom_call_target="tpu_custom_call", output_to_operand_aliasing={{}: (2, {})} | custom-call | tf_op jit(solution)/shard_map/place/pallas_call | solution.py:193
  (36 shorter events, 0.3 us)
Async XLA Ops:
  19.4 23.2 %copy-start = (f32[832,1024]{1,0:T(8,128)S(1)}, f32[832,1024]{1,0:T(8,128)}, u32[]{:S(2)}) copy-start(f32[832,1024]{1,0:T(8,128)} %get-tuple-element.30) | copy-start | bytes 10223620
  19.4 4.1 %collective-permute-start.4 = (bf16[832,1024]{1,0:T(8,128)(2,1)}, bf16[832,1024]{1,0:T(8,128)(2,1)}, u32[]{:S(2)}, u32[]{:S(2)}) collective-permute-start(bf16[832,1024]{1,0:T(8,128)(2,1)} %get-tuple-element.31), channel_id=1, source_target_pairs={{0,1},{1,0},{2,3},{3,2},{4,5},{5,4},{6,7},{7,6},{8,9},{9,8},{10,11... | collective-permute-start | bytes 5111816 | tf_op jit(solution)/shard_map/ppermute | solution.py:237
  19.9 15.8 %collective-permute-start = (bf16[832,384]{1,0:T(8,128)(2,1)}, bf16[832,384]{1,0:T(8,128)(2,1)}, u32[]{:S(2)}, u32[]{:S(2)}) collective-permute-start(bf16[832,384]{1,0:T(8,128)(2,1)} %get-tuple-element.29), channel_id=1, source_target_pairs={{0,1},{1,0},{2,3},{3,2},{4,5},{5,4},{6,7},{7,6},{8,9},{9,8},{10,11... | collective-permute-start | bytes 1916936 | tf_op jit(solution)/shard_map/ppermute | solution.py:237
  26.4 16.1 %collective-permute-start.6 = (bf16[208,1024]{1,0:T(8,128)(2,1)}, bf16[208,1024]{1,0:T(8,128)(2,1)}, u32[]{:S(2)}, u32[]{:S(2)}) collective-permute-start(bf16[208,1024]{1,0:T(8,128)(2,1)} %get-tuple-element.48), channel_id=1, source_target_pairs={{0,2},{1,5},{2,0},{3,7},{4,6},{5,1},{6,4},{7,3},{8,10},{9,13},{10,... | collective-permute-start | bytes 1277960 | tf_op jit(solution)/shard_map/ppermute | solution.py:273
  30.8 16.9 %collective-permute-start.12 = (bf16[52,1024]{1,0:T(8,128)(2,1)}, bf16[52,1024]{1,0:T(8,128)(2,1)S(1)}, u32[]{:S(2)}, u32[]{:S(2)}) collective-permute-start(bf16[52,1024]{1,0:T(8,128)(2,1)} %slice.31), channel_id=1, source_target_pairs={{0,0},{1,8},{2,16},{3,24},{4,2},{5,10},{6,18},{7,26},{8,4},{9,12},... | collective-permute-start | bytes 319496 | tf_op jit(solution)/shard_map/ppermute | solution.py:353
  33.7 10.2 %collective-permute-start.11 = (bf16[52,384]{1,0:T(8,128)(2,1)}, bf16[52,384]{1,0:T(8,128)(2,1)}, u32[]{:S(2)}, u32[]{:S(2)}) collective-permute-start(bf16[52,384]{1,0:T(8,128)(2,1)} %slice.30), channel_id=1, source_target_pairs={{0,0},{1,2},{2,4},{3,6},{4,8},{5,10},{6,12},{7,14},{8,16},{9,18},{... | collective-permute-start | bytes 119816 | tf_op jit(solution)/shard_map/ppermute | solution.py:352
  35.8 8.2 %copy-start.1 = (bf16[208,1024]{1,0:T(8,128)(2,1)S(1)}, bf16[208,1024]{1,0:T(8,128)(2,1)}, u32[]{:S(2)}) copy-start(bf16[208,1024]{1,0:T(8,128)(2,1)} %get-tuple-element.47) | copy-start | bytes 1277956
  37.2 12.3 %collective-permute-start.1 = (bf16[208,384]{1,0:T(8,128)(2,1)S(1)}, bf16[208,384]{1,0:T(8,128)(2,1)S(1)}, u32[]{:S(2)}, u32[]{:S(2)}) collective-permute-start(bf16[208,384]{1,0:T(8,128)(2,1)S(1)} %get-tuple-element.49), channel_id=1, source_target_pairs={{0,24},{1,25},{2,26},{3,27},{4,28},{5,29},{6,30},{7,31},{8,16},{9,... | collective-permute-start | bytes 479240 | tf_op jit(solution)/shard_map/ppermute | solution.py:237
  41.5 15.5 %collective-permute-start.2 = (bf16[208,384]{1,0:T(8,128)(2,1)S(1)}, bf16[208,384]{1,0:T(8,128)(2,1)S(1)}, u32[]{:S(2)}, u32[]{:S(2)}) collective-permute-start(bf16[208,384]{1,0:T(8,128)(2,1)S(1)} %get-tuple-element.51), channel_id=1, source_target_pairs={{0,16},{1,17},{2,18},{3,19},{4,20},{5,21},{6,22},{7,23},{8,24},{9,... | collective-permute-start | bytes 479240 | tf_op jit(solution)/shard_map/ppermute | solution.py:237
  42.4 14.6 %collective-permute-start.3 = (bf16[208,384]{1,0:T(8,128)(2,1)S(1)}, bf16[208,384]{1,0:T(8,128)(2,1)S(1)}, u32[]{:S(2)}, u32[]{:S(2)}) collective-permute-start(bf16[208,384]{1,0:T(8,128)(2,1)S(1)} %get-tuple-element.50), channel_id=1, source_target_pairs={{0,8},{1,9},{2,10},{3,11},{4,12},{5,13},{6,14},{7,15},{8,0},{9,1},... | collective-permute-start | bytes 479240 | tf_op jit(solution)/shard_map/ppermute | solution.py:237
  43.9 14.2 %collective-permute-start.5 = (bf16[208,1024]{1,0:T(8,128)(2,1)S(1)}, bf16[208,1024]{1,0:T(8,128)(2,1)S(1)}, u32[]{:S(2)}, u32[]{:S(2)}) collective-permute-start(bf16[208,1024]{1,0:T(8,128)(2,1)S(1)} %copy-done.1), channel_id=1, source_target_pairs={{0,2},{1,5},{2,0},{3,7},{4,6},{5,1},{6,4},{7,3},{8,10},{9,13},{10,... | collective-permute-start | bytes 1277960 | tf_op jit(solution)/shard_map/ppermute | solution.py:274
  47.7 11.7 %collective-permute-start.7 = (bf16[208,1024]{1,0:T(8,128)(2,1)S(1)}, bf16[208,1024]{1,0:T(8,128)(2,1)S(1)}, u32[]{:S(2)}, u32[]{:S(2)}) collective-permute-start(bf16[208,1024]{1,0:T(8,128)(2,1)S(1)} %add_convert_fusion), channel_id=1, source_target_pairs={{0,4},{1,3},{2,6},{3,1},{4,0},{5,7},{6,2},{7,5},{8,12},{9,11},{10,... | collective-permute-start | bytes 1277960 | tf_op jit(solution)/shard_map/ppermute | solution.py:276
  60.6 5.8 %collective-permute-start.10 = (bf16[56,384]{1,0:T(8,128)(2,1)S(1)}, bf16[56,384]{1,0:T(8,128)(2,1)S(1)}, u32[]{:S(2)}, u32[]{:S(2)}) collective-permute-start(bf16[56,384]{1,0:T(8,128)(2,1)S(1)} %get-tuple-element.60), channel_id=1, source_target_pairs={{0,2},{1,3},{2,0},{3,1},{4,6},{5,7},{6,4},{7,5},{8,10},{9,11},{10,... | collective-permute-start | bytes 129032 | tf_op jit(solution)/shard_map/ppermute | solution.py:237
  62.8 6.1 %collective-permute-start.8 = (bf16[56,384]{1,0:T(8,128)(2,1)S(1)}, bf16[56,384]{1,0:T(8,128)(2,1)S(1)}, u32[]{:S(2)}, u32[]{:S(2)}) collective-permute-start(bf16[56,384]{1,0:T(8,128)(2,1)S(1)} %get-tuple-element.59), channel_id=1, source_target_pairs={{0,6},{1,7},{2,4},{3,5},{4,2},{5,3},{6,0},{7,1},{8,14},{9,15},{10,... | collective-permute-start | bytes 129032 | tf_op jit(solution)/shard_map/ppermute | solution.py:237
  63.9 4.9 %collective-permute-start.9 = (bf16[56,384]{1,0:T(8,128)(2,1)S(1)}, bf16[56,384]{1,0:T(8,128)(2,1)S(1)}, u32[]{:S(2)}, u32[]{:S(2)}) collective-permute-start(bf16[56,384]{1,0:T(8,128)(2,1)S(1)} %get-tuple-element.61), channel_id=1, source_target_pairs={{0,4},{1,5},{2,6},{3,7},{4,0},{5,1},{6,2},{7,3},{8,12},{9,13},{10,... | collective-permute-start | bytes 129032 | tf_op jit(solution)/shard_map/ppermute | solution.py:237
  64.4 7.9 %collective-permute-start.13 = (bf16[56,1024]{1,0:T(8,128)(2,1)S(1)}, bf16[56,1024]{1,0:T(8,128)(2,1)S(1)}, u32[]{:S(2)}, u32[]{:S(2)}) collective-permute-start(bf16[56,1024]{1,0:T(8,128)(2,1)S(1)} %get-tuple-element.52), channel_id=1, source_target_pairs={{0,24},{1,25},{2,26},{3,27},{4,28},{5,29},{6,30},{7,31},{8,16},{9,... | collective-permute-start | bytes 344072 | tf_op jit(solution)/shard_map/ppermute | solution.py:237
  66.4 9.9 %collective-permute-start.14 = (bf16[56,1024]{1,0:T(8,128)(2,1)S(1)}, bf16[56,1024]{1,0:T(8,128)(2,1)S(1)}, u32[]{:S(2)}, u32[]{:S(2)}) collective-permute-start(bf16[56,1024]{1,0:T(8,128)(2,1)S(1)} %get-tuple-element.54), channel_id=1, source_target_pairs={{0,16},{1,17},{2,18},{3,19},{4,20},{5,21},{6,22},{7,23},{8,24},{9,... | collective-permute-start | bytes 344072 | tf_op jit(solution)/shard_map/ppermute | solution.py:237
  66.5 9.9 %collective-permute-start.15 = (bf16[56,1024]{1,0:T(8,128)(2,1)S(1)}, bf16[56,1024]{1,0:T(8,128)(2,1)S(1)}, u32[]{:S(2)}, u32[]{:S(2)}) collective-permute-start(bf16[56,1024]{1,0:T(8,128)(2,1)S(1)} %get-tuple-element.53), channel_id=1, source_target_pairs={{0,8},{1,9},{2,10},{3,11},{4,12},{5,13},{6,14},{7,15},{8,0},{9,1},... | collective-permute-start | bytes 344072 | tf_op jit(solution)/shard_map/ppermute | solution.py:237
  77.4 13.4 %collective-permute-start.19 = (bf16[56,1024]{1,0:T(8,128)(2,1)S(1)}, bf16[56,1024]{1,0:T(8,128)(2,1)S(1)}, u32[]{:S(2)}, u32[]{:S(2)}) collective-permute-start(bf16[56,1024]{1,0:T(8,128)(2,1)S(1)} %subtract_convert_fusion), channel_id=1, source_target_pairs={{0,8},{1,9},{2,10},{3,11},{4,12},{5,13},{6,14},{7,15},{8,0},{9,1},... | collective-permute-start | bytes 344072 | tf_op jit(solution)/shard_map/ppermute | solution.py:237
  77.5 13.3 %collective-permute-start.20 = (bf16[56,1024]{1,0:T(8,128)(2,1)S(1)}, bf16[56,1024]{1,0:T(8,128)(2,1)S(1)}, u32[]{:S(2)}, u32[]{:S(2)}) collective-permute-start(bf16[56,1024]{1,0:T(8,128)(2,1)S(1)} %subtract_convert_fusion), channel_id=1, source_target_pairs={{0,16},{1,17},{2,18},{3,19},{4,20},{5,21},{6,22},{7,23},{8,24},{9,... | collective-permute-start | bytes 344072 | tf_op jit(solution)/shard_map/ppermute | solution.py:237
  80.6 10.2 %collective-permute-start.21 = (bf16[56,1024]{1,0:T(8,128)(2,1)S(1)}, bf16[56,1024]{1,0:T(8,128)(2,1)S(1)}, u32[]{:S(2)}, u32[]{:S(2)}) collective-permute-start(bf16[56,1024]{1,0:T(8,128)(2,1)S(1)} %subtract_convert_fusion), channel_id=1, source_target_pairs={{0,24},{1,25},{2,26},{3,27},{4,28},{5,29},{6,30},{7,31},{8,16},{9,... | collective-permute-start | bytes 344072 | tf_op jit(solution)/shard_map/ppermute | solution.py:237
  81.8 4.0 %collective-permute-start.16 = (bf16[56,384]{1,0:T(8,128)(2,1)S(1)}, bf16[56,384]{1,0:T(8,128)(2,1)S(1)}, u32[]{:S(2)}, u32[]{:S(2)}) collective-permute-start(bf16[56,384]{1,0:T(8,128)(2,1)S(1)} %subtract_convert_fusion.1), channel_id=1, source_target_pairs={{0,2},{1,3},{2,0},{3,1},{4,6},{5,7},{6,4},{7,5},{8,10},{9,11},{10,... | collective-permute-start | bytes 129032 | tf_op jit(solution)/shard_map/ppermute | solution.py:237
  83.5 4.4 %collective-permute-start.17 = (bf16[56,384]{1,0:T(8,128)(2,1)S(1)}, bf16[56,384]{1,0:T(8,128)(2,1)S(1)}, u32[]{:S(2)}, u32[]{:S(2)}) collective-permute-start(bf16[56,384]{1,0:T(8,128)(2,1)S(1)} %subtract_convert_fusion.1), channel_id=1, source_target_pairs={{0,4},{1,5},{2,6},{3,7},{4,0},{5,1},{6,2},{7,3},{8,12},{9,13},{10,... | collective-permute-start | bytes 129032 | tf_op jit(solution)/shard_map/ppermute | solution.py:237
  85.9 4.9 %collective-permute-start.18 = (bf16[56,384]{1,0:T(8,128)(2,1)S(1)}, bf16[56,384]{1,0:T(8,128)(2,1)S(1)}, u32[]{:S(2)}, u32[]{:S(2)}) collective-permute-start(bf16[56,384]{1,0:T(8,128)(2,1)S(1)} %subtract_convert_fusion.1), channel_id=1, source_target_pairs={{0,6},{1,7},{2,4},{3,5},{4,2},{5,3},{6,0},{7,1},{8,14},{9,15},{10,... | collective-permute-start | bytes 129032 | tf_op jit(solution)/shard_map/ppermute | solution.py:237
  91.1 12.3 %collective-permute-start.22 = (bf16[208,1024]{1,0:T(8,128)(2,1)S(1)}, bf16[208,1024]{1,0:T(8,128)(2,1)S(1)}, u32[]{:S(2)}, u32[]{:S(2)}) collective-permute-start(bf16[208,1024]{1,0:T(8,128)(2,1)S(1)} %pad_maximum_fusion.refs_1_), channel_id=1, source_target_pairs={{0,4},{1,3},{2,6},{3,1},{4,0},{5,7},{6,2},{7,5},{8,12},{9,11},{10,... | collective-permute-start | bytes 1277960 | tf_op jit(solution)/shard_map/ppermute | solution.py:282
  93.3 18.8 %collective-permute-start.31 = (bf16[208,1024]{1,0:T(8,128)(2,1)S(1)}, bf16[208,1024]{1,0:T(8,128)(2,1)S(1)}, u32[]{:S(2)}, u32[]{:S(2)}) collective-permute-start(bf16[208,1024]{1,0:T(8,128)(2,1)S(1)} %pad_maximum_fusion.refs_1_), channel_id=1, source_target_pairs={{0,2},{1,5},{2,0},{3,7},{4,6},{5,1},{6,4},{7,3},{8,10},{9,13},{10,... | collective-permute-start | bytes 1277960 | tf_op jit(solution)/shard_map/ppermute | solution.py:283
  103.4 8.7 %collective-permute-start.23 = (bf16[208,1024]{1,0:T(8,128)(2,1)S(1)}, bf16[208,1024]{1,0:T(8,128)(2,1)S(1)}, u32[]{:S(2)}, u32[]{:S(2)}) collective-permute-start(bf16[208,1024]{1,0:T(8,128)(2,1)S(1)} %collective-permute-done.22.refs_0_), channel_id=1, source_target_pairs={{0,2},{1,5},{2,0},{3,7},{4,6},{5,1},{6,4},{7,3},{8,10},{9,13},{10,... | collective-permute-start | bytes 1277960 | tf_op jit(solution)/shard_map/ppermute | solution.py:284
  104.5 1.5 %collective-permute-start.34 = (bf16[208,384]{1,0:T(8,128)(2,1)S(1)}, bf16[208,384]{1,0:T(8,128)(2,1)S(1)}, u32[]{:S(2)}, u32[]{:S(2)}) collective-permute-start(bf16[208,384]{1,0:T(8,128)(2,1)S(1)} %pad_maximum_fusion.1.refs_0_), channel_id=1, source_target_pairs={{0,1},{1,0},{2,3},{3,2},{4,5},{5,4},{6,7},{7,6},{8,9},{9,8},{10,11... | collective-permute-start | bytes 479240 | tf_op jit(solution)/shard_map/ppermute | solution.py:237
  104.5 6.5 %collective-permute-start.25 = (bf16[208,384]{1,0:T(8,128)(2,1)S(1)}, bf16[208,384]{1,0:T(8,128)(2,1)S(1)}, u32[]{:S(2)}, u32[]{:S(2)}) collective-permute-start(bf16[208,384]{1,0:T(8,128)(2,1)S(1)} %pad_maximum_fusion.1.refs_0_), channel_id=1, source_target_pairs={{0,8},{1,9},{2,10},{3,11},{4,12},{5,13},{6,14},{7,15},{8,0},{9,1},... | collective-permute-start | bytes 479240 | tf_op jit(solution)/shard_map/ppermute | solution.py:237
  104.6 24.3 %collective-permute-start.35 = (bf16[208,1024]{1,0:T(8,128)(2,1)S(1)}, bf16[208,1024]{1,0:T(8,128)(2,1)S(1)}, u32[]{:S(2)}, u32[]{:S(2)}) collective-permute-start(bf16[208,1024]{1,0:T(8,128)(2,1)S(1)} %pad_maximum_fusion.refs_1_), channel_id=1, source_target_pairs={{0,1},{1,0},{2,3},{3,2},{4,5},{5,4},{6,7},{7,6},{8,9},{9,8},{10,11... | collective-permute-start | bytes 1277960 | tf_op jit(solution)/shard_map/ppermute | solution.py:237
  105.9 23.5 %collective-permute-start.32 = (bf16[208,1024]{1,0:T(8,128)(2,1)S(1)}, bf16[208,1024]{1,0:T(8,128)(2,1)S(1)}, u32[]{:S(2)}, u32[]{:S(2)}) collective-permute-start(bf16[208,1024]{1,0:T(8,128)(2,1)S(1)} %collective-permute-done.22.refs_0_), channel_id=1, source_target_pairs={{0,1},{1,0},{2,3},{3,2},{4,5},{5,4},{6,7},{7,6},{8,9},{9,8},{10,11... | collective-permute-start | bytes 1277960 | tf_op jit(solution)/shard_map/ppermute | solution.py:237
  111.1 9.9 %collective-permute-start.26 = (bf16[208,384]{1,0:T(8,128)(2,1)S(1)}, bf16[208,384]{1,0:T(8,128)(2,1)S(1)}, u32[]{:S(2)}, u32[]{:S(2)}) collective-permute-start(bf16[208,384]{1,0:T(8,128)(2,1)S(1)} %pad_maximum_fusion.1.refs_0_), channel_id=1, source_target_pairs={{0,16},{1,17},{2,18},{3,19},{4,20},{5,21},{6,22},{7,23},{8,24},{9,... | collective-permute-start | bytes 479240 | tf_op jit(solution)/shard_map/ppermute | solution.py:237
  112.1 19.3 %collective-permute-start.33 = (bf16[208,1024]{1,0:T(8,128)(2,1)S(1)}, bf16[208,1024]{1,0:T(8,128)(2,1)S(1)}, u32[]{:S(2)}, u32[]{:S(2)}) collective-permute-start(bf16[208,1024]{1,0:T(8,128)(2,1)S(1)} %collective-permute-done.31.refs_1_), channel_id=1, source_target_pairs={{0,1},{1,0},{2,3},{3,2},{4,5},{5,4},{6,7},{7,6},{8,9},{9,8},{10,11... | collective-permute-start | bytes 1277960 | tf_op jit(solution)/shard_map/ppermute | solution.py:237
  112.1 23.8 %collective-permute-start.24 = (bf16[208,1024]{1,0:T(8,128)(2,1)S(1)}, bf16[208,1024]{1,0:T(8,128)(2,1)S(1)}, u32[]{:S(2)}, u32[]{:S(2)}) collective-permute-start(bf16[208,1024]{1,0:T(8,128)(2,1)S(1)} %collective-permute-done.23.refs_0_), channel_id=1, source_target_pairs={{0,1},{1,0},{2,3},{3,2},{4,5},{5,4},{6,7},{7,6},{8,9},{9,8},{10,11... | collective-permute-start | bytes 1277960 | tf_op jit(solution)/shard_map/ppermute | solution.py:237
  121.0 7.9 %collective-permute-start.27 = (bf16[208,384]{1,0:T(8,128)(2,1)S(1)}, bf16[208,384]{1,0:T(8,128)(2,1)S(1)}, u32[]{:S(2)}, u32[]{:S(2)}) collective-permute-start(bf16[208,384]{1,0:T(8,128)(2,1)S(1)} %pad_maximum_fusion.1.refs_0_), channel_id=1, source_target_pairs={{0,24},{1,25},{2,26},{3,27},{4,28},{5,29},{6,30},{7,31},{8,16},{9,... | collective-permute-start | bytes 479240 | tf_op jit(solution)/shard_map/ppermute | solution.py:237
  128.9 4.7 %collective-permute-start.28 = (bf16[208,384]{1,0:T(8,128)(2,1)S(1)}, bf16[208,384]{1,0:T(8,128)(2,1)S(1)}, u32[]{:S(2)}, u32[]{:S(2)}) collective-permute-start(bf16[208,384]{1,0:T(8,128)(2,1)S(1)} %collective-permute-done.25.refs_0_), channel_id=1, source_target_pairs={{0,1},{1,0},{2,3},{3,2},{4,5},{5,4},{6,7},{7,6},{8,9},{9,8},{10,11... | collective-permute-start | bytes 479240 | tf_op jit(solution)/shard_map/ppermute | solution.py:237
  128.9 4.7 %collective-permute-start.29 = (bf16[208,384]{1,0:T(8,128)(2,1)S(1)}, bf16[208,384]{1,0:T(8,128)(2,1)S(1)}, u32[]{:S(2)}, u32[]{:S(2)}) collective-permute-start(bf16[208,384]{1,0:T(8,128)(2,1)S(1)} %collective-permute-done.26.refs_1_), channel_id=1, source_target_pairs={{0,1},{1,0},{2,3},{3,2},{4,5},{5,4},{6,7},{7,6},{8,9},{9,8},{10,11... | collective-permute-start | bytes 479240 | tf_op jit(solution)/shard_map/ppermute | solution.py:237
  129.4 4.2 %collective-permute-start.30 = (bf16[208,384]{1,0:T(8,128)(2,1)S(1)}, bf16[208,384]{1,0:T(8,128)(2,1)S(1)}, u32[]{:S(2)}, u32[]{:S(2)}) collective-permute-start(bf16[208,384]{1,0:T(8,128)(2,1)S(1)} %collective-permute-done.27.refs_2_), channel_id=1, source_target_pairs={{0,1},{1,0},{2,3},{3,2},{4,5},{5,4},{6,7},{7,6},{8,9},{9,8},{10,11... | collective-permute-start | bytes 479240 | tf_op jit(solution)/shard_map/ppermute | solution.py:237
